TPU v7x, 1024 devices: a whole 4x8x16 slice. The times are simulated.
1024 devices in a mesh: section: 8 (over z_lo), dp: 32 (over y, x), mp: 4 (over z_hi, core).
Axes of the slice: x: 4, y: 8, z: 16 (z_hi: 2, z_lo: 8; z = z_hi * 8 + z_lo), core: 2. Of those that a mesh axis runs over, the one named last changes fastest.
Arguments:
- fwd_in: bfloat16 [8, 16384, 1024], P('section', ('dp', 'mp')), may hold values from -6 to 6
- stash: bfloat16 [8, 16384, 1024], P('section', ('dp', 'mp')), may hold values from -6 to 6
- cot: bfloat16 [8, 16384, 1024], P('section', ('dp', 'mp')), may hold values from -24 to 24
- w_in: bfloat16 [8, 2048, 1024], P('section', 'mp'), may hold values from -0.1875 to 0.1875
- w_out: bfloat16 [8, 2048, 1024], P('section', 'mp'), may hold values from -0.125 to 0.125
- gain: float32 [8, 1024], P('section'), may hold values from 0.1 to 1.9
Outputs:
- passed_fwd: bfloat16 [8, 16384, 1024], P('section', ('dp', 'mp'))
- passed_grad: bfloat16 [8, 16384, 1024], P('section', ('dp', 'mp'))
- grad_w_in: bfloat16 [8, 2048, 1024], P('section', 'mp', 'dp')
- grad_w_out: bfloat16 [8, 2048, 1024], P('section', 'mp', 'dp')
All inputs are finite; a program needn't handle non-finite values.
Results may differ from a plain program's by a relative error of at most 0.015.
Values may be sent and summed in bfloat16 or wider, within the bound.
No kernel may reach another device: no remote copies, remote signals or barrier semaphores. Data moves between devices by JAX's collectives and lax.ppermute only.
A program may use at most 32 MiB of HBM per device.

v0:
```python
import jax
import jax.numpy as jnp
from jax import lax
from jax.sharding import PartitionSpec as P

norm_eps = 1e-05
gelu_coef = 0.7978845608


def from_everyone(x, axis):
    copies = jnp.broadcast_to(x, (lax.axis_size(axis), *x.shape))
    return lax.all_to_all(copies, axis, split_axis=0, concat_axis=0, tiled=True)


def laid_out(pieces, dim):
    lengths = list(pieces.shape[1:])
    lengths[dim] *= pieces.shape[0]
    return jnp.moveaxis(pieces, 0, dim).reshape(lengths)


def gather_directly(x, axis, dim):
    pieces = from_everyone(x, axis)
    return laid_out(pieces, dim)


def in_blocks(x, dim, length):
    before, after = (x.shape[:dim], x.shape[dim + 1 :])
    return jnp.moveaxis(x.reshape(*before, length, -1, *after), dim, 0)


def summed_on_arrival(x, axis, dim):
    length = lax.axis_size(axis)
    pieces = lax.all_to_all(in_blocks(x, dim, length), axis, 0, 0, tiled=True)
    return jnp.sum(pieces.astype(jnp.float32), axis=0)


def shifted(x, axis, by):
    length = lax.axis_size(axis)
    return lax.ppermute(x, axis, [(i, (i + by) % length) for i in range(length)])


def side_by_side(arrays, axis, dim, along):
    ends, at = ([], 0)
    for a in arrays[:-1]:
        at += a.shape[along]
        ends.append(at)
    both = jnp.concatenate(arrays, axis=along)
    return tuple(jnp.split(lax.all_gather(both, axis, axis=dim, tiled=True), ends, axis=along))


def in_one_piece(arrays, axis, dim, along):
    widths = [a.shape[along] for a in arrays]
    both = jnp.concatenate(arrays, axis=along)
    whole = summed_on_arrival(both, axis, dim)
    return tuple(jnp.split(whole, [sum(widths[:k]) for k in range(1, len(widths))], axis=along))


def gelu_value(v):
    inner = jnp.tanh(gelu_coef * (v + 0.044715 * v * v * v))
    return 0.5 * v * (1.0 + inner)


def gelu_slope(v):
    inner = jnp.tanh(gelu_coef * (v + 0.044715 * v * v * v))
    return 0.5 * (1.0 + inner) + 0.5 * v * (1.0 - inner * inner) * gelu_coef * (
        1.0 + 0.134145 * v * v
    )


def prepare(x, w_first, gain_row):
    xf = x.astype(jnp.float32)
    scale = lax.rsqrt(jnp.mean(xf * xf, axis=-1, keepdims=True) + norm_eps)
    normed = (xf * scale * gain_row[None, :]).astype(jnp.bfloat16)
    pre = lax.dot_general(
        normed, w_first, (((1,), (1,)), ((), ())), preferred_element_type=jnp.float32
    )
    act = gelu_value(pre).astype(jnp.bfloat16)
    return (scale, normed, pre, act)


def on_device(fwd_in, stash, cot, w_in, w_out, gain):
    x_fwd = fwd_in[0]
    x_bwd = stash[0]
    cot_local = cot[0]
    w_first = w_in[0]
    w_second = w_out[0]
    gain_row = gain[0]
    local_rows = x_fwd.shape[0]
    scale, normed, pre, act = prepare(gather_directly(x_fwd, "mp", 0), w_first, gain_row)
    terms = jnp.dot(act, w_second, preferred_element_type=jnp.float32)
    branch = summed_on_arrival(terms.astype(jnp.bfloat16), "mp", 0)
    out = (x_fwd.astype(jnp.float32) + branch).astype(jnp.bfloat16)
    passed_fwd = shifted(out, "section", 1)
    rows_x, rows_cot = side_by_side((x_bwd, cot_local), "mp", 0, 1)
    scale, normed, pre, act = prepare(rows_x, w_first, gain_row)
    d_act = lax.dot_general(
        rows_cot, w_second, (((1,), (1,)), ((), ())), preferred_element_type=jnp.float32
    )
    d_pre = (d_act * gelu_slope(pre)).astype(jnp.bfloat16)
    d_norm = summed_on_arrival(
        jnp.dot(d_pre, w_first, preferred_element_type=jnp.float32).astype(jnp.bfloat16), "mp", 0
    )
    offset = lax.axis_index("mp") * local_rows
    own_scale = lax.dynamic_slice_in_dim(scale, offset, local_rows, 0)
    shard_x = x_bwd.astype(jnp.float32)
    push = d_norm * gain_row[None, :]
    mixed = jnp.mean(shard_x * push, axis=-1, keepdims=True)
    dx = (
        cot_local.astype(jnp.float32)
        + own_scale * push
        - shard_x * own_scale * own_scale * own_scale * mixed
    )
    passed_grad = shifted(dx.astype(jnp.bfloat16), "section", -1)
    term_out = lax.dot_general(
        act, rows_cot, (((0,), (0,)), ((), ())), preferred_element_type=jnp.float32
    )
    term_in = lax.dot_general(
        d_pre, normed, (((0,), (0,)), ((), ())), preferred_element_type=jnp.float32
    )
    sum_in, sum_out = in_one_piece(
        (term_in.astype(jnp.bfloat16), term_out.astype(jnp.bfloat16)), "dp", 1, 0
    )
    return (
        passed_fwd[None],
        passed_grad[None],
        sum_in.astype(jnp.bfloat16)[None],
        sum_out.astype(jnp.bfloat16)[None],
    )


def solution(mesh):
    in_specs = (
        P("section", ("dp", "mp"), None),
        P("section", ("dp", "mp"), None),
        P("section", ("dp", "mp"), None),
        P("section", "mp", None),
        P("section", "mp", None),
        P("section", None),
    )
    out_specs = (
        P("section", ("dp", "mp"), None),
        P("section", ("dp", "mp"), None),
        P("section", "mp", "dp"),
        P("section", "mp", "dp"),
    )
    return jax.shard_map(
        on_device, mesh=mesh, in_specs=in_specs, out_specs=out_specs, check_vma=False
    )
```

profile of v0, /device:TPU:336, one launch (start us, length us, event | category | flops | bytes accessed | tf_op | source)
XLA Modules:
  0.0 307.1 jit_solution(2575969294859077426)
XLA Ops:
  7.2 2.0 pad_maximum_fusion.1
  9.2 2.1 broadcast_in_dim.18
  11.3 13.0 %all-to-all-start = ((bf16[4,128,1024]{2,1,0:T(8,128)(2,1)}), bf16[4,128,1024]{2,1,0:T(8,128)(2,1)S(1)}, u32[]{:S(2)}, u32[]{:S(2)}) async-start(bf16[4,128,1024]{2,1,0:T(8,128)(2,1)} %broadcast_in_dim.18), calls=%async_computation | async-start | bytes 2097152 | tf_op jit(solution)/shard_map/all_to_all | solution.py:12
  24.3 89.5 %all-gather.2.cloned.1.call-done = bf16[512,2048]{1,0:T(8,128)(2,1)} async-done(((bf16[128,2048]{1,0:T(8,128)(2,1)}), bf16[512,2048]{1,0:T(8,128)(2,1)}) %all-gather.2.cloned.1.call-update) | async-done | bytes 2097168 | tf_op jit(solution)/shard_map/all_gather | solution.py:48
  113.8 1.5 fusion.3
  115.3 2.1 fusion.20
  117.5 1.2 fusion.6
  118.7 0.8 copy-done.10
  119.5 1.7 convolution_convert_fusion.2
  121.2 3.5 %all-to-all-start.2 = ((bf16[4,128,1024]{2,1,0:T(8,128)(2,1)}), bf16[4,128,1024]{2,1,0:T(8,128)(2,1)S(1)}, u32[]{:S(2)}, u32[]{:S(2)}) async-start(bf16[4,128,1024]{2,1,0:T(8,128)(2,1)} %bitcast.41), calls=%async_computation.2 | async-start | bytes 2097152 | tf_op jit(solution)/shard_map/all_to_all | solution.py:33
  124.8 0.3 fusion
  125.0 1.3 fusion.2
  126.4 3.9 %convolution_convert_fusion.3 = bf16[512,1024]{1,0:T(8,128)(2,1)} fusion(bf16[1,512,1024]{2,1,0:T(8,128)(2,1)} %param.10, bf16[512,1024]{1,0:T(8,128)(2,1)} %bitcast.40, bf16[1,512,1024]{2,1,0:T(8,128)(2,1)S(1)} %copy-done), kind=kOutput, calls=%fused_computation.19 | convolution fusion | flops 1076625408 | bytes 4194304 | tf_op jit(solution)/shard_map/dot_general | solution.py:90
  130.3 51.4 %all-to-all-done.2 = bf16[4,128,1024]{2,1,0:T(8,128)(2,1)S(1)} async-done(((bf16[4,128,1024]{2,1,0:T(8,128)(2,1)}), bf16[4,128,1024]{2,1,0:T(8,128)(2,1)S(1)}, u32[]{:S(2)}, u32[]{:S(2)}) %all-to-all-start.2) | async-done | bytes 1048608 | tf_op jit(solution)/shard_map/all_to_all | solution.py:33
  181.7 4.2 %all-to-all-start.1 = ((bf16[4,128,1024]{2,1,0:T(8,128)(2,1)}), bf16[4,128,1024]{2,1,0:T(8,128)(2,1)}, u32[]{:S(2)}, u32[]{:S(2)}) async-start(bf16[4,128,1024]{2,1,0:T(8,128)(2,1)} %bitcast.5), calls=%async_computation.1 | async-start | bytes 2097152 | tf_op jit(solution)/shard_map/all_to_all | solution.py:33
  186.0 2.2 convolution_convert_fusion.1
  188.2 0.8 convolution_convert_fusion
  189.2 2.6 copy.11
  191.8 44.6 %all-to-all-done.1 = bf16[4,128,1024]{2,1,0:T(8,128)(2,1)} async-done(((bf16[4,128,1024]{2,1,0:T(8,128)(2,1)}), bf16[4,128,1024]{2,1,0:T(8,128)(2,1)}, u32[]{:S(2)}, u32[]{:S(2)}) %all-to-all-start.1) | async-done | bytes 1048608 | tf_op jit(solution)/shard_map/all_to_all | solution.py:33
  236.4 10.2 %all-to-all-start.3 = ((bf16[32,1024,32]{1,2,0:T(8,128)(2,1)}), bf16[32,1024,32]{1,2,0:T(8,128)(2,1)S(1)}, u32[]{:S(2)}, u32[]{:S(2)}) async-start(bf16[32,1024,32]{1,2,0:T(8,128)(2,1)} %bitcast.12), calls=%async_computation.3 | async-start | bytes 4194304 | tf_op jit(solution)/shard_map/all_to_all | solution.py:33
  246.7 1.5 convert_reduce_fusion
  248.4 0.2 fusion.34
  248.6 1.9 collective-permute-start.1
  250.5 1.5 convert_reduce_fusion.1
  252.1 3.9 %collective-permute-start = (bf16[128,1024]{1,0:T(8,128)(2,1)S(1)}, bf16[128,1024]{1,0:T(8,128)(2,1)S(1)}, u32[]{:S(2)}, u32[]{:S(2)}) collective-permute-start(bf16[128,1024]{1,0:T(8,128)(2,1)S(1)} %add_convert_fusion), channel_id=1, source_target_pairs={{0,128},{128,256},{256,384},{384,512},{512,640},{640,768},{768,896... | collective-permute-start | bytes 786440 | tf_op jit(solution)/shard_map/ppermute | solution.py:39
  256.0 6.8 %collective-permute-done.1 = bf16[128,1024]{1,0:T(8,128)(2,1)S(1)} collective-permute-done((bf16[128,1024]{1,0:T(8,128)(2,1)S(1)}, bf16[128,1024]{1,0:T(8,128)(2,1)S(1)}, u32[]{:S(2)}, u32[]{:S(2)}) %collective-permute-start.1) | collective-permute-done | bytes 262176 | tf_op jit(solution)/shard_map/ppermute | solution.py:39
  262.8 0.7 copy-done.7
  263.5 33.3 %all-to-all-done.3 = bf16[32,1024,32]{1,2,0:T(8,128)(2,1)S(1)} async-done(((bf16[32,1024,32]{1,2,0:T(8,128)(2,1)}), bf16[32,1024,32]{1,2,0:T(8,128)(2,1)S(1)}, u32[]{:S(2)}, u32[]{:S(2)}) %all-to-all-start.3) | async-done | bytes 2097184 | tf_op jit(solution)/shard_map/all_to_all | solution.py:33
  296.9 0.4 reduce.1
  297.2 0.6 slice_bitcast_fusion
  297.9 1.7 copy.14
  299.5 0.7 copy.15
  (37 shorter events, 0.6 us)
Async XLA Ops:
  7.2 108.1 %copy-start = (bf16[1,512,1024]{2,1,0:T(8,128)(2,1)S(1)}, bf16[1,512,1024]{2,1,0:T(8,128)(2,1)}, u32[]{:S(2)}) copy-start(bf16[1,512,1024]{2,1,0:T(8,128)(2,1)} %param.9) | copy-start | bytes 3145732
  7.2 106.6 %all-gather.2.cloned.1.call-start = ((), (), s32[]{:S(2)}) async-start(), calls=%async_computation.4 | async-start | bytes 2621440 | tf_op jit(solution)/shard_map/all_gather | solution.py:48
  9.2 106.1 %copy-start.8 = (f32[1,1024]{1,0:T(1,128)S(1)}, f32[1,1024]{1,0:T(1,128)}, u32[]{:S(2)}) copy-start(f32[1,1024]{1,0:T(1,128)} %param.11) | copy-start | bytes 12292
  11.3 109.9 %all-to-all-start = ((bf16[4,128,1024]{2,1,0:T(8,128)(2,1)}), bf16[4,128,1024]{2,1,0:T(8,128)(2,1)S(1)}, u32[]{:S(2)}, u32[]{:S(2)}) async-start(bf16[4,128,1024]{2,1,0:T(8,128)(2,1)} %broadcast_in_dim.18), calls=%async_computation | async-start | bytes 2097152 | tf_op jit(solution)/shard_map/all_to_all | solution.py:12
  115.3 2.2 copy-start.5
  115.3 2.2 copy-start.9
  117.5 1.2 copy-start.12
  118.7 0.8 copy-start.10
  121.2 60.5 %all-to-all-start.2 = ((bf16[4,128,1024]{2,1,0:T(8,128)(2,1)}), bf16[4,128,1024]{2,1,0:T(8,128)(2,1)S(1)}, u32[]{:S(2)}, u32[]{:S(2)}) async-start(bf16[4,128,1024]{2,1,0:T(8,128)(2,1)} %bitcast.41), calls=%async_computation.2 | async-start | bytes 2097152 | tf_op jit(solution)/shard_map/all_to_all | solution.py:33
  130.3 55.7 %copy-start.11 = (bf16[512,512]{1,0:T(8,128)(2,1)S(1)}, bf16[512,512]{1,0:T(8,128)(2,1)}, u32[]{:S(2)}) copy-start(bf16[512,512]{1,0:T(8,128)(2,1)} %copy-done.10) | copy-start | bytes 1572868
  181.7 6.5 %copy-start.1 = (bf16[4,128,1024]{2,1,0:T(8,128)(2,1)}, bf16[4,128,1024]{2,1,0:T(8,128)(2,1)S(1)}, u32[]{:S(2)}) copy-start(bf16[4,128,1024]{2,1,0:T(8,128)(2,1)S(1)} %all-to-all-done.2) | copy-start | bytes 3145732
  181.7 54.7 %all-to-all-start.1 = ((bf16[4,128,1024]{2,1,0:T(8,128)(2,1)}), bf16[4,128,1024]{2,1,0:T(8,128)(2,1)}, u32[]{:S(2)}, u32[]{:S(2)}) async-start(bf16[4,128,1024]{2,1,0:T(8,128)(2,1)} %bitcast.5), calls=%async_computation.1 | async-start | bytes 2097152 | tf_op jit(solution)/shard_map/all_to_all | solution.py:33
  186.0 2.2 copy-start.6
  186.0 2.2 copy-start.13
  236.4 11.8 %copy-start.2 = (bf16[1,128,1024]{2,1,0:T(8,128)(2,1)S(1)}, bf16[1,128,1024]{2,1,0:T(8,128)(2,1)}, u32[]{:S(2)}) copy-start(bf16[1,128,1024]{2,1,0:T(8,128)(2,1)} %param.7) | copy-start | bytes 786436
  236.4 60.4 %all-to-all-start.3 = ((bf16[32,1024,32]{1,2,0:T(8,128)(2,1)}), bf16[32,1024,32]{1,2,0:T(8,128)(2,1)S(1)}, u32[]{:S(2)}, u32[]{:S(2)}) async-start(bf16[32,1024,32]{1,2,0:T(8,128)(2,1)} %bitcast.12), calls=%async_computation.3 | async-start | bytes 4194304 | tf_op jit(solution)/shard_map/all_to_all | solution.py:33
  246.6 1.7 copy-start.4
  248.2 3.8 %copy-start.3 = (bf16[1,128,1024]{2,1,0:T(8,128)(2,1)S(1)}, bf16[1,128,1024]{2,1,0:T(8,128)(2,1)}, u32[]{:S(2)}) copy-start(bf16[1,128,1024]{2,1,0:T(8,128)(2,1)} %param.6) | copy-start | bytes 786436
  248.6 14.2 %collective-permute-start.1 = (bf16[128,1024]{1,0:T(8,128)(2,1)S(1)}, bf16[128,1024]{1,0:T(8,128)(2,1)S(1)}, u32[]{:S(2)}, u32[]{:S(2)}) collective-permute-start(bf16[128,1024]{1,0:T(8,128)(2,1)S(1)} %fusion.34), channel_id=1, source_target_pairs={{0,896},{128,0},{256,128},{384,256},{512,384},{640,512},{768,640},... | collective-permute-start | bytes 786440 | tf_op jit(solution)/shard_map/ppermute | solution.py:39
  252.1 10.7 %collective-permute-start = (bf16[128,1024]{1,0:T(8,128)(2,1)S(1)}, bf16[128,1024]{1,0:T(8,128)(2,1)S(1)}, u32[]{:S(2)}, u32[]{:S(2)}) collective-permute-start(bf16[128,1024]{1,0:T(8,128)(2,1)S(1)} %add_convert_fusion), channel_id=1, source_target_pairs={{0,128},{128,256},{256,384},{384,512},{512,640},{640,768},{768,896... | collective-permute-start | bytes 786440 | tf_op jit(solution)/shard_map/ppermute | solution.py:39
  262.8 0.7 copy-start.7
Sparse Core Ops, SparseCore 0:
  10.7 103.0 all-gather.1
where the time goes:
time: 308 us; the launch traced here: 307 us
  waiting for transfers between devices  226 us (73%)
  starting transfers between devices  36.8 us (12%)
  between operations  14.3 us (5%)
  matrix products  12 us (4%)
  local copies, waits for them, and re-layouts  9.3 us (3%)
  other arithmetic  9 us (3%)
    all_to_all x3, waiting for transfers between devices, summed_on_arrival(): pieces = lax.all_to_all(in_blocks(x, dim, length), axis, 0, 0, tiled=True)  129 us
    all_gather x1, waiting for transfers between devices, side_by_side(): lax.all_gather(both, axis, axis=dim, tiled=True)  89.5 us
    all_to_all x3, starting transfers between devices, summed_on_arrival(): pieces = lax.all_to_all(in_blocks(x, dim, length), axis, 0, 0, tiled=True)  17.9 us
    all_to_all x1, starting transfers between devices, from_everyone(): return lax.all_to_all(copies, axis, split_axis=0, concat_axis=0, tiled=True)  13 us
    ppermute x2, waiting for transfers between devices, shifted(): lax.ppermute(x, axis, [(i, (i + by) % length) for i in range(length)])  6.82 us
  transfers between devices with their start and end apart: 7, of which 5 were waited for; matrix products, arithmetic and copies ran while one was open for 8% of the time, Pallas kernels for 0%

commit v1 on v0

v1 whole, which is shorter than its diff:
```python
import jax
import jax.numpy as jnp
from jax import lax
from jax.sharding import PartitionSpec as P


norm_eps = 1e-05
gelu_coef = 0.7978845608


NX, NY = 4, 8
x_groups = [[NX * y + x for x in range(NX)] for y in range(NY)]
y_groups = [[NX * y + x for y in range(NY)] for x in range(NX)]
other_chip = [(0, 2), (1, 3), (2, 0), (3, 1)]
other_core = [(0, 1), (1, 0), (2, 3), (3, 2)]

f32, bf16 = jnp.float32, jnp.bfloat16


def to_chip(x):
    return lax.ppermute(x, "mp", other_chip)


def to_core(x):
    return lax.ppermute(x, "mp", other_core)


def shifted(x, axis, by):
    length = lax.axis_size(axis)
    return lax.ppermute(x, axis, [(i, (i + by) % length) for i in range(length)])


def gathered(x, groups):
    copies = jnp.broadcast_to(x, (len(groups[0]), *x.shape))
    return lax.all_to_all(copies, "dp", 0, 0, tiled=True, axis_index_groups=groups)


def summed(x, groups):
    pieces = lax.all_to_all(x, "dp", 0, 0, tiled=True, axis_index_groups=groups)
    return jnp.sum(pieces.astype(f32), axis=0)


def gelu_both(v):
    t = jnp.tanh(gelu_coef * (v + 0.044715 * v * v * v))
    value = 0.5 * v * (1.0 + t)
    slope = 0.5 * (1.0 + t) + 0.5 * v * (1.0 - t * t) * gelu_coef * (1.0 + 0.134145 * v * v)
    return value, slope


def scale_of(x):
    xf = x.astype(f32)
    return lax.rsqrt(jnp.mean(xf * xf, axis=-1, keepdims=True) + norm_eps)


def norm(x, gain_row):
    return (x.astype(f32) * scale_of(x) * gain_row[None, :]).astype(bf16)


def nt(a, b):
    return lax.dot_general(a, b, (((1,), (1,)), ((), ())), preferred_element_type=f32)


def tn(a, b):
    return lax.dot_general(a, b, (((0,), (0,)), ((), ())), preferred_element_type=f32)


def nn(a, b):
    return jnp.dot(a, b, preferred_element_type=f32)


def layer(fwd_in, stash, cot, w_in, w_out, gain):
    xf, xb, ct = fwd_in[0], stash[0], cot[0]
    wi, wo, gain_row = w_in[0], w_out[0], gain[0]
    rows = xf.shape[0]
    n_dp = lax.axis_size("dp")
    d = lax.axis_index("dp")
    part = wi.shape[0] // n_dp
    at = (d % NX * NY + d // NX) * part
    mine = jnp.stack(
        [lax.dynamic_slice_in_dim(wi, at, part, 0), lax.dynamic_slice_in_dim(wo, at, part, 0)]
    )
    piece = to_chip(mine)
    far = to_chip(jnp.concatenate([xb, ct]))
    near = to_core(jnp.concatenate([xf, xb, ct]))
    f2 = jnp.concatenate([xf, near[:rows]])
    b2 = jnp.concatenate([xb, near[rows : 2 * rows]])
    c2 = jnp.concatenate([ct, near[2 * rows :]])
    nf, nb = norm(f2, gain_row), norm(b2, gain_row)
    act_f, _ = gelu_both(nt(nf, wi))
    branch = nn(act_f.astype(bf16), wo)
    act_b, slope_b = gelu_both(nt(nb, wi))
    d_pre = (nt(c2, wo) * slope_b).astype(bf16)
    d_norm = nn(d_pre, wi)
    col = gathered(piece, y_groups)
    whole = gathered(col.reshape(NY, 2, part, -1), x_groups).reshape(n_dp, 2, part, -1)
    wi2 = whole[:, 0].reshape(wi.shape)
    wo2 = whole[:, 1].reshape(wo.shape)
    act_f2, _ = gelu_both(nt(nf, wi2))
    branch = branch + nn(act_f2.astype(bf16), wo2)
    branch = branch[:rows] + to_core(branch[rows:].astype(bf16)).astype(f32)
    out = (xf.astype(f32) + branch).astype(bf16)
    passed_fwd = shifted(out, "section", 1)
    _, slope_b2 = gelu_both(nt(nb, wi2))
    d_pre2 = (nt(c2, wo2) * slope_b2).astype(bf16)
    d_norm = d_norm + nn(d_pre2, wi2)
    d_norm = d_norm[:rows] + to_core(d_norm[rows:].astype(bf16)).astype(f32)
    scale = scale_of(xb)
    shard_x = xb.astype(f32)
    push = d_norm * gain_row[None, :]
    mixed = jnp.mean(shard_x * push, axis=-1, keepdims=True)
    dx = ct.astype(f32) + scale * push - shard_x * scale * scale * scale * mixed
    passed_grad = shifted(dx.astype(bf16), "section", -1)
    far2 = to_core(far)
    b3 = jnp.concatenate([far[:rows], far2[:rows]])
    c3 = jnp.concatenate([far[rows:], far2[rows:]])
    nb3 = norm(b3, gain_row)
    act_b3, slope_b3 = gelu_both(nt(nb3, wi))
    d_pre3 = (nt(c3, wo) * slope_b3).astype(bf16)
    g_in = tn(jnp.concatenate([nb, nb3]), jnp.concatenate([d_pre, d_pre3]))
    g_out = tn(
        jnp.concatenate([c2, c3]), jnp.concatenate([act_b.astype(bf16), act_b3.astype(bf16)])
    )
    hid = wi.shape[0]
    g = jnp.concatenate([g_in.astype(bf16), g_out.astype(bf16)], axis=1)
    g = g.reshape(NY, NX, -1, 2 * hid).swapaxes(0, 1)
    g = summed(g, x_groups).astype(bf16)
    g = summed(g, y_groups).astype(bf16)
    return (passed_fwd[None], passed_grad[None], g[:, :hid].T[None], g[:, hid:].T[None])


def solution(mesh):
    in_specs = (
        P("section", ("dp", "mp"), None),
        P("section", ("dp", "mp"), None),
        P("section", ("dp", "mp"), None),
        P("section", "mp", None),
        P("section", "mp", None),
        P("section", None),
    )
    out_specs = (
        P("section", ("dp", "mp"), None),
        P("section", ("dp", "mp"), None),
        P("section", "mp", "dp"),
        P("section", "mp", "dp"),
    )
    return jax.shard_map(layer, mesh=mesh, in_specs=in_specs, out_specs=out_specs, check_vma=False)
```

time: 308 us -> 196 us (0.64)
  the two profiles are of different devices: /device:TPU:336 before, /device:TPU:8 now
where the time goes in v1:
time: 196 us; the launch traced here: 195 us
  starting transfers between devices  99.3 us (51%)
  waiting for transfers between devices  45.2 us (23%)
  local copies, waits for them, and re-layouts  20.9 us (11%)
  matrix products  17.6 us (9%)
  other arithmetic  11.1 us (6%)
    all_to_all x2, starting transfers between devices, gathered(): lax.all_to_all(copies, 'dp', 0, 0, tiled=True, axis_index_groups=groups)  32.7 us
    ppermute x2, starting transfers between devices, to_chip(): return lax.ppermute(x, 'mp', other_chip)  21.4 us
    ppermute x2, starting transfers between devices, shifted(): lax.ppermute(x, axis, [(i, (i + by) % length) for i in range(length)])  20.3 us
    all_to_all x2, waiting for transfers between devices, gathered(): lax.all_to_all(copies, 'dp', 0, 0, tiled=True, axis_index_groups=groups)  18.6 us
    all_to_all x2, starting transfers between devices, summed(): pieces = lax.all_to_all(x, 'dp', 0, 0, tiled=True, axis_index_groups=groups)  16.8 us
    ppermute x2, waiting for transfers between devices, to_chip(): return lax.ppermute(x, 'mp', other_chip)  13.1 us
    ppermute x2, waiting for transfers between devices, shifted(): lax.ppermute(x, axis, [(i, (i + by) % length) for i in range(length)])  12.9 us
    dot_general x4, matrix products, nn(): return jnp.dot(a, b, preferred_element_type=f32)  12.3 us
  transfers between devices with their start and end apart: 12, of which 6 were waited for; matrix products, arithmetic and copies ran while one was open for 23% of the time, Pallas kernels for 0%

profile of v1, /device:TPU:8, one launch (start us, length us, event | category | flops | bytes accessed | tf_op | source)
XLA Modules:
  0.0 195.1 jit_solution(17938163866838475390)
XLA Ops:
  1.8 1.9 collective-permute-start
  4.8 19.4 %collective-permute-start.6 = (bf16[256,1024]{1,0:T(8,128)(2,1)S(1)}, bf16[256,1024]{1,0:T(8,128)(2,1)}, u32[]{:S(2)}, u32[]{:S(2)}) collective-permute-start(bf16[256,1024]{1,0:T(8,128)(2,1)S(1)} %pad_maximum_fusion.2), channel_id=1, source_target_pairs={{0,2},{1,3},{2,0},{3,1},{4,6},{5,7},{6,4},{7,5},{8,10},{9,11},{10,... | collective-permute-start | bytes 1572872 | tf_op jit(solution)/shard_map/ppermute | solution.py:21
  25.0 2.1 %collective-permute-start.1 = (bf16[2,16,1024]{2,1,0:T(8,128)(2,1)S(1)}, bf16[2,16,1024]{2,1,0:T(8,128)(2,1)S(1)}, u32[]{:S(2)}, u32[]{:S(2)}) collective-permute-start(bf16[2,16,1024]{2,1,0:T(8,128)(2,1)S(1)} %pad_maximum_fusion.10), channel_id=1, source_target_pairs={{0,2},{1,3},{2,0},{3,1},{4,6},{5,7},{6,4},{7,5},{8,10},{9,11},{10,... | collective-permute-start | bytes 196616 | tf_op jit(solution)/shard_map/ppermute | solution.py:21
  27.1 13.1 %collective-permute-done.1 = bf16[2,16,1024]{2,1,0:T(8,128)(2,1)S(1)} collective-permute-done((bf16[2,16,1024]{2,1,0:T(8,128)(2,1)S(1)}, bf16[2,16,1024]{2,1,0:T(8,128)(2,1)S(1)}, u32[]{:S(2)}, u32[]{:S(2)}) %collective-permute-start.1) | collective-permute-done | bytes 65568 | tf_op jit(solution)/shard_map/ppermute | solution.py:21
  41.0 28.9 %all-to-all-start = ((bf16[8,2,16,1024]{3,2,1,0:T(8,128)(2,1)}), bf16[8,2,16,1024]{3,2,1,0:T(8,128)(2,1)S(1)}, u32[]{:S(2)}, u32[]{:S(2)}) async-start(bf16[8,2,16,1024]{3,2,1,0:T(8,128)(2,1)} %broadcast_in_dim.23), calls=%async_computation | async-start | bytes 1048576 | tf_op jit(solution)/shard_map/all_to_all | solution.py:35
  69.9 1.9 collective-permute-start.7
  71.9 1.8 fusion.134
  74.8 11.1 %all-to-all-done = bf16[8,2,16,1024]{3,2,1,0:T(8,128)(2,1)S(1)} async-done(((bf16[8,2,16,1024]{3,2,1,0:T(8,128)(2,1)}), bf16[8,2,16,1024]{3,2,1,0:T(8,128)(2,1)S(1)}, u32[]{:S(2)}, u32[]{:S(2)}) %all-to-all-start) | async-done | bytes 524320 | tf_op jit(solution)/shard_map/all_to_all | solution.py:35
  85.9 1.6 broadcast_in_dim.24
  87.5 3.7 %all-to-all-start.1 = ((bf16[4,8,2,16,1024]{4,3,2,1,0:T(8,128)(2,1)}), bf16[4,8,2,16,1024]{4,3,2,1,0:T(8,128)(2,1)S(1)}, u32[]{:S(2)}, u32[]{:S(2)}) async-start(bf16[4,8,2,16,1024]{4,3,2,1,0:T(8,128)(2,1)} %broadcast_in_dim.24), calls=%async_computation.1 | async-start | bytes 4194304 | tf_op jit(solution)/shard_map/all_to_all | solution.py:35
  98.0 1.5 pad_maximum_fusion
  99.6 3.9 %copy.13 = bf16[1024,1024]{1,0:T(8,128)(2,1)} copy(bf16[1024,1024]{0,1:T(8,128)(2,1)} %pad_maximum_fusion) | data formatting | bytes 4194304 | tf_op jit(solution)/shard_map/concatenate | solution.py:124
  103.5 3.2 %copy.14 = bf16[4,8,32,1024]{3,2,1,0:T(8,128)(2,1)} copy(bf16[4,8,32,1024]{3,2,0,1:T(8,128)(2,1)} %bitcast.63) | data formatting | bytes 4194304 | tf_op jit(solution)/shard_map/transpose | solution.py:125
  106.7 7.5 %all-to-all-done.1 = bf16[4,8,2,16,1024]{4,3,2,1,0:T(8,128)(2,1)S(1)} async-done(((bf16[4,8,2,16,1024]{4,3,2,1,0:T(8,128)(2,1)}), bf16[4,8,2,16,1024]{4,3,2,1,0:T(8,128)(2,1)S(1)}, u32[]{:S(2)}, u32[]{:S(2)}) %all-to-all-start.1) | async-done | bytes 2097184 | tf_op jit(solution)/shard_map/all_to_all | solution.py:35
  114.2 4.4 %all-to-all-start.2 = ((bf16[4,8,32,1024]{3,2,1,0:T(8,128)(2,1)}), bf16[4,8,32,1024]{3,2,1,0:T(8,128)(2,1)}, u32[]{:S(2)}, u32[]{:S(2)}) async-start(bf16[4,8,32,1024]{3,2,1,0:T(8,128)(2,1)} %copy.14), calls=%async_computation.2 | async-start | bytes 4194304 | tf_op jit(solution)/shard_map/all_to_all | solution.py:39
  118.7 3.4 %fusion.24 = f32[256,1024]{1,0:T(8,128)} fusion(bf16[1,512,1024]{2,1,0:T(8,128)(2,1)} %param.10, bf16[1,512,1024]{2,1,0:T(8,128)(2,1)} %param.9, f32[1024]{0:T(1024)S(1)} %bitcast.81, f32[256]{0:T(256)S(1)} %add_rsqrt_fusion.2, bf16[128,1024]{1,0:T(8,128)(2,1)S(1)} %get-tuple-element.10, bf16[128,1024]{1,0:T(8,128)(2,1)S(1)} %bitcast.69), kind=kOutput, calls=%fused_computation.38 | convolution fusion | flops 539885568 | bytes 3675136 | tf_op jit(solution)/shard_map/dot_general | solution.py:68
  122.1 2.6 %fusion.28 = f32[256,1024]{1,0:T(8,128)} fusion(bf16[256,512]{1,0:T(8,128)(2,1)S(1)} %fusion, bf16[1,512,1024]{2,1,0:T(8,128)(2,1)} %param.9), kind=kOutput, calls=%fused_computation.42 | convolution fusion | flops 268435456 | bytes 2359296 | tf_op jit(solution)/shard_map/dot_general | solution.py:68
  124.8 1.2 fusion.132
  126.0 1.3 fusion.136
  127.3 2.8 %convolution_add_fusion = f32[256,1024]{1,0:T(8,128)S(1)} fusion(f32[256,1024]{1,0:T(8,128)} %fusion.28, bf16[512,1024]{1,0:T(8,128)(2,1)S(1)} %bitcast.65, bf16[512,1024]{1,0:T(8,128)(2,1)} %bitcast.76, f32[256,512]{1,0:T(8,128)} %fusion.136, bf16[128,1024]{1,0:T(8,128)(2,1)S(1)} %copy-done.12, bf16[128,1024]{1,0:T(8,128)(2,1)S(1)} %bitcast.75), kind=kOutput, calls=%fused_computation.3 | convolution fusion | flops 540672000 | bytes 5242880 | tf_op jit(solution)/shard_map/dot_general | solution.py:68
  130.9 1.9 collective-permute-start.4
  132.8 3.4 %convolution_add_fusion.1 = f32[256,1024]{1,0:T(8,128)} fusion(f32[256,1024]{1,0:T(8,128)} %fusion.24, bf16[512,1024]{1,0:T(8,128)(2,1)} %bitcast.77, bf16[512,1024]{1,0:T(8,128)(2,1)S(1)} %bitcast.66, f32[1024]{0:T(1024)S(1)} %bitcast.82, f32[256]{0:T(256)S(1)} %add_rsqrt_fusion.2, bf16[128,1024]{1,0:T(8,128)(2,1)S(1)} %copy-done.9, ...), kind=kOutput, calls=%fused_computation.4 | convolution fusion | flops 540147712 | bytes 4723712 | tf_op jit(solution)/shard_map/dot_general | solution.py:68
  136.2 1.8 slice.94
  138.0 2.4 %collective-permute-start.2 = (bf16[128,1024]{1,0:T(8,128)(2,1)}, bf16[128,1024]{1,0:T(8,128)(2,1)}, u32[]{:S(2)}, u32[]{:S(2)}) collective-permute-start(bf16[128,1024]{1,0:T(8,128)(2,1)} %slice.94), channel_id=1, source_target_pairs={{0,1},{1,0},{2,3},{3,2},{4,5},{5,4},{6,7},{7,6},{8,9},{9,8},{10,11... | collective-permute-start | bytes 786440 | tf_op jit(solution)/shard_map/ppermute | solution.py:25
  141.0 2.9 %reduce_sum.74 = bf16[8,32,1024]{2,1,0:T(8,128)(2,1)} reduce(bf16[4,8,32,1024]{3,2,1,0:T(8,128)(2,1)} %all-to-all-done.2, bf16[]{:T(256)} %constant.66.clone.1), dimensions={0}, to_apply=%region_5.6 | reduce | flops 786432 | bytes 2621442 | tf_op jit(solution)/shard_map/reduce_sum | solution.py:40
  143.9 12.4 %all-to-all-start.3 = ((bf16[8,32,1024]{2,1,0:T(8,128)(2,1)}), bf16[8,32,1024]{2,1,0:T(8,128)(2,1)S(1)}, u32[]{:S(2)}, u32[]{:S(2)}) async-start(bf16[8,32,1024]{2,1,0:T(8,128)(2,1)} %reduce_sum.74), calls=%async_computation.3 | async-start | bytes 1048576 | tf_op jit(solution)/shard_map/all_to_all | solution.py:39
  156.3 1.2 fusion.44
  157.5 1.2 fusion.49
  158.7 3.0 %collective-permute-start.5 = (bf16[128,1024]{1,0:T(8,128)(2,1)S(1)}, bf16[128,1024]{1,0:T(8,128)(2,1)S(1)}, u32[]{:S(2)}, u32[]{:S(2)}) collective-permute-start(bf16[128,1024]{1,0:T(8,128)(2,1)S(1)} %fusion.49), channel_id=1, source_target_pairs={{0,896},{128,0},{256,128},{384,256},{512,384},{640,512},{768,640},... | collective-permute-start | bytes 786440 | tf_op jit(solution)/shard_map/ppermute | solution.py:30
  162.8 17.3 %collective-permute-start.3 = (bf16[128,1024]{1,0:T(8,128)(2,1)S(1)}, bf16[128,1024]{1,0:T(8,128)(2,1)S(1)}, u32[]{:S(2)}, u32[]{:S(2)}) collective-permute-start(bf16[128,1024]{1,0:T(8,128)(2,1)S(1)} %fusion.69), channel_id=1, source_target_pairs={{0,128},{128,256},{256,384},{384,512},{512,640},{640,768},{768,896... | collective-permute-start | bytes 786440 | tf_op jit(solution)/shard_map/ppermute | solution.py:30
  180.1 1.3 collective-permute-done.5
  181.4 11.6 %collective-permute-done.3 = bf16[128,1024]{1,0:T(8,128)(2,1)S(1)} collective-permute-done((bf16[128,1024]{1,0:T(8,128)(2,1)S(1)}, bf16[128,1024]{1,0:T(8,128)(2,1)S(1)}, u32[]{:S(2)}, u32[]{:S(2)}) %collective-permute-start.3) | collective-permute-done | bytes 262176 | tf_op jit(solution)/shard_map/ppermute | solution.py:30
  (67 shorter events, 16.2 us)
Async XLA Ops:
  1.8 71.8 %collective-permute-start = (bf16[384,1024]{1,0:T(8,128)(2,1)S(1)}, bf16[384,1024]{1,0:T(8,128)(2,1)S(1)}, u32[]{:S(2)}, u32[]{:S(2)}) collective-permute-start(bf16[384,1024]{1,0:T(8,128)(2,1)S(1)} %pad_maximum_fusion.1), channel_id=1, source_target_pairs={{0,1},{1,0},{2,3},{3,2},{4,5},{5,4},{6,7},{7,6},{8,9},{9,8},{10,11... | collective-permute-start | bytes 2359304 | tf_op jit(solution)/shard_map/ppermute | solution.py:25
  4.8 65.2 %collective-permute-start.6 = (bf16[256,1024]{1,0:T(8,128)(2,1)S(1)}, bf16[256,1024]{1,0:T(8,128)(2,1)}, u32[]{:S(2)}, u32[]{:S(2)}) collective-permute-start(bf16[256,1024]{1,0:T(8,128)(2,1)S(1)} %pad_maximum_fusion.2), channel_id=1, source_target_pairs={{0,2},{1,3},{2,0},{3,1},{4,6},{5,7},{6,4},{7,5},{8,10},{9,11},{10,... | collective-permute-start | bytes 1572872 | tf_op jit(solution)/shard_map/ppermute | solution.py:21
  25.0 49.4 %copy-start = (bf16[1,128,1024]{2,1,0:T(8,128)(2,1)S(1)}, bf16[1,128,1024]{2,1,0:T(8,128)(2,1)}, u32[]{:S(2)}) copy-start(bf16[1,128,1024]{2,1,0:T(8,128)(2,1)} %param.7) | copy-start | bytes 786436
  25.0 15.2 %collective-permute-start.1 = (bf16[2,16,1024]{2,1,0:T(8,128)(2,1)S(1)}, bf16[2,16,1024]{2,1,0:T(8,128)(2,1)S(1)}, u32[]{:S(2)}, u32[]{:S(2)}) collective-permute-start(bf16[2,16,1024]{2,1,0:T(8,128)(2,1)S(1)} %pad_maximum_fusion.10), channel_id=1, source_target_pairs={{0,2},{1,3},{2,0},{3,1},{4,6},{5,7},{6,4},{7,5},{8,10},{9,11},{10,... | collective-permute-start | bytes 196616 | tf_op jit(solution)/shard_map/ppermute | solution.py:21
  41.0 33.5 %copy-start.1 = (bf16[1,128,1024]{2,1,0:T(8,128)(2,1)S(1)}, bf16[1,128,1024]{2,1,0:T(8,128)(2,1)}, u32[]{:S(2)}) copy-start(bf16[1,128,1024]{2,1,0:T(8,128)(2,1)} %param.6) | copy-start | bytes 786436
  41.0 44.9 %all-to-all-start = ((bf16[8,2,16,1024]{3,2,1,0:T(8,128)(2,1)}), bf16[8,2,16,1024]{3,2,1,0:T(8,128)(2,1)S(1)}, u32[]{:S(2)}, u32[]{:S(2)}) async-start(bf16[8,2,16,1024]{3,2,1,0:T(8,128)(2,1)} %broadcast_in_dim.23), calls=%async_computation | async-start | bytes 1048576 | tf_op jit(solution)/shard_map/all_to_all | solution.py:35
  69.9 21.3 %collective-permute-start.7 = (bf16[256,1024]{1,0:T(8,128)(2,1)}, bf16[256,1024]{1,0:T(8,128)(2,1)}, u32[]{:S(2)}, u32[]{:S(2)}) collective-permute-start(bf16[256,1024]{1,0:T(8,128)(2,1)} %collective-permute-done.6), channel_id=1, source_target_pairs={{0,1},{1,0},{2,3},{3,2},{4,5},{5,4},{6,7},{7,6},{8,9},{9,8},{10,11... | collective-permute-start | bytes 1572872 | tf_op jit(solution)/shard_map/ppermute | solution.py:25
  74.4 44.3 %copy-start.8 = (bf16[128,1024]{1,0:T(8,128)(2,1)}, bf16[128,1024]{1,0:T(8,128)(2,1)S(1)}, u32[]{:S(2)}) copy-start(bf16[128,1024]{1,0:T(8,128)(2,1)S(1)} %get-tuple-element.10) | copy-start | bytes 786436
  87.5 5.1 %copy-start.14 = (f32[1,1024]{1,0:T(1,128)S(1)}, f32[1,1024]{1,0:T(1,128)}, u32[]{:S(2)}) copy-start(f32[1,1024]{1,0:T(1,128)} %param.11) | copy-start | bytes 12292
  87.5 26.8 %all-to-all-start.1 = ((bf16[4,8,2,16,1024]{4,3,2,1,0:T(8,128)(2,1)}), bf16[4,8,2,16,1024]{4,3,2,1,0:T(8,128)(2,1)S(1)}, u32[]{:S(2)}, u32[]{:S(2)}) async-start(bf16[4,8,2,16,1024]{4,3,2,1,0:T(8,128)(2,1)} %broadcast_in_dim.24), calls=%async_computation.1 | async-start | bytes 4194304 | tf_op jit(solution)/shard_map/all_to_all | solution.py:35
  91.2 1.7 copy-start.7
  92.6 1.0 copy-start.3
  92.6 1.0 copy-start.11
  92.6 1.6 copy-start.15
  92.9 3.6 %copy-start.5 = (bf16[256,1024]{1,0:T(8,128)(2,1)}, bf16[256,1024]{1,0:T(8,128)(2,1)S(1)}, u32[]{:S(2)}) copy-start(bf16[256,1024]{1,0:T(8,128)(2,1)S(1)} %get-tuple-element.18) | copy-start | bytes 1572868
  94.8 1.0 copy-start.13
  114.2 26.7 %all-to-all-start.2 = ((bf16[4,8,32,1024]{3,2,1,0:T(8,128)(2,1)}), bf16[4,8,32,1024]{3,2,1,0:T(8,128)(2,1)}, u32[]{:S(2)}, u32[]{:S(2)}) async-start(bf16[4,8,32,1024]{3,2,1,0:T(8,128)(2,1)} %copy.14), calls=%async_computation.2 | async-start | bytes 4194304 | tf_op jit(solution)/shard_map/all_to_all | solution.py:39
  124.8 1.2 copy-start.6
  126.0 1.3 copy-start.4
  126.0 1.3 copy-start.12
  127.3 5.5 %copy-start.2 = (bf16[1,128,1024]{2,1,0:T(8,128)(2,1)S(1)}, bf16[1,128,1024]{2,1,0:T(8,128)(2,1)}, u32[]{:S(2)}) copy-start(bf16[1,128,1024]{2,1,0:T(8,128)(2,1)} %param.6) | copy-start | bytes 786436
  127.3 5.5 %copy-start.9 = (bf16[128,1024]{1,0:T(8,128)(2,1)S(1)}, bf16[128,1024]{1,0:T(8,128)(2,1)}, u32[]{:S(2)}) copy-start(bf16[128,1024]{1,0:T(8,128)(2,1)} %copy-done.8) | copy-start | bytes 786436
  130.9 25.4 %collective-permute-start.4 = (bf16[128,1024]{1,0:T(8,128)(2,1)}, bf16[128,1024]{1,0:T(8,128)(2,1)}, u32[]{:S(2)}, u32[]{:S(2)}) collective-permute-start(bf16[128,1024]{1,0:T(8,128)(2,1)} %slice.93), channel_id=1, source_target_pairs={{0,1},{1,0},{2,3},{3,2},{4,5},{5,4},{6,7},{7,6},{8,9},{9,8},{10,11... | collective-permute-start | bytes 786440 | tf_op jit(solution)/shard_map/ppermute | solution.py:25
  138.0 23.7 %collective-permute-start.2 = (bf16[128,1024]{1,0:T(8,128)(2,1)}, bf16[128,1024]{1,0:T(8,128)(2,1)}, u32[]{:S(2)}, u32[]{:S(2)}) collective-permute-start(bf16[128,1024]{1,0:T(8,128)(2,1)} %slice.94), channel_id=1, source_target_pairs={{0,1},{1,0},{2,3},{3,2},{4,5},{5,4},{6,7},{7,6},{8,9},{9,8},{10,11... | collective-permute-start | bytes 786440 | tf_op jit(solution)/shard_map/ppermute | solution.py:25
  143.9 17.8 %copy-start.10 = (f32[256,1024]{1,0:T(8,128)S(1)}, f32[256,1024]{1,0:T(8,128)}, u32[]{:S(2)}) copy-start(f32[256,1024]{1,0:T(8,128)} %convolution_add_fusion.1) | copy-start | bytes 3145732
  143.9 49.1 %all-to-all-start.3 = ((bf16[8,32,1024]{2,1,0:T(8,128)(2,1)}), bf16[8,32,1024]{2,1,0:T(8,128)(2,1)S(1)}, u32[]{:S(2)}, u32[]{:S(2)}) async-start(bf16[8,32,1024]{2,1,0:T(8,128)(2,1)} %reduce_sum.74), calls=%async_computation.3 | async-start | bytes 1048576 | tf_op jit(solution)/shard_map/all_to_all | solution.py:39
  158.7 22.7 %collective-permute-start.5 = (bf16[128,1024]{1,0:T(8,128)(2,1)S(1)}, bf16[128,1024]{1,0:T(8,128)(2,1)S(1)}, u32[]{:S(2)}, u32[]{:S(2)}) collective-permute-start(bf16[128,1024]{1,0:T(8,128)(2,1)S(1)} %fusion.49), channel_id=1, source_target_pairs={{0,896},{128,0},{256,128},{384,256},{512,384},{640,512},{768,640},... | collective-permute-start | bytes 786440 | tf_op jit(solution)/shard_map/ppermute | solution.py:30
  162.8 30.2 %collective-permute-start.3 = (bf16[128,1024]{1,0:T(8,128)(2,1)S(1)}, bf16[128,1024]{1,0:T(8,128)(2,1)S(1)}, u32[]{:S(2)}, u32[]{:S(2)}) collective-permute-start(bf16[128,1024]{1,0:T(8,128)(2,1)S(1)} %fusion.69), channel_id=1, source_target_pairs={{0,128},{128,256},{256,384},{384,512},{512,640},{640,768},{768,896... | collective-permute-start | bytes 786440 | tf_op jit(solution)/shard_map/ppermute | solution.py:30

commit v2 on v1

v2 whole, which is shorter than its diff:
```python
import jax
import jax.numpy as jnp
from jax import lax
from jax.experimental import pallas as pl
from jax.experimental.pallas import tpu as pltpu
from jax.sharding import PartitionSpec as P


norm_eps = 1e-05
gelu_coef = 0.7978845608


NX, NY = 4, 8
x_groups = [[NX * y + x for x in range(NX)] for y in range(NY)]
y_groups = [[NX * y + x for y in range(NY)] for x in range(NX)]
other_chip = [(0, 2), (1, 3), (2, 0), (3, 1)]
other_core = [(0, 1), (1, 0), (2, 3), (3, 2)]

f32, bf16 = jnp.float32, jnp.bfloat16
CHUNK = 32
TILE = 256


def to_chip(x):
    return lax.ppermute(x, "mp", other_chip)


def to_core(x):
    return lax.ppermute(x, "mp", other_core)


def shifted(x, axis, by):
    length = lax.axis_size(axis)
    return lax.ppermute(x, axis, [(i, (i + by) % length) for i in range(length)])


def gathered(x, groups):
    copies = jnp.broadcast_to(x, (len(groups[0]), *x.shape))
    return lax.all_to_all(copies, "dp", 0, 0, tiled=True, axis_index_groups=groups)


def exchanged(x, groups):
    return lax.all_to_all(x, "dp", 0, 0, tiled=True, axis_index_groups=groups)


def gelu_both(v):
    t = jnp.tanh(gelu_coef * (v + 0.044715 * v * v * v))
    value = 0.5 * v * (1.0 + t)
    slope = 0.5 * (1.0 + t) + 0.5 * v * (1.0 - t * t) * gelu_coef * (1.0 + 0.134145 * v * v)
    return value, slope


def scale_of(xf):
    return lax.rsqrt(jnp.mean(xf * xf, axis=-1, keepdims=True) + norm_eps)


def nt(a, b):
    return lax.dot_general(a, b, (((1,), (1,)), ((), ())), preferred_element_type=f32)


def tn(a, b):
    return lax.dot_general(a, b, (((0,), (0,)), ((), ())), preferred_element_type=f32)


def nn(a, b):
    return jnp.dot(a, b, preferred_element_type=f32)


def norm_into(src, at, gain, dst, to, rows):
    def step(i, _):
        r = pl.multiple_of(i * CHUNK, CHUNK)
        x = src[pl.ds(at + r, CHUNK), :].astype(f32)
        dst[pl.ds(to + r, CHUNK), :] = (x * scale_of(x) * gain[...]).astype(bf16)

    lax.fori_loop(0, rows // CHUNK, step, None)


def own_kernel(xf, xb, ct, near, wi, wo, gain, nf, nb, c2, act, dp, br, dn, act_f):
    rows = xf.shape[0]
    norm_into(xf, 0, gain, nf, 0, rows)
    norm_into(near, 0, gain, nf, rows, rows)
    norm_into(xb, 0, gain, nb, 0, rows)
    norm_into(near, rows, gain, nb, rows, rows)
    c2[:rows, :] = ct[...]
    c2[rows:, :] = near[2 * rows :, :]

    def hidden(j, _):
        h = pl.ds(pl.multiple_of(j * TILE, TILE), TILE)
        value, _ = gelu_both(nt(nf[...], wi[h, :]))
        act_f[:, h] = value.astype(bf16)
        value, slope = gelu_both(nt(nb[...], wi[h, :]))
        act[:, h] = value.astype(bf16)
        dp[:, h] = (nt(c2[...], wo[h, :]) * slope).astype(bf16)

    lax.fori_loop(0, wi.shape[0] // TILE, hidden, None)

    def back(j, _):
        c = pl.ds(pl.multiple_of(j * TILE, TILE), TILE)
        br[:, c] = nn(act_f[...], wo[:, c])
        dn[:, c] = nn(dp[...], wi[:, c])

    lax.fori_loop(0, wi.shape[1] // TILE, back, None)


def rest_kernel(whole, nf, nb, c2, br, dn, keep, send, act_f, dp, wi, wo):
    rows = keep.shape[1]

    def split(i, _):
        r = pl.ds(pl.multiple_of(i * 16, 16), 16)
        wi[r, :] = whole[i, 0]
        wo[r, :] = whole[i, 1]

    lax.fori_loop(0, whole.shape[0], split, None)

    def hidden(j, _):
        h = pl.ds(pl.multiple_of(j * TILE, TILE), TILE)
        value, _ = gelu_both(nt(nf[...], wi[h, :]))
        act_f[:, h] = value.astype(bf16)
        _, slope = gelu_both(nt(nb[...], wi[h, :]))
        dp[:, h] = (nt(c2[...], wo[h, :]) * slope).astype(bf16)

    lax.fori_loop(0, wi.shape[0] // TILE, hidden, None)

    def back(j, _):
        c = pl.ds(pl.multiple_of(j * TILE, TILE), TILE)
        b = br[:, c] + nn(act_f[...], wo[:, c])
        keep[0, :, c] = b[:rows]
        send[0, :, c] = b[rows:].astype(bf16)
        g = dn[:, c] + nn(dp[...], wi[:, c])
        keep[1, :, c] = g[:rows]
        send[1, :, c] = g[rows:].astype(bf16)

    lax.fori_loop(0, wi.shape[1] // TILE, back, None)


def grad_kernel(far, far2, wi, wo, gain, nb, c2, act, dp, g, nb3, c3, act3, dp3):
    rows = far.shape[0] // 2
    hid = wi.shape[0]
    norm_into(far, 0, gain, nb3, 0, rows)
    norm_into(far2, 0, gain, nb3, rows, rows)
    c3[:rows, :] = far[rows:, :]
    c3[rows:, :] = far2[rows:, :]

    def hidden(j, _):
        h = pl.ds(pl.multiple_of(j * TILE, TILE), TILE)
        value, slope = gelu_both(nt(nb3[...], wi[h, :]))
        act3[:, h] = value.astype(bf16)
        dp3[:, h] = (nt(c3[...], wo[h, :]) * slope).astype(bf16)

    lax.fori_loop(0, hid // TILE, hidden, None)

    def grads(y, _):
        c = pl.ds(pl.multiple_of(y * 128, 128), 128)
        gi = tn(nb[:, c], dp[...]) + tn(nb3[:, c], dp3[...])
        g[:, y, :, :hid] = gi.astype(bf16).reshape(NX, 32, hid)
        go = tn(c2[:, c], act[...]) + tn(c3[:, c], act3[...])
        g[:, y, :, hid:] = go.astype(bf16).reshape(NX, 32, hid)

    lax.fori_loop(0, NY, grads, None)


def sum_kernel(pieces, total):
    total[...] = jnp.sum(pieces[...].astype(f32), axis=0).astype(bf16)


def local(kernel, outs, scratch, flops, moved):
    return pl.pallas_call(
        kernel,
        out_shape=[jax.ShapeDtypeStruct(s, t) for s, t in outs],
        scratch_shapes=[pltpu.VMEM(s, t) for s, t in scratch],
        compiler_params=pltpu.CompilerParams(vmem_limit_bytes=28 * 2**20),
        cost_estimate=pl.CostEstimate(flops=flops, bytes_accessed=moved, transcendentals=0),
    )


def layer(fwd_in, stash, cot, w_in, w_out, gain):
    xf, xb, ct = fwd_in[0], stash[0], cot[0]
    wi, wo = w_in[0], w_out[0]
    rows, dim = xf.shape
    hid = wi.shape[0]
    both = 2 * rows
    n_dp = lax.axis_size("dp")
    d = lax.axis_index("dp")
    part = hid // n_dp
    at = (d % NX * NY + d // NX) * part
    mine = jnp.stack(
        [lax.dynamic_slice_in_dim(wi, at, part, 0), lax.dynamic_slice_in_dim(wo, at, part, 0)]
    )
    piece = to_chip(mine)
    far = to_chip(jnp.concatenate([xb, ct]))
    near = to_core(jnp.concatenate([xf, xb, ct]))
    nf, nb, c2, act, dp, br, dn = local(
        own_kernel,
        [((both, dim), bf16)] * 3 + [((both, hid), bf16)] * 2 + [((both, dim), f32)] * 2,
        [((both, hid), bf16)],
        10 * both * hid * dim,
        8 * 2**20,
    )(xf, xb, ct, near, wi, wo, gain)
    col = gathered(piece, y_groups)
    whole = gathered(col, x_groups).reshape(n_dp, 2, part, dim)
    keep, send = local(
        rest_kernel,
        [((2, rows, dim), f32), ((2, rows, dim), bf16)],
        [((both, hid), bf16)] * 2 + [((hid, dim), bf16)] * 2,
        10 * both * hid * dim,
        8 * 2**20,
    )(whole, nf, nb, c2, br, dn)
    sums = keep + to_core(send).astype(f32)
    out = (xf.astype(f32) + sums[0]).astype(bf16)
    passed_fwd = shifted(out, "section", 1)
    shard_x = xb.astype(f32)
    scale = scale_of(shard_x)
    push = sums[1] * gain
    mixed = jnp.mean(shard_x * push, axis=-1, keepdims=True)
    dx = ct.astype(f32) + scale * push - shard_x * scale * scale * scale * mixed
    passed_grad = shifted(dx.astype(bf16), "section", -1)
    far2 = to_core(far)
    (g,) = local(
        grad_kernel,
        [((NX, NY, dim // n_dp, 2 * hid), bf16)],
        [((both, dim), bf16)] * 2 + [((both, hid), bf16)] * 2,
        12 * both * hid * dim,
        8 * 2**20,
    )(far, far2, wi, wo, gain, nb, c2, act, dp)
    g = exchanged(g, x_groups)
    g = pl.pallas_call(
        sum_kernel,
        grid=(NY,),
        in_specs=[pl.BlockSpec((NX, 1, *g.shape[2:]), lambda i: (0, i, 0, 0))],
        out_specs=pl.BlockSpec((1, *g.shape[2:]), lambda i: (i, 0, 0)),
        out_shape=jax.ShapeDtypeStruct(g.shape[1:], bf16),
        compiler_params=pltpu.CompilerParams(vmem_limit_bytes=16 * 2**20),
        cost_estimate=pl.CostEstimate(flops=2**21, bytes_accessed=2**21, transcendentals=0),
    )(g)
    g = exchanged(g, y_groups)
    g = jnp.sum(g.astype(f32), axis=0).astype(bf16)
    return (passed_fwd[None], passed_grad[None], g[:, :hid].T[None], g[:, hid:].T[None])


def solution(mesh):
    in_specs = (
        P("section", ("dp", "mp"), None),
        P("section", ("dp", "mp"), None),
        P("section", ("dp", "mp"), None),
        P("section", "mp", None),
        P("section", "mp", None),
        P("section", None),
    )
    out_specs = (
        P("section", ("dp", "mp"), None),
        P("section", ("dp", "mp"), None),
        P("section", "mp", "dp"),
        P("section", "mp", "dp"),
    )
    return jax.shard_map(layer, mesh=mesh, in_specs=in_specs, out_specs=out_specs, check_vma=False)
```

time: 196 us -> 183 us (0.934)
  the two profiles are of different devices: /device:TPU:8 before, /device:TPU:1 now
where the time goes in v2:
time: 183 us; the launch traced here: 182 us
  starting transfers between devices  102 us (56%)
  waiting for transfers between devices  25.1 us (14%)
  blocking collectives  19.6 us (11%)
  Pallas kernels  17.6 us (10%)
  local copies, waits for them, and re-layouts  16.5 us (9%)
    all_to_all x2, starting transfers between devices, exchanged(): return lax.all_to_all(x, 'dp', 0, 0, tiled=True, axis_index_groups=groups)  33.8 us
    ppermute x2, starting transfers between devices, to_chip(): return lax.ppermute(x, 'mp', other_chip)  31.7 us
    ppermute x3, starting transfers between devices, to_core(): return lax.ppermute(x, 'mp', other_core)  20.1 us
    all_to_all x1, blocking collectives, gathered(): lax.all_to_all(copies, 'dp', 0, 0, tiled=True, axis_index_groups=groups)  19.6 us
    unnamed x38, local copies, waits for them, and re-layouts  13.4 us
    all_to_all x2, waiting for transfers between devices, exchanged(): return lax.all_to_all(x, 'dp', 0, 0, tiled=True, axis_index_groups=groups)  12.8 us
    ppermute x2, starting transfers between devices, shifted(): lax.ppermute(x, axis, [(i, (i + by) % length) for i in range(length)])  11.9 us
    ppermute x2, waiting for transfers between devices, shifted(): lax.ppermute(x, axis, [(i, (i + by) % length) for i in range(length)])  10.4 us
  transfers between devices with their start and end apart: 10, of which 4 were waited for; matrix products, arithmetic and copies ran while one was open for 0% of the time, Pallas kernels for 10%

profile of v2, /device:TPU:1, one launch (start us, length us, event | category | flops | bytes accessed | tf_op | source)
XLA Modules:
  0.0 182.2 jit_solution(16380278648136894411)
XLA Ops:
  0.7 0.8 constant_dynamic-slice_fusion
  1.5 19.9 %collective-permute-start = (bf16[2,16,1024]{2,1,0:T(8,128)(2,1)S(1)}, bf16[2,16,1024]{2,1,0:T(8,128)(2,1)S(1)}, u32[]{:S(2)}, u32[]{:S(2)}) collective-permute-start(bf16[2,16,1024]{2,1,0:T(8,128)(2,1)S(1)} %pad_maximum_fusion.2), channel_id=1, source_target_pairs={{0,2},{1,3},{2,0},{3,1},{4,6},{5,7},{6,4},{7,5},{8,10},{9,11},{10,... | collective-permute-start | bytes 196616 | tf_op jit(solution)/shard_map/ppermute | solution.py:25
  21.4 1.8 collective-permute-done
  23.2 19.6 %all_to_all.20 = bf16[8,2,16,1024]{3,2,1,0:T(8,128)(2,1)S(1)} all-to-all(bf16[8,2,16,1024]{3,2,1,0:T(8,128)(2,1)S(1)} %broadcast_in_dim.20), channel_id=1, replica_groups={{0,16,32,48,64,80,96,112},{4,20,36,52,68,84,100,116},{8,24,40,56,72,88,..., dimensions={0} | all-to-all | bytes 1048576 | tf_op jit(solution)/shard_map/all_to_all | solution.py:39
  42.9 1.6 broadcast_in_dim.21
  44.5 4.1 %all-to-all-start.1 = ((bf16[4,8,2,16,1024]{4,3,2,1,0:T(8,128)(2,1)}), bf16[4,8,2,16,1024]{4,3,2,1,0:T(8,128)(2,1)S(1)}, u32[]{:S(2)}, u32[]{:S(2)}) async-start(bf16[4,8,2,16,1024]{4,3,2,1,0:T(8,128)(2,1)} %broadcast_in_dim.21), calls=%async_computation.1 | async-start | bytes 4194304 | tf_op jit(solution)/shard_map/all_to_all | solution.py:39
  48.7 11.8 %collective-permute-start.5 = (bf16[256,1024]{1,0:T(8,128)(2,1)S(1)}, bf16[256,1024]{1,0:T(8,128)(2,1)S(1)}, u32[]{:S(2)}, u32[]{:S(2)}) collective-permute-start(bf16[256,1024]{1,0:T(8,128)(2,1)S(1)} %pad_maximum_fusion.1), channel_id=1, source_target_pairs={{0,2},{1,3},{2,0},{3,1},{4,6},{5,7},{6,4},{7,5},{8,10},{9,11},{10,... | collective-permute-start | bytes 1572872 | tf_op jit(solution)/shard_map/ppermute | solution.py:25
  60.5 8.4 %collective-permute-start.1 = (bf16[384,1024]{1,0:T(8,128)(2,1)S(1)}, bf16[384,1024]{1,0:T(8,128)(2,1)S(1)}, u32[]{:S(2)}, u32[]{:S(2)}) collective-permute-start(bf16[384,1024]{1,0:T(8,128)(2,1)S(1)} %pad_maximum_fusion), channel_id=1, source_target_pairs={{0,1},{1,0},{2,3},{3,2},{4,5},{5,4},{6,7},{7,6},{8,9},{9,8},{10,11... | collective-permute-start | bytes 2359304 | tf_op jit(solution)/shard_map/ppermute | solution.py:29
  69.0 9.5 %collective-permute-start.6 = (bf16[256,1024]{1,0:T(8,128)(2,1)S(1)}, bf16[256,1024]{1,0:T(8,128)(2,1)S(1)}, u32[]{:S(2)}, u32[]{:S(2)}) collective-permute-start(bf16[256,1024]{1,0:T(8,128)(2,1)S(1)} %collective-permute-done.5.far), channel_id=1, source_target_pairs={{0,1},{1,0},{2,3},{3,2},{4,5},{5,4},{6,7},{7,6},{8,9},{9,8},{10,11... | collective-permute-start | bytes 1572872 | tf_op jit(solution)/shard_map/ppermute | solution.py:29
  78.5 4.7 %shard_map.93 = (bf16[256,1024]{1,0:T(8,128)(2,1)S(1)}, bf16[256,1024]{1,0:T(8,128)(2,1)S(1)}, bf16[256,1024]{1,0:T(8,128)(2,1)S(1)}, bf16[256,512]{1,0:T(8,128)...) custom-call(bf16[128,1024]{1,0:T(8,128)(2,1)S(1)} %bitcast.48, ...), custom_call_target="tpu_custom_call" | custom-call | flops 1342177280 | bytes 8388608 | tf_op jit(solution)/shard_map/pallas_call | solution.py:192
  83.2 1.0 copy-done.11
  84.2 1.0 copy-done.13
  85.2 0.8 copy-done.15
  86.0 6.3 %shard_map.95 = bf16[4,8,32,1024]{3,2,1,0:T(8,128)(2,1)} custom-call(bf16[256,1024]{1,0:T(8,128)(2,1)S(1)} %collective-permute-done.5.far, bf16[256,1024]{1,0:T(8,128)(2,1)S(1)} %collective-permute-done.6.far2, bf16[512,1024]{1,0:T(8,128)(2,1)S(1)} %bitcast.46, bf16[512,1024]{1,0:T(8,128)(2,1)S(1)} %bitcast.44, f32[1,1024]{1,0:T(1,128)S(1)} %copy-done.17, ...), custom_call_target="tpu_custom_call" | custom-call | flops 1610612736 | bytes 8388608 | tf_op jit(solution)/shard_map/pallas_call | solution.py:218
  92.3 0.8 copy-done.4
  93.1 1.3 copy-done
  94.4 4.5 %all-to-all-start.2 = ((bf16[4,8,32,1024]{3,2,1,0:T(8,128)(2,1)}), bf16[4,8,32,1024]{3,2,1,0:T(8,128)(2,1)S(1)}, u32[]{:S(2)}, u32[]{:S(2)}) async-start(bf16[4,8,32,1024]{3,2,1,0:T(8,128)(2,1)} %shard_map.95), calls=%async_computation.2 | async-start | bytes 4194304 | tf_op jit(solution)/shard_map/all_to_all | solution.py:43
  98.9 1.6 copy-done.1
  100.5 1.0 copy-done.5
  101.5 1.2 copy-done.12
  102.8 1.2 copy-done.14
  104.0 1.0 copy-done.16
  105.0 3.9 %shard_map.94 = (f32[2,128,1024]{2,1,0:T(8,128)S(1)}, bf16[2,128,1024]{2,1,0:T(8,128)(2,1)}) custom-call(bf16[32,2,16,1024]{3,2,1,0:T(8,128)(2,1)S(1)} %bitcast.36, bf16[256,1024]{1,0:T(8,128)(2,1)S(1)} %copy-done.16, bf16[256,1024]{1,0:T(8,128)(2,1)S(1)} %get-tuple-element.14.nb, bf16[256,1024]{1,0:T(8,128)(2,1)S(1)} %copy-done.5, ...), custom_call_target="tpu_custom_call" | custom-call | flops 1342177280 | bytes 8388608 | tf_op jit(solution)/shard_map/pallas_call | solution.py:201
  108.9 1.0 copy-done.8
  109.9 2.2 %collective-permute-start.2 = (bf16[2,128,1024]{2,1,0:T(8,128)(2,1)}, bf16[2,128,1024]{2,1,0:T(8,128)(2,1)S(1)}, u32[]{:S(2)}, u32[]{:S(2)}) collective-permute-start(bf16[2,128,1024]{2,1,0:T(8,128)(2,1)} %get-tuple-element.19), channel_id=1, source_target_pairs={{0,1},{1,0},{2,3},{3,2},{4,5},{5,4},{6,7},{7,6},{8,9},{9,8},{10,11... | collective-permute-start | bytes 1572872 | tf_op jit(solution)/shard_map/ppermute | solution.py:29
  112.1 12.8 %all-to-all-done.2.pieces = bf16[4,8,32,1024]{3,2,1,0:T(8,128)(2,1)S(1)} async-done(((bf16[4,8,32,1024]{3,2,1,0:T(8,128)(2,1)}), bf16[4,8,32,1024]{3,2,1,0:T(8,128)(2,1)S(1)}, u32[]{:S(2)}, u32[]{:S(2)}) %all-to-all-start.2) | async-done | bytes 2097184 | tf_op jit(solution)/shard_map/all_to_all | solution.py:43
  125.0 2.8 %shard_map.96 = bf16[8,32,1024]{2,1,0:T(8,128)(2,1)} custom-call(bf16[4,8,32,1024]{3,2,1,0:T(8,128)(2,1)S(1)} %all-to-all-done.2.pieces), custom_call_target="tpu_custom_call" | custom-call | flops 2097152 | bytes 2097152 | tf_op jit(solution)/shard_map/pallas_call | solution.py:226
  127.8 29.3 %all-to-all-start.3 = ((bf16[8,32,1024]{2,1,0:T(8,128)(2,1)}), bf16[8,32,1024]{2,1,0:T(8,128)(2,1)S(1)}, u32[]{:S(2)}, u32[]{:S(2)}) async-start(bf16[8,32,1024]{2,1,0:T(8,128)(2,1)} %shard_map.96), calls=%async_computation.3 | async-start | bytes 1048576 | tf_op jit(solution)/shard_map/all_to_all | solution.py:43
  157.7 10.0 %collective-permute-start.3 = (bf16[128,1024]{1,0:T(8,128)(2,1)S(1)}, bf16[128,1024]{1,0:T(8,128)(2,1)S(1)}, u32[]{:S(2)}, u32[]{:S(2)}) collective-permute-start(bf16[128,1024]{1,0:T(8,128)(2,1)S(1)} %get-tuple-element.25), channel_id=1, source_target_pairs={{0,128},{128,256},{256,384},{384,512},{512,640},{640,768},{768,896... | collective-permute-start | bytes 786440 | tf_op jit(solution)/shard_map/ppermute | solution.py:34
  167.8 1.9 %collective-permute-start.4 = (bf16[128,1024]{1,0:T(8,128)(2,1)S(1)}, bf16[128,1024]{1,0:T(8,128)(2,1)S(1)}, u32[]{:S(2)}, u32[]{:S(2)}) collective-permute-start(bf16[128,1024]{1,0:T(8,128)(2,1)S(1)} %get-tuple-element.24), channel_id=1, source_target_pairs={{0,896},{128,0},{256,128},{384,256},{512,384},{640,512},{768,640},... | collective-permute-start | bytes 786440 | tf_op jit(solution)/shard_map/ppermute | solution.py:34
  169.7 2.9 %collective-permute-done.3 = bf16[128,1024]{1,0:T(8,128)(2,1)S(1)} collective-permute-done((bf16[128,1024]{1,0:T(8,128)(2,1)S(1)}, bf16[128,1024]{1,0:T(8,128)(2,1)S(1)}, u32[]{:S(2)}, u32[]{:S(2)}) %collective-permute-start.3) | collective-permute-done | bytes 262176 | tf_op jit(solution)/shard_map/ppermute | solution.py:34
  172.6 7.5 %collective-permute-done.4 = bf16[128,1024]{1,0:T(8,128)(2,1)S(1)} collective-permute-done((bf16[128,1024]{1,0:T(8,128)(2,1)S(1)}, bf16[128,1024]{1,0:T(8,128)(2,1)S(1)}, u32[]{:S(2)}, u32[]{:S(2)}) %collective-permute-start.4) | collective-permute-done | bytes 262176 | tf_op jit(solution)/shard_map/ppermute | solution.py:34
  (44 shorter events, 2.9 us)
Async XLA Ops:
  1.5 21.7 %collective-permute-start = (bf16[2,16,1024]{2,1,0:T(8,128)(2,1)S(1)}, bf16[2,16,1024]{2,1,0:T(8,128)(2,1)S(1)}, u32[]{:S(2)}, u32[]{:S(2)}) collective-permute-start(bf16[2,16,1024]{2,1,0:T(8,128)(2,1)S(1)} %pad_maximum_fusion.2), channel_id=1, source_target_pairs={{0,2},{1,3},{2,0},{3,1},{4,6},{5,7},{6,4},{7,5},{8,10},{9,11},{10,... | collective-permute-start | bytes 196616 | tf_op jit(solution)/shard_map/ppermute | solution.py:25
  44.5 4.2 %copy-start.2 = (bf16[1,128,1024]{2,1,0:T(8,128)(2,1)S(1)}, bf16[1,128,1024]{2,1,0:T(8,128)(2,1)}, u32[]{:S(2)}) copy-start(bf16[1,128,1024]{2,1,0:T(8,128)(2,1)} %param.7) | copy-start | bytes 786436
  44.5 4.2 %copy-start.3 = (bf16[1,128,1024]{2,1,0:T(8,128)(2,1)S(1)}, bf16[1,128,1024]{2,1,0:T(8,128)(2,1)}, u32[]{:S(2)}) copy-start(bf16[1,128,1024]{2,1,0:T(8,128)(2,1)} %param.8) | copy-start | bytes 786436
  44.5 16.0 %copy-start.10 = (bf16[1,128,1024]{2,1,0:T(8,128)(2,1)S(1)}, bf16[1,128,1024]{2,1,0:T(8,128)(2,1)}, u32[]{:S(2)}) copy-start(bf16[1,128,1024]{2,1,0:T(8,128)(2,1)} %param.6) | copy-start | bytes 786436
  44.5 48.6 %all-to-all-start.1 = ((bf16[4,8,2,16,1024]{4,3,2,1,0:T(8,128)(2,1)}), bf16[4,8,2,16,1024]{4,3,2,1,0:T(8,128)(2,1)S(1)}, u32[]{:S(2)}, u32[]{:S(2)}) async-start(bf16[4,8,2,16,1024]{4,3,2,1,0:T(8,128)(2,1)} %broadcast_in_dim.21), calls=%async_computation.1 | async-start | bytes 4194304 | tf_op jit(solution)/shard_map/all_to_all | solution.py:39
  48.6 29.9 %copy-start.6 = (bf16[1,512,1024]{2,1,0:T(8,128)(2,1)S(1)}, bf16[1,512,1024]{2,1,0:T(8,128)(2,1)}, u32[]{:S(2)}) copy-start(bf16[1,512,1024]{2,1,0:T(8,128)(2,1)} %param.10) | copy-start | bytes 3145732
  48.6 29.9 %copy-start.7 = (bf16[1,512,1024]{2,1,0:T(8,128)(2,1)S(1)}, bf16[1,512,1024]{2,1,0:T(8,128)(2,1)}, u32[]{:S(2)}) copy-start(bf16[1,512,1024]{2,1,0:T(8,128)(2,1)} %param.9) | copy-start | bytes 3145732
  48.6 29.9 %copy-start.17 = (f32[1,1024]{1,0:T(1,128)S(1)}, f32[1,1024]{1,0:T(1,128)}, u32[]{:S(2)}) copy-start(f32[1,1024]{1,0:T(1,128)} %gain.3) | copy-start | bytes 12292
  48.7 20.3 %collective-permute-start.5 = (bf16[256,1024]{1,0:T(8,128)(2,1)S(1)}, bf16[256,1024]{1,0:T(8,128)(2,1)S(1)}, u32[]{:S(2)}, u32[]{:S(2)}) collective-permute-start(bf16[256,1024]{1,0:T(8,128)(2,1)S(1)} %pad_maximum_fusion.1), channel_id=1, source_target_pairs={{0,2},{1,3},{2,0},{3,1},{4,6},{5,7},{6,4},{7,5},{8,10},{9,11},{10,... | collective-permute-start | bytes 1572872 | tf_op jit(solution)/shard_map/ppermute | solution.py:25
  60.5 17.9 %collective-permute-start.1 = (bf16[384,1024]{1,0:T(8,128)(2,1)S(1)}, bf16[384,1024]{1,0:T(8,128)(2,1)S(1)}, u32[]{:S(2)}, u32[]{:S(2)}) collective-permute-start(bf16[384,1024]{1,0:T(8,128)(2,1)S(1)} %pad_maximum_fusion), channel_id=1, source_target_pairs={{0,1},{1,0},{2,3},{3,2},{4,5},{5,4},{6,7},{7,6},{8,9},{9,8},{10,11... | collective-permute-start | bytes 2359304 | tf_op jit(solution)/shard_map/ppermute | solution.py:29
  69.0 17.0 %collective-permute-start.6 = (bf16[256,1024]{1,0:T(8,128)(2,1)S(1)}, bf16[256,1024]{1,0:T(8,128)(2,1)S(1)}, u32[]{:S(2)}, u32[]{:S(2)}) collective-permute-start(bf16[256,1024]{1,0:T(8,128)(2,1)S(1)} %collective-permute-done.5.far), channel_id=1, source_target_pairs={{0,1},{1,0},{2,3},{3,2},{4,5},{5,4},{6,7},{7,6},{8,9},{9,8},{10,11... | collective-permute-start | bytes 1572872 | tf_op jit(solution)/shard_map/ppermute | solution.py:29
  83.2 1.0 copy-start.11
  84.2 1.0 copy-start.13
  85.2 0.8 copy-start.15
  92.3 0.8 copy-start.4
  93.1 1.3 copy-start
  94.4 30.6 %all-to-all-start.2 = ((bf16[4,8,32,1024]{3,2,1,0:T(8,128)(2,1)}), bf16[4,8,32,1024]{3,2,1,0:T(8,128)(2,1)S(1)}, u32[]{:S(2)}, u32[]{:S(2)}) async-start(bf16[4,8,32,1024]{3,2,1,0:T(8,128)(2,1)} %shard_map.95), calls=%async_computation.2 | async-start | bytes 4194304 | tf_op jit(solution)/shard_map/all_to_all | solution.py:43
  98.9 1.6 copy-start.1
  100.5 1.0 copy-start.5
  101.5 1.2 copy-start.12
  102.7 1.2 copy-start.14
  104.0 1.0 copy-start.16
  108.9 1.0 copy-start.8
  109.9 47.2 %collective-permute-start.2 = (bf16[2,128,1024]{2,1,0:T(8,128)(2,1)}, bf16[2,128,1024]{2,1,0:T(8,128)(2,1)S(1)}, u32[]{:S(2)}, u32[]{:S(2)}) collective-permute-start(bf16[2,128,1024]{2,1,0:T(8,128)(2,1)} %get-tuple-element.19), channel_id=1, source_target_pairs={{0,1},{1,0},{2,3},{3,2},{4,5},{5,4},{6,7},{7,6},{8,9},{9,8},{10,11... | collective-permute-start | bytes 1572872 | tf_op jit(solution)/shard_map/ppermute | solution.py:29
  127.8 29.3 %copy-start.9 = (f32[2,128,1024]{2,1,0:T(8,128)S(1)}, f32[2,128,1024]{2,1,0:T(8,128)}, u32[]{:S(2)}) copy-start(f32[2,128,1024]{2,1,0:T(8,128)} %copy-done.8) | copy-start | bytes 3145732
  127.8 52.3 %all-to-all-start.3 = ((bf16[8,32,1024]{2,1,0:T(8,128)(2,1)}), bf16[8,32,1024]{2,1,0:T(8,128)(2,1)S(1)}, u32[]{:S(2)}, u32[]{:S(2)}) async-start(bf16[8,32,1024]{2,1,0:T(8,128)(2,1)} %shard_map.96), calls=%async_computation.3 | async-start | bytes 1048576 | tf_op jit(solution)/shard_map/all_to_all | solution.py:43
  157.7 14.9 %collective-permute-start.3 = (bf16[128,1024]{1,0:T(8,128)(2,1)S(1)}, bf16[128,1024]{1,0:T(8,128)(2,1)S(1)}, u32[]{:S(2)}, u32[]{:S(2)}) collective-permute-start(bf16[128,1024]{1,0:T(8,128)(2,1)S(1)} %get-tuple-element.25), channel_id=1, source_target_pairs={{0,128},{128,256},{256,384},{384,512},{512,640},{640,768},{768,896... | collective-permute-start | bytes 786440 | tf_op jit(solution)/shard_map/ppermute | solution.py:34
  167.8 12.4 %collective-permute-start.4 = (bf16[128,1024]{1,0:T(8,128)(2,1)S(1)}, bf16[128,1024]{1,0:T(8,128)(2,1)S(1)}, u32[]{:S(2)}, u32[]{:S(2)}) collective-permute-start(bf16[128,1024]{1,0:T(8,128)(2,1)S(1)} %get-tuple-element.24), channel_id=1, source_target_pairs={{0,896},{128,0},{256,128},{384,256},{512,384},{640,512},{768,640},... | collective-permute-start | bytes 786440 | tf_op jit(solution)/shard_map/ppermute | solution.py:34

commit v3 on v2

--- a/solution.py
+++ b/solution.py
@@ -10,9 +10,9 @@
 gelu_coef = 0.7978845608
 
 
-NX, NY = 4, 8
-x_groups = [[NX * y + x for x in range(NX)] for y in range(NY)]
-y_groups = [[NX * y + x for y in range(NY)] for x in range(NX)]
+NEAR, FAR = 8, 4
+near_groups = [[NEAR * k + j for j in range(NEAR)] for k in range(FAR)]
+far_groups = [[NEAR * k + j for k in range(FAR)] for j in range(NEAR)]
 other_chip = [(0, 2), (1, 3), (2, 0), (3, 1)]
 other_core = [(0, 1), (1, 0), (2, 3), (3, 2)]
 
@@ -75,8 +75,9 @@
     lax.fori_loop(0, rows // CHUNK, step, None)
 
 
-def own_kernel(xf, xb, ct, near, wi, wo, gain, nf, nb, c2, act, dp, br, dn, act_f):
+def own_kernel(xf, xb, ct, near, wi, wo, gain, nf, nb, c2, br, dn, p, act_f, act, dp):
     rows = xf.shape[0]
+    hid = wi.shape[0]
     norm_into(xf, 0, gain, nf, 0, rows)
     norm_into(near, 0, gain, nf, rows, rows)
     norm_into(xb, 0, gain, nb, 0, rows)
@@ -98,6 +99,8 @@
         c = pl.ds(pl.multiple_of(j * TILE, TILE), TILE)
         br[:, c] = nn(act_f[...], wo[:, c])
         dn[:, c] = nn(dp[...], wi[:, c])
+        p[c, :hid] = tn(nb[:, c], dp[...])
+        p[c, hid:] = tn(c2[:, c], act[...])
 
     lax.fori_loop(0, wi.shape[1] // TILE, back, None)
 
@@ -133,43 +136,73 @@
     lax.fori_loop(0, wi.shape[1] // TILE, back, None)
 
 
-def grad_kernel(far, far2, wi, wo, gain, nb, c2, act, dp, g, nb3, c3, act3, dp3):
+def grad_kernel(far, far2, wi, wo, gain, p, g, vfar, vwi, vwo, vp, vg, nb3, c3, act3, dp3, arrived, sent):
     rows = far.shape[0] // 2
     hid = wi.shape[0]
-    norm_into(far, 0, gain, nb3, 0, rows)
-    norm_into(far2, 0, gain, nb3, rows, rows)
-    c3[:rows, :] = far[rows:, :]
-    c3[rows:, :] = far2[rows:, :]
+    loads = [
+        pltpu.make_async_copy(src, dst, arrived.at[i])
+        for i, (src, dst) in enumerate(
+            [(far, vfar.at[0]), (far2, vfar.at[1]), (wi, vwi), (wo, vwo), (p, vp)]
+        )
+    ]
+    for load in loads:
+        load.start()
+    for k in range(2):
+        loads[k].wait()
+        norm_into(vfar.at[k], 0, gain, nb3, k * rows, rows)
+        c3[k * rows : (k + 1) * rows, :] = vfar[k, rows:, :]
+    loads[2].wait()
+    loads[3].wait()
 
     def hidden(j, _):
         h = pl.ds(pl.multiple_of(j * TILE, TILE), TILE)
-        value, slope = gelu_both(nt(nb3[...], wi[h, :]))
+        value, slope = gelu_both(nt(nb3[...], vwi[h, :]))
         act3[:, h] = value.astype(bf16)
-        dp3[:, h] = (nt(c3[...], wo[h, :]) * slope).astype(bf16)
+        dp3[:, h] = (nt(c3[...], vwo[h, :]) * slope).astype(bf16)
 
     lax.fori_loop(0, hid // TILE, hidden, None)
-
-    def grads(y, _):
-        c = pl.ds(pl.multiple_of(y * 128, 128), 128)
-        gi = tn(nb[:, c], dp[...]) + tn(nb3[:, c], dp3[...])
-        g[:, y, :, :hid] = gi.astype(bf16).reshape(NX, 32, hid)
-        go = tn(c2[:, c], act[...]) + tn(c3[:, c], act3[...])
-        g[:, y, :, hid:] = go.astype(bf16).reshape(NX, 32, hid)
-
-    lax.fori_loop(0, NY, grads, None)
+    loads[4].wait()
+    stores = []
+    for k in range(FAR):
+        c = slice(k * TILE, (k + 1) * TILE)
+        gi = vp[c, :hid] + tn(nb3[:, c], dp3[...])
+        vg[:, k, :, :hid] = gi.astype(bf16).reshape(NEAR, -1, hid)
+        go = vp[c, hid:] + tn(c3[:, c], act3[...])
+        vg[:, k, :, hid:] = go.astype(bf16).reshape(NEAR, -1, hid)
+        store = pltpu.make_async_copy(vg.at[:, k], g.at[:, k], sent.at[k])
+        store.start()
+        stores.append(store)
+    for store in stores:
+        store.wait()
 
 
 def sum_kernel(pieces, total):
-    total[...] = jnp.sum(pieces[...].astype(f32), axis=0).astype(bf16)
-
-
-def local(kernel, outs, scratch, flops, moved):
+    def step(k, _):
+        total[k] = jnp.sum(pieces[:, k].astype(f32), axis=0).astype(bf16)
+
+    lax.fori_loop(0, pieces.shape[1], step, None)
+
+
+def last_kernel(pieces, g_in, g_out):
+    hid = g_in.shape[1]
+    total = jnp.sum(pieces[...].astype(f32), axis=0).astype(bf16)
+    g_in[...] = total[:, :hid]
+    g_out[...] = total[:, hid:]
+
+
+def landed_kernel(a, b, c, d):
+    c[0] = a[...]
+    d[0] = b[...]
+
+
+def local(kernel, outs, scratch, flops, moved, mib=56, **specs):
     return pl.pallas_call(
         kernel,
         out_shape=[jax.ShapeDtypeStruct(s, t) for s, t in outs],
-        scratch_shapes=[pltpu.VMEM(s, t) for s, t in scratch],
-        compiler_params=pltpu.CompilerParams(vmem_limit_bytes=28 * 2**20),
+        scratch_shapes=[pltpu.VMEM(*a) if isinstance(a, tuple) else a for a in scratch],
+        compiler_params=pltpu.CompilerParams(vmem_limit_bytes=mib * 2**20),
         cost_estimate=pl.CostEstimate(flops=flops, bytes_accessed=moved, transcendentals=0),
+        **specs,
     )
 
 
@@ -182,22 +215,22 @@
     n_dp = lax.axis_size("dp")
     d = lax.axis_index("dp")
     part = hid // n_dp
-    at = (d % NX * NY + d // NX) * part
+    at = (d % NEAR * FAR + d // NEAR) * part
     mine = jnp.stack(
         [lax.dynamic_slice_in_dim(wi, at, part, 0), lax.dynamic_slice_in_dim(wo, at, part, 0)]
     )
     piece = to_chip(mine)
     far = to_chip(jnp.concatenate([xb, ct]))
     near = to_core(jnp.concatenate([xf, xb, ct]))
-    nf, nb, c2, act, dp, br, dn = local(
+    nf, nb, c2, br, dn, p = local(
         own_kernel,
-        [((both, dim), bf16)] * 3 + [((both, hid), bf16)] * 2 + [((both, dim), f32)] * 2,
-        [((both, hid), bf16)],
-        10 * both * hid * dim,
-        8 * 2**20,
+        [((both, dim), bf16)] * 3 + [((both, dim), f32)] * 2 + [((dim, 2 * hid), f32)],
+        [((both, hid), bf16)] * 3,
+        14 * both * hid * dim,
+        11 * 2**20,
     )(xf, xb, ct, near, wi, wo, gain)
-    col = gathered(piece, y_groups)
-    whole = gathered(col, x_groups).reshape(n_dp, 2, part, dim)
+    col = gathered(piece, far_groups)
+    whole = gathered(col, near_groups).reshape(n_dp, 2, part, dim)
     keep, send = local(
         rest_kernel,
         [((2, rows, dim), f32), ((2, rows, dim), bf16)],
@@ -215,26 +248,37 @@
     dx = ct.astype(f32) + scale * push - shard_x * scale * scale * scale * mixed
     passed_grad = shifted(dx.astype(bf16), "section", -1)
     far2 = to_core(far)
+    cut = dim // n_dp
     (g,) = local(
         grad_kernel,
-        [((NX, NY, dim // n_dp, 2 * hid), bf16)],
-        [((both, dim), bf16)] * 2 + [((both, hid), bf16)] * 2,
-        12 * both * hid * dim,
-        8 * 2**20,
-    )(far, far2, wi, wo, gain, nb, c2, act, dp)
-    g = exchanged(g, x_groups)
-    g = pl.pallas_call(
-        sum_kernel,
-        grid=(NY,),
-        in_specs=[pl.BlockSpec((NX, 1, *g.shape[2:]), lambda i: (0, i, 0, 0))],
-        out_specs=pl.BlockSpec((1, *g.shape[2:]), lambda i: (i, 0, 0)),
-        out_shape=jax.ShapeDtypeStruct(g.shape[1:], bf16),
-        compiler_params=pltpu.CompilerParams(vmem_limit_bytes=16 * 2**20),
-        cost_estimate=pl.CostEstimate(flops=2**21, bytes_accessed=2**21, transcendentals=0),
-    )(g)
-    g = exchanged(g, y_groups)
-    g = jnp.sum(g.astype(f32), axis=0).astype(bf16)
-    return (passed_fwd[None], passed_grad[None], g[:, :hid].T[None], g[:, hid:].T[None])
+        [((NEAR, FAR, cut, 2 * hid), bf16)],
+        [
+            ((2, both, dim), bf16),
+            ((hid, dim), bf16),
+            ((hid, dim), bf16),
+            ((dim, 2 * hid), f32),
+            ((NEAR, FAR, cut, 2 * hid), bf16),
+            ((both, dim), bf16),
+            ((both, dim), bf16),
+            ((both, hid), bf16),
+            ((both, hid), bf16),
+            pltpu.SemaphoreType.DMA((5,)),
+            pltpu.SemaphoreType.DMA((FAR,)),
+        ],
+        8 * both * hid * dim,
+        9 * 2**20,
+        in_specs=[pl.BlockSpec(memory_space=pl.ANY)] * 4
+        + [pl.BlockSpec(memory_space=pltpu.VMEM), pl.BlockSpec(memory_space=pl.ANY)],
+        out_specs=[pl.BlockSpec(memory_space=pl.ANY)],
+    )(far, far2, wi, wo, gain, p)
+    g = exchanged(g, near_groups)
+    (g,) = local(sum_kernel, [(g.shape[1:], bf16)], [], 2**21, 2**21, mib=16)(g)
+    g = exchanged(g, far_groups)
+    passed_fwd, passed_grad = local(
+        landed_kernel, [((1, rows, dim), bf16)] * 2, [], 2**20, 2**20, mib=16
+    )(passed_fwd, passed_grad)
+    g_in, g_out = local(last_kernel, [((cut, hid), bf16)] * 2, [], 2**18, 2**18, mib=16)(g)
+    return passed_fwd, passed_grad, g_in.T[None], g_out.T[None]
 
 
 def solution(mesh):

time: 183 us -> 180 us (0.984)
  local copies, waits for them, and re-layouts: 16.5 us -> 5.5 us
  Pallas kernels: 17.6 us -> 24.7 us
  blocking collectives: 19.6 us -> 14.9 us
  waiting for transfers between devices: 25.1 us -> 27.8 us
  other arithmetic: 0.8 us -> 2.96 us
    unnamed x38 -> x18, local copies, waits for them, and re-layouts: 13.4 us -> 3.05 us
    all_to_all x1, blocking collectives: 19.6 us -> 14.9 us  [gathered(): lax.all_to_all(copies, 'dp', 0, 0, tiled=True, axis_index_groups=groups)]
    pallas_call x3 -> x5, Pallas kernels: 13.7 us -> 17.9 us  [the longest x1 9.85 us: layer(): local(own_kernel, [((both, dim), bf16)] * 3 + [((both, dim), f32)] * 2 +...]
    pallas_call x1, Pallas kernels: 3.9 us -> 6.8 us  [layer(): local(rest_kernel, [((2, rows, dim), f32), ((2, rows, dim), bf16)], [((bo...]
  transfers between devices with their start and end apart: 10 -> 10, of which waited for: 4 -> 5; matrix products, arithmetic and copies ran while one was open for 0% -> 2% of each run, Pallas kernels for 10% -> 13%
where the time goes in v3:
time: 180 us
  starting transfers between devices  103 us (57%)
  waiting for transfers between devices  27.8 us (15%)
  Pallas kernels  24.7 us (14%)
  blocking collectives  14.9 us (8%)
  local copies, waits for them, and re-layouts  5.5 us (3%)
  other arithmetic  2.96 us (2%)
    all_to_all x2, starting transfers between devices, exchanged(): return lax.all_to_all(x, 'dp', 0, 0, tiled=True, axis_index_groups=groups)  34.2 us
    ppermute x2, starting transfers between devices, to_chip(): return lax.ppermute(x, 'mp', other_chip)  32 us
    ppermute x3, starting transfers between devices, to_core(): return lax.ppermute(x, 'mp', other_core)  20 us
    all_to_all x1, blocking collectives, gathered(): lax.all_to_all(copies, 'dp', 0, 0, tiled=True, axis_index_groups=groups)  14.9 us
    all_to_all x2, waiting for transfers between devices, exchanged(): return lax.all_to_all(x, 'dp', 0, 0, tiled=True, axis_index_groups=groups)  13.7 us
    ppermute x2, starting transfers between devices, shifted(): lax.ppermute(x, axis, [(i, (i + by) % length) for i in range(length)])  11.9 us
    ppermute x2, waiting for transfers between devices, shifted(): lax.ppermute(x, axis, [(i, (i + by) % length) for i in range(length)])  10.4 us
    pallas_call x1, Pallas kernels, layer(): local(own_kernel, [((both, dim), bf16)] * 3 + [((both, dim), f32)] * 2 +...  9.85 us
  transfers between devices with their start and end apart: 10, of which 5 were waited for; matrix products, arithmetic and copies ran while one was open for 2% of the time, Pallas kernels for 13%

profile of v3, /device:TPU:1, one launch (start us, length us, event | category | flops | bytes accessed | tf_op | source)
XLA Modules:
  0.0 179.6 jit_solution(12257770098032989207)
XLA Ops:
  0.7 0.8 constant_dynamic-slice_fusion
  1.5 19.9 %collective-permute-start = (bf16[2,16,1024]{2,1,0:T(8,128)(2,1)S(1)}, bf16[2,16,1024]{2,1,0:T(8,128)(2,1)S(1)}, u32[]{:S(2)}, u32[]{:S(2)}) collective-permute-start(bf16[2,16,1024]{2,1,0:T(8,128)(2,1)S(1)} %pad_maximum_fusion.2), channel_id=1, source_target_pairs={{0,2},{1,3},{2,0},{3,1},{4,6},{5,7},{6,4},{7,5},{8,10},{9,11},{10,... | collective-permute-start | bytes 196616 | tf_op jit(solution)/shard_map/ppermute | solution.py:25
  21.4 1.8 %collective-permute-done = bf16[2,16,1024]{2,1,0:T(8,128)(2,1)S(1)} collective-permute-done((bf16[2,16,1024]{2,1,0:T(8,128)(2,1)S(1)}, bf16[2,16,1024]{2,1,0:T(8,128)(2,1)S(1)}, u32[]{:S(2)}, u32[]{:S(2)}) %collective-permute-start) | collective-permute-done | bytes 65568 | tf_op jit(solution)/shard_map/ppermute | solution.py:25
  23.2 14.9 %all_to_all.20 = bf16[4,2,16,1024]{3,2,1,0:T(8,128)(2,1)S(1)} all-to-all(bf16[4,2,16,1024]{3,2,1,0:T(8,128)(2,1)S(1)} %broadcast_in_dim.14), channel_id=1, replica_groups={{0,32,64,96},{4,36,68,100},{8,40,72,104},{12,44,76,108},{16,48,80,112},..., dimensions={0} | all-to-all | bytes 524288 | tf_op jit(solution)/shard_map/all_to_all | solution.py:39
  38.1 1.6 broadcast_in_dim.15
  39.7 4.9 %all-to-all-start.1 = ((bf16[8,4,2,16,1024]{4,3,2,1,0:T(8,128)(2,1)}), bf16[8,4,2,16,1024]{4,3,2,1,0:T(8,128)(2,1)S(1)}, u32[]{:S(2)}, u32[]{:S(2)}) async-start(bf16[8,4,2,16,1024]{4,3,2,1,0:T(8,128)(2,1)} %broadcast_in_dim.15), calls=%async_computation.1 | async-start | bytes 4194304 | tf_op jit(solution)/shard_map/all_to_all | solution.py:39
  44.7 12.1 %collective-permute-start.5 = (bf16[256,1024]{1,0:T(8,128)(2,1)S(1)}, bf16[256,1024]{1,0:T(8,128)(2,1)S(1)}, u32[]{:S(2)}, u32[]{:S(2)}) collective-permute-start(bf16[256,1024]{1,0:T(8,128)(2,1)S(1)} %pad_maximum_fusion.1), channel_id=1, source_target_pairs={{0,2},{1,3},{2,0},{3,1},{4,6},{5,7},{6,4},{7,5},{8,10},{9,11},{10,... | collective-permute-start | bytes 1572872 | tf_op jit(solution)/shard_map/ppermute | solution.py:25
  56.8 0.1 pad_maximum_fusion
  56.9 8.8 %collective-permute-start.1 = (bf16[384,1024]{1,0:T(8,128)(2,1)S(1)}, bf16[384,1024]{1,0:T(8,128)(2,1)S(1)}, u32[]{:S(2)}, u32[]{:S(2)}) collective-permute-start(bf16[384,1024]{1,0:T(8,128)(2,1)S(1)} %pad_maximum_fusion), channel_id=1, source_target_pairs={{0,1},{1,0},{2,3},{3,2},{4,5},{5,4},{6,7},{7,6},{8,9},{9,8},{10,11... | collective-permute-start | bytes 2359304 | tf_op jit(solution)/shard_map/ppermute | solution.py:29
  65.7 8.9 %collective-permute-start.6 = (bf16[256,1024]{1,0:T(8,128)(2,1)S(1)}, bf16[256,1024]{1,0:T(8,128)(2,1)S(1)}, u32[]{:S(2)}, u32[]{:S(2)}) collective-permute-start(bf16[256,1024]{1,0:T(8,128)(2,1)S(1)} %collective-permute-done.5.far), channel_id=1, source_target_pairs={{0,1},{1,0},{2,3},{3,2},{4,5},{5,4},{6,7},{7,6},{8,9},{9,8},{10,11... | collective-permute-start | bytes 1572872 | tf_op jit(solution)/shard_map/ppermute | solution.py:29
  74.6 0.9 copy-done.8
  75.5 9.9 %shard_map.93 = (bf16[256,1024]{1,0:T(8,128)(2,1)}, bf16[256,1024]{1,0:T(8,128)(2,1)}, bf16[256,1024]{1,0:T(8,128)(2,1)}, f32[256,1024]{1,0:T(8,128)}, f32[256,1024]{1,0:T(8,128)}, /*index=5*/f32[1024,1024]{1,0:T(8,128)}) custom-call(bf16[128,1024]{1,0:T(8,128)(2,1)} %bitcast.43, bf16[128,1024]{1,0:T(8,128)(2,1)} %bitcast.33, bf16[128,1024]{1,0:T(8,128)(2,1)} %bitcast.36, ...), custom_call_target="tpu_custom_call" | custom-call | flops 1879048192 | bytes 11534336 | tf_op jit(solution)/shard_map/pallas_call | solution.py:225
  85.3 0.0 collective-permute-done.6.far2
  85.3 0.8 copy-done.6
  86.2 5.6 %shard_map.96 = bf16[8,4,32,1024]{3,2,1,0:T(8,128)(2,1)} custom-call(bf16[256,1024]{1,0:T(8,128)(2,1)} %copy-done.5, bf16[256,1024]{1,0:T(8,128)(2,1)} %copy-done.6, bf16[512,1024]{1,0:T(8,128)(2,1)} %bitcast.42, bf16[512,1024]{1,0:T(8,128)(2,1)} %bitcast.40, f32[1,1024]{1,0:T(1,128)} %gain.3, f32[1024,1024]{1,0:T(8,128)} %get-tuple-element.25.p), custom_call_target="tpu_custom_call" | custom-call | flops 1073741824 | bytes 9437184 | tf_op jit(solution)/shard_map/pallas_call | solution.py:252
  91.8 1.3 copy-done
  93.1 5.4 %all-to-all-start.2 = ((bf16[8,4,32,1024]{3,2,1,0:T(8,128)(2,1)}), bf16[8,4,32,1024]{3,2,1,0:T(8,128)(2,1)S(1)}, u32[]{:S(2)}, u32[]{:S(2)}) async-start(bf16[8,4,32,1024]{3,2,1,0:T(8,128)(2,1)} %shard_map.96), calls=%async_computation.2 | async-start | bytes 4194304 | tf_op jit(solution)/shard_map/all_to_all | solution.py:43
  98.5 6.8 %shard_map.94 = (f32[2,128,1024]{2,1,0:T(8,128)}, bf16[2,128,1024]{2,1,0:T(8,128)(2,1)}) custom-call(bf16[32,2,16,1024]{3,2,1,0:T(8,128)(2,1)} %bitcast.32, bf16[256,1024]{1,0:T(8,128)(2,1)} %get-tuple-element.16.nf, bf16[256,1024]{1,0:T(8,128)(2,1)} %get-tuple-element.17.nb, bf16[256,1024]{1,0:T(8,128)(2,1)} %get-tuple-element.18.c2, ...), custom_call_target="tpu_custom_call" | custom-call | flops 1342177280 | bytes 8388608 | tf_op jit(solution)/shard_map/pallas_call | solution.py:234
  105.3 2.3 %collective-permute-start.2 = (bf16[2,128,1024]{2,1,0:T(8,128)(2,1)}, bf16[2,128,1024]{2,1,0:T(8,128)(2,1)S(1)}, u32[]{:S(2)}, u32[]{:S(2)}) collective-permute-start(bf16[2,128,1024]{2,1,0:T(8,128)(2,1)} %get-tuple-element.22), channel_id=1, source_target_pairs={{0,1},{1,0},{2,3},{3,2},{4,5},{5,4},{6,7},{7,6},{8,9},{9,8},{10,11... | collective-permute-start | bytes 1572872 | tf_op jit(solution)/shard_map/ppermute | solution.py:29
  107.7 1.8 %collective-permute-done.2 = bf16[2,128,1024]{2,1,0:T(8,128)(2,1)S(1)} collective-permute-done((bf16[2,128,1024]{2,1,0:T(8,128)(2,1)}, bf16[2,128,1024]{2,1,0:T(8,128)(2,1)S(1)}, u32[]{:S(2)}, u32[]{:S(2)}) %collective-permute-start.2) | collective-permute-done | bytes 524320 | tf_op jit(solution)/shard_map/ppermute | solution.py:29
  109.5 1.4 convert_add_fusion
  110.9 0.2 fusion
  111.1 13.7 %all-to-all-done.2.pieces = bf16[8,4,32,1024]{3,2,1,0:T(8,128)(2,1)S(1)} async-done(((bf16[8,4,32,1024]{3,2,1,0:T(8,128)(2,1)}), bf16[8,4,32,1024]{3,2,1,0:T(8,128)(2,1)S(1)}, u32[]{:S(2)}, u32[]{:S(2)}) %all-to-all-start.2) | async-done | bytes 2097184 | tf_op jit(solution)/shard_map/all_to_all | solution.py:43
  124.7 1.0 shard_map.97
  125.7 28.8 %all-to-all-start.3 = ((bf16[4,32,1024]{2,1,0:T(8,128)(2,1)}), bf16[4,32,1024]{2,1,0:T(8,128)(2,1)S(1)}, u32[]{:S(2)}, u32[]{:S(2)}) async-start(bf16[4,32,1024]{2,1,0:T(8,128)(2,1)} %shard_map.97), calls=%async_computation.3 | async-start | bytes 524288 | tf_op jit(solution)/shard_map/all_to_all | solution.py:43
  154.5 1.3 fusion.5
  155.8 8.3 %collective-permute-start.3 = (bf16[128,1024]{1,0:T(8,128)(2,1)S(1)}, bf16[128,1024]{1,0:T(8,128)(2,1)S(1)}, u32[]{:S(2)}, u32[]{:S(2)}) collective-permute-start(bf16[128,1024]{1,0:T(8,128)(2,1)S(1)} %get-tuple-element.31), channel_id=1, source_target_pairs={{0,128},{128,256},{256,384},{384,512},{512,640},{640,768},{768,896... | collective-permute-start | bytes 786440 | tf_op jit(solution)/shard_map/ppermute | solution.py:34
  164.1 3.6 %collective-permute-start.4 = (bf16[128,1024]{1,0:T(8,128)(2,1)S(1)}, bf16[128,1024]{1,0:T(8,128)(2,1)S(1)}, u32[]{:S(2)}, u32[]{:S(2)}) collective-permute-start(bf16[128,1024]{1,0:T(8,128)(2,1)S(1)} %get-tuple-element.30), channel_id=1, source_target_pairs={{0,896},{128,0},{256,128},{384,256},{512,384},{640,512},{768,640},... | collective-permute-start | bytes 786440 | tf_op jit(solution)/shard_map/ppermute | solution.py:34
  167.7 3.4 %collective-permute-done.3.a = bf16[128,1024]{1,0:T(8,128)(2,1)S(1)} collective-permute-done((bf16[128,1024]{1,0:T(8,128)(2,1)S(1)}, bf16[128,1024]{1,0:T(8,128)(2,1)S(1)}, u32[]{:S(2)}, u32[]{:S(2)}) %collective-permute-start.3) | collective-permute-done | bytes 262176 | tf_op jit(solution)/shard_map/ppermute | solution.py:34
  171.1 7.0 %collective-permute-done.4.b = bf16[128,1024]{1,0:T(8,128)(2,1)S(1)} collective-permute-done((bf16[128,1024]{1,0:T(8,128)(2,1)S(1)}, bf16[128,1024]{1,0:T(8,128)(2,1)S(1)}, u32[]{:S(2)}, u32[]{:S(2)}) %collective-permute-start.4) | collective-permute-done | bytes 262176 | tf_op jit(solution)/shard_map/ppermute | solution.py:34
  178.1 0.8 shard_map.95
  179.0 0.7 shard_map.98
  (24 shorter events, 0.1 us)
Async XLA Ops:
  1.5 21.7 %collective-permute-start = (bf16[2,16,1024]{2,1,0:T(8,128)(2,1)S(1)}, bf16[2,16,1024]{2,1,0:T(8,128)(2,1)S(1)}, u32[]{:S(2)}, u32[]{:S(2)}) collective-permute-start(bf16[2,16,1024]{2,1,0:T(8,128)(2,1)S(1)} %pad_maximum_fusion.2), channel_id=1, source_target_pairs={{0,2},{1,3},{2,0},{3,1},{4,6},{5,7},{6,4},{7,5},{8,10},{9,11},{10,... | collective-permute-start | bytes 196616 | tf_op jit(solution)/shard_map/ppermute | solution.py:25
  39.7 4.9 %copy-start.1 = (bf16[1,128,1024]{2,1,0:T(8,128)(2,1)S(1)}, bf16[1,128,1024]{2,1,0:T(8,128)(2,1)}, u32[]{:S(2)}) copy-start(bf16[1,128,1024]{2,1,0:T(8,128)(2,1)} %param.7) | copy-start | bytes 786436
  39.7 4.9 %copy-start.3 = (bf16[1,128,1024]{2,1,0:T(8,128)(2,1)S(1)}, bf16[1,128,1024]{2,1,0:T(8,128)(2,1)}, u32[]{:S(2)}) copy-start(bf16[1,128,1024]{2,1,0:T(8,128)(2,1)} %param.8) | copy-start | bytes 786436
  39.7 17.1 %copy-start.4 = (bf16[1,128,1024]{2,1,0:T(8,128)(2,1)S(1)}, bf16[1,128,1024]{2,1,0:T(8,128)(2,1)}, u32[]{:S(2)}) copy-start(bf16[1,128,1024]{2,1,0:T(8,128)(2,1)} %param.6) | copy-start | bytes 786436
  39.7 52.0 %all-to-all-start.1 = ((bf16[8,4,2,16,1024]{4,3,2,1,0:T(8,128)(2,1)}), bf16[8,4,2,16,1024]{4,3,2,1,0:T(8,128)(2,1)S(1)}, u32[]{:S(2)}, u32[]{:S(2)}) async-start(bf16[8,4,2,16,1024]{4,3,2,1,0:T(8,128)(2,1)} %broadcast_in_dim.15), calls=%async_computation.1 | async-start | bytes 4194304 | tf_op jit(solution)/shard_map/all_to_all | solution.py:39
  44.7 21.0 %collective-permute-start.5 = (bf16[256,1024]{1,0:T(8,128)(2,1)S(1)}, bf16[256,1024]{1,0:T(8,128)(2,1)S(1)}, u32[]{:S(2)}, u32[]{:S(2)}) collective-permute-start(bf16[256,1024]{1,0:T(8,128)(2,1)S(1)} %pad_maximum_fusion.1), channel_id=1, source_target_pairs={{0,2},{1,3},{2,0},{3,1},{4,6},{5,7},{6,4},{7,5},{8,10},{9,11},{10,... | collective-permute-start | bytes 1572872 | tf_op jit(solution)/shard_map/ppermute | solution.py:25
  56.9 17.7 %collective-permute-start.1 = (bf16[384,1024]{1,0:T(8,128)(2,1)S(1)}, bf16[384,1024]{1,0:T(8,128)(2,1)S(1)}, u32[]{:S(2)}, u32[]{:S(2)}) collective-permute-start(bf16[384,1024]{1,0:T(8,128)(2,1)S(1)} %pad_maximum_fusion), channel_id=1, source_target_pairs={{0,1},{1,0},{2,3},{3,2},{4,5},{5,4},{6,7},{7,6},{8,9},{9,8},{10,11... | collective-permute-start | bytes 2359304 | tf_op jit(solution)/shard_map/ppermute | solution.py:29
  65.7 19.6 %copy-start.5 = (bf16[256,1024]{1,0:T(8,128)(2,1)}, bf16[256,1024]{1,0:T(8,128)(2,1)S(1)}, u32[]{:S(2)}) copy-start(bf16[256,1024]{1,0:T(8,128)(2,1)S(1)} %collective-permute-done.5.far) | copy-start | bytes 1572868
  65.7 19.6 %collective-permute-start.6 = (bf16[256,1024]{1,0:T(8,128)(2,1)S(1)}, bf16[256,1024]{1,0:T(8,128)(2,1)S(1)}, u32[]{:S(2)}, u32[]{:S(2)}) collective-permute-start(bf16[256,1024]{1,0:T(8,128)(2,1)S(1)} %collective-permute-done.5.far), channel_id=1, source_target_pairs={{0,1},{1,0},{2,3},{3,2},{4,5},{5,4},{6,7},{7,6},{8,9},{9,8},{10,11... | collective-permute-start | bytes 1572872 | tf_op jit(solution)/shard_map/ppermute | solution.py:29
  74.6 0.9 copy-start.8
  85.3 0.9 copy-start.6
  91.8 1.3 copy-start
  93.1 31.6 %all-to-all-start.2 = ((bf16[8,4,32,1024]{3,2,1,0:T(8,128)(2,1)}), bf16[8,4,32,1024]{3,2,1,0:T(8,128)(2,1)S(1)}, u32[]{:S(2)}, u32[]{:S(2)}) async-start(bf16[8,4,32,1024]{3,2,1,0:T(8,128)(2,1)} %shard_map.96), calls=%async_computation.2 | async-start | bytes 4194304 | tf_op jit(solution)/shard_map/all_to_all | solution.py:43
  105.3 5.5 %copy-start.2 = (bf16[1,128,1024]{2,1,0:T(8,128)(2,1)S(1)}, bf16[1,128,1024]{2,1,0:T(8,128)(2,1)}, u32[]{:S(2)}) copy-start(bf16[1,128,1024]{2,1,0:T(8,128)(2,1)} %param.7) | copy-start | bytes 786436
  105.3 5.5 %copy-start.7 = (f32[1,1024]{1,0:T(1,128)S(1)}, f32[1,1024]{1,0:T(1,128)}, u32[]{:S(2)}) copy-start(f32[1,1024]{1,0:T(1,128)} %gain.3) | copy-start | bytes 12292
  105.3 4.1 %collective-permute-start.2 = (bf16[2,128,1024]{2,1,0:T(8,128)(2,1)}, bf16[2,128,1024]{2,1,0:T(8,128)(2,1)S(1)}, u32[]{:S(2)}, u32[]{:S(2)}) collective-permute-start(bf16[2,128,1024]{2,1,0:T(8,128)(2,1)} %get-tuple-element.22), channel_id=1, source_target_pairs={{0,1},{1,0},{2,3},{3,2},{4,5},{5,4},{6,7},{7,6},{8,9},{9,8},{10,11... | collective-permute-start | bytes 1572872 | tf_op jit(solution)/shard_map/ppermute | solution.py:29
  125.7 53.2 %all-to-all-start.3 = ((bf16[4,32,1024]{2,1,0:T(8,128)(2,1)}), bf16[4,32,1024]{2,1,0:T(8,128)(2,1)S(1)}, u32[]{:S(2)}, u32[]{:S(2)}) async-start(bf16[4,32,1024]{2,1,0:T(8,128)(2,1)} %shard_map.97), calls=%async_computation.3 | async-start | bytes 524288 | tf_op jit(solution)/shard_map/all_to_all | solution.py:43
  155.8 15.3 %collective-permute-start.3 = (bf16[128,1024]{1,0:T(8,128)(2,1)S(1)}, bf16[128,1024]{1,0:T(8,128)(2,1)S(1)}, u32[]{:S(2)}, u32[]{:S(2)}) collective-permute-start(bf16[128,1024]{1,0:T(8,128)(2,1)S(1)} %get-tuple-element.31), channel_id=1, source_target_pairs={{0,128},{128,256},{256,384},{384,512},{512,640},{640,768},{768,896... | collective-permute-start | bytes 786440 | tf_op jit(solution)/shard_map/ppermute | solution.py:34
  164.1 14.0 %collective-permute-start.4 = (bf16[128,1024]{1,0:T(8,128)(2,1)S(1)}, bf16[128,1024]{1,0:T(8,128)(2,1)S(1)}, u32[]{:S(2)}, u32[]{:S(2)}) collective-permute-start(bf16[128,1024]{1,0:T(8,128)(2,1)S(1)} %get-tuple-element.30), channel_id=1, source_target_pairs={{0,896},{128,0},{256,128},{384,256},{512,384},{640,512},{768,640},... | collective-permute-start | bytes 786440 | tf_op jit(solution)/shard_map/ppermute | solution.py:34

commit v4 on v3

--- a/solution.py
+++ b/solution.py
@@ -17,6 +17,8 @@
 other_core = [(0, 1), (1, 0), (2, 3), (3, 2)]
 
 f32, bf16 = jnp.float32, jnp.bfloat16
+vmem = pl.BlockSpec(memory_space=pltpu.VMEM)
+hbm = pl.BlockSpec(memory_space=pltpu.HBM)
 CHUNK = 32
 TILE = 256
 
@@ -136,23 +138,20 @@
     lax.fori_loop(0, wi.shape[1] // TILE, back, None)
 
 
-def grad_kernel(far, far2, wi, wo, gain, p, g, vfar, vwi, vwo, vp, vg, nb3, c3, act3, dp3, arrived, sent):
+def grad_kernel(far, far2, wi, wo, gain, p, g, vwi, vwo, vp, vg, nb3, c3, act3, dp3, arrived, sent):
     rows = far.shape[0] // 2
     hid = wi.shape[0]
     loads = [
         pltpu.make_async_copy(src, dst, arrived.at[i])
-        for i, (src, dst) in enumerate(
-            [(far, vfar.at[0]), (far2, vfar.at[1]), (wi, vwi), (wo, vwo), (p, vp)]
-        )
+        for i, (src, dst) in enumerate([(wi, vwi), (wo, vwo), (p, vp)])
     ]
     for load in loads:
         load.start()
-    for k in range(2):
-        loads[k].wait()
-        norm_into(vfar.at[k], 0, gain, nb3, k * rows, rows)
-        c3[k * rows : (k + 1) * rows, :] = vfar[k, rows:, :]
-    loads[2].wait()
-    loads[3].wait()
+    for k, half in enumerate((far, far2)):
+        norm_into(half, 0, gain, nb3, k * rows, rows)
+        c3[k * rows : (k + 1) * rows, :] = half[rows:, :]
+    loads[0].wait()
+    loads[1].wait()
 
     def hidden(j, _):
         h = pl.ds(pl.multiple_of(j * TILE, TILE), TILE)
@@ -161,7 +160,7 @@
         dp3[:, h] = (nt(c3[...], vwo[h, :]) * slope).astype(bf16)
 
     lax.fori_loop(0, hid // TILE, hidden, None)
-    loads[4].wait()
+    loads[2].wait()
     stores = []
     for k in range(FAR):
         c = slice(k * TILE, (k + 1) * TILE)
@@ -195,7 +194,7 @@
     d[0] = b[...]
 
 
-def local(kernel, outs, scratch, flops, moved, mib=56, **specs):
+def local(kernel, outs, scratch, flops, moved, mib=62, **specs):
     return pl.pallas_call(
         kernel,
         out_shape=[jax.ShapeDtypeStruct(s, t) for s, t in outs],
@@ -237,6 +236,7 @@
         [((both, hid), bf16)] * 2 + [((hid, dim), bf16)] * 2,
         10 * both * hid * dim,
         8 * 2**20,
+        mib=56,
     )(whole, nf, nb, c2, br, dn)
     sums = keep + to_core(send).astype(f32)
     out = (xf.astype(f32) + sums[0]).astype(bf16)
@@ -253,7 +253,6 @@
         grad_kernel,
         [((NEAR, FAR, cut, 2 * hid), bf16)],
         [
-            ((2, both, dim), bf16),
             ((hid, dim), bf16),
             ((hid, dim), bf16),
             ((dim, 2 * hid), f32),
@@ -262,14 +261,14 @@
             ((both, dim), bf16),
             ((both, hid), bf16),
             ((both, hid), bf16),
-            pltpu.SemaphoreType.DMA((5,)),
+            pltpu.SemaphoreType.DMA((3,)),
             pltpu.SemaphoreType.DMA((FAR,)),
         ],
         8 * both * hid * dim,
         9 * 2**20,
-        in_specs=[pl.BlockSpec(memory_space=pl.ANY)] * 4
-        + [pl.BlockSpec(memory_space=pltpu.VMEM), pl.BlockSpec(memory_space=pl.ANY)],
-        out_specs=[pl.BlockSpec(memory_space=pl.ANY)],
+        mib=60,
+        in_specs=[vmem, vmem, hbm, hbm, vmem, hbm],
+        out_specs=[hbm],
     )(far, far2, wi, wo, gain, p)
     g = exchanged(g, near_groups)
     (g,) = local(sum_kernel, [(g.shape[1:], bf16)], [], 2**21, 2**21, mib=16)(g)

time: 180 us -> 181 us (level)
  starting transfers between devices: 103 us -> 105 us
    all_to_all x2, starting transfers between devices: 34.2 us -> 36.1 us  [exchanged(): return lax.all_to_all(x, 'dp', 0, 0, tiled=True, axis_index_groups=groups)]
where the time goes in v4:
time: 181 us; the launch traced here: 180 us
  starting transfers between devices  105 us (58%)
  waiting for transfers between devices  27.4 us (15%)
  Pallas kernels  25 us (14%)
  blocking collectives  14.9 us (8%)
  local copies, waits for them, and re-layouts  4.2 us (2%)
  other arithmetic  2.96 us (2%)
    all_to_all x2, starting transfers between devices, exchanged(): return lax.all_to_all(x, 'dp', 0, 0, tiled=True, axis_index_groups=groups)  36.1 us
    ppermute x2, starting transfers between devices, to_chip(): return lax.ppermute(x, 'mp', other_chip)  32 us
    ppermute x3, starting transfers between devices, to_core(): return lax.ppermute(x, 'mp', other_core)  20 us
    all_to_all x1, blocking collectives, gathered(): lax.all_to_all(copies, 'dp', 0, 0, tiled=True, axis_index_groups=groups)  14.9 us
    all_to_all x2, waiting for transfers between devices, exchanged(): return lax.all_to_all(x, 'dp', 0, 0, tiled=True, axis_index_groups=groups)  13.6 us
    ppermute x2, starting transfers between devices, shifted(): lax.ppermute(x, axis, [(i, (i + by) % length) for i in range(length)])  11.9 us
    ppermute x2, waiting for transfers between devices, shifted(): lax.ppermute(x, axis, [(i, (i + by) % length) for i in range(length)])  10.1 us
    pallas_call x1, Pallas kernels, layer(): local(own_kernel, [((both, dim), bf16)] * 3 + [((both, dim), f32)] * 2 +...  9.92 us
  transfers between devices with their start and end apart: 10, of which 5 were waited for; matrix products, arithmetic and copies ran while one was open for 2% of the time, Pallas kernels for 13%

profile of v4, /device:TPU:1, one launch (start us, length us, event | category | flops | bytes accessed | tf_op | source)
XLA Modules:
  0.0 180.2 jit_solution(2739657860064289735)
XLA Ops:
  0.7 0.8 constant_dynamic-slice_fusion
  1.5 19.9 %collective-permute-start = (bf16[2,16,1024]{2,1,0:T(8,128)(2,1)S(1)}, bf16[2,16,1024]{2,1,0:T(8,128)(2,1)S(1)}, u32[]{:S(2)}, u32[]{:S(2)}) collective-permute-start(bf16[2,16,1024]{2,1,0:T(8,128)(2,1)S(1)} %pad_maximum_fusion.2), channel_id=1, source_target_pairs={{0,2},{1,3},{2,0},{3,1},{4,6},{5,7},{6,4},{7,5},{8,10},{9,11},{10,... | collective-permute-start | bytes 196616 | tf_op jit(solution)/shard_map/ppermute | solution.py:27
  21.4 1.8 %collective-permute-done = bf16[2,16,1024]{2,1,0:T(8,128)(2,1)S(1)} collective-permute-done((bf16[2,16,1024]{2,1,0:T(8,128)(2,1)S(1)}, bf16[2,16,1024]{2,1,0:T(8,128)(2,1)S(1)}, u32[]{:S(2)}, u32[]{:S(2)}) %collective-permute-start) | collective-permute-done | bytes 65568 | tf_op jit(solution)/shard_map/ppermute | solution.py:27
  23.2 14.9 %all_to_all.20 = bf16[4,2,16,1024]{3,2,1,0:T(8,128)(2,1)S(1)} all-to-all(bf16[4,2,16,1024]{3,2,1,0:T(8,128)(2,1)S(1)} %broadcast_in_dim.14), channel_id=1, replica_groups={{0,32,64,96},{4,36,68,100},{8,40,72,104},{12,44,76,108},{16,48,80,112},..., dimensions={0} | all-to-all | bytes 524288 | tf_op jit(solution)/shard_map/all_to_all | solution.py:41
  38.1 1.6 broadcast_in_dim.15
  39.7 4.9 %all-to-all-start.1 = ((bf16[8,4,2,16,1024]{4,3,2,1,0:T(8,128)(2,1)}), bf16[8,4,2,16,1024]{4,3,2,1,0:T(8,128)(2,1)}, u32[]{:S(2)}, u32[]{:S(2)}) async-start(bf16[8,4,2,16,1024]{4,3,2,1,0:T(8,128)(2,1)} %broadcast_in_dim.15), calls=%async_computation.1 | async-start | bytes 4194304 | tf_op jit(solution)/shard_map/all_to_all | solution.py:41
  44.7 12.1 %collective-permute-start.5 = (bf16[256,1024]{1,0:T(8,128)(2,1)S(1)}, bf16[256,1024]{1,0:T(8,128)(2,1)S(1)}, u32[]{:S(2)}, u32[]{:S(2)}) collective-permute-start(bf16[256,1024]{1,0:T(8,128)(2,1)S(1)} %pad_maximum_fusion.1), channel_id=1, source_target_pairs={{0,2},{1,3},{2,0},{3,1},{4,6},{5,7},{6,4},{7,5},{8,10},{9,11},{10,... | collective-permute-start | bytes 1572872 | tf_op jit(solution)/shard_map/ppermute | solution.py:27
  56.8 0.1 pad_maximum_fusion
  56.9 8.8 %collective-permute-start.1 = (bf16[384,1024]{1,0:T(8,128)(2,1)S(1)}, bf16[384,1024]{1,0:T(8,128)(2,1)S(1)}, u32[]{:S(2)}, u32[]{:S(2)}) collective-permute-start(bf16[384,1024]{1,0:T(8,128)(2,1)S(1)} %pad_maximum_fusion), channel_id=1, source_target_pairs={{0,1},{1,0},{2,3},{3,2},{4,5},{5,4},{6,7},{7,6},{8,9},{9,8},{10,11... | collective-permute-start | bytes 2359304 | tf_op jit(solution)/shard_map/ppermute | solution.py:31
  65.7 8.9 %collective-permute-start.6 = (bf16[256,1024]{1,0:T(8,128)(2,1)S(1)}, bf16[256,1024]{1,0:T(8,128)(2,1)S(1)}, u32[]{:S(2)}, u32[]{:S(2)}) collective-permute-start(bf16[256,1024]{1,0:T(8,128)(2,1)S(1)} %collective-permute-done.5.far), channel_id=1, source_target_pairs={{0,1},{1,0},{2,3},{3,2},{4,5},{5,4},{6,7},{7,6},{8,9},{9,8},{10,11... | collective-permute-start | bytes 1572872 | tf_op jit(solution)/shard_map/ppermute | solution.py:31
  74.6 0.0 collective-permute-done.1.near
  74.6 1.0 copy-done.7
  75.5 9.9 %shard_map.93 = (bf16[256,1024]{1,0:T(8,128)(2,1)}, bf16[256,1024]{1,0:T(8,128)(2,1)}, bf16[256,1024]{1,0:T(8,128)(2,1)}, f32[256,1024]{1,0:T(8,128)}, f32[256,1024]{1,0:T(8,128)}, /*index=5*/f32[1024,1024]{1,0:T(8,128)}) custom-call(bf16[128,1024]{1,0:T(8,128)(2,1)} %bitcast.42, bf16[128,1024]{1,0:T(8,128)(2,1)} %bitcast.32, bf16[128,1024]{1,0:T(8,128)(2,1)} %bitcast.35, ...), custom_call_target="tpu_custom_call" | custom-call | flops 1879048192 | bytes 11534336 | tf_op jit(solution)/shard_map/pallas_call | solution.py:224
  85.5 0.8 copy-done.5
  86.3 5.8 %shard_map.96 = bf16[8,4,32,1024]{3,2,1,0:T(8,128)(2,1)} custom-call(bf16[256,1024]{1,0:T(8,128)(2,1)} %copy-done.4, bf16[256,1024]{1,0:T(8,128)(2,1)} %copy-done.5, bf16[512,1024]{1,0:T(8,128)(2,1)} %bitcast.41, bf16[512,1024]{1,0:T(8,128)(2,1)} %bitcast.39, f32[1,1024]{1,0:T(1,128)} %gain.3, f32[1024,1024]{1,0:T(8,128)} %get-tuple-element.25.p), custom_call_target="tpu_custom_call" | custom-call | flops 1073741824 | bytes 9437184 | tf_op jit(solution)/shard_map/pallas_call | solution.py:252
  92.1 0.0 all-to-all-done.1
  92.1 5.4 %all-to-all-start.2 = ((bf16[8,4,32,1024]{3,2,1,0:T(8,128)(2,1)}), bf16[8,4,32,1024]{3,2,1,0:T(8,128)(2,1)S(1)}, u32[]{:S(2)}, u32[]{:S(2)}) async-start(bf16[8,4,32,1024]{3,2,1,0:T(8,128)(2,1)} %shard_map.96), calls=%async_computation.2 | async-start | bytes 4194304 | tf_op jit(solution)/shard_map/all_to_all | solution.py:45
  97.5 6.8 %shard_map.94 = (f32[2,128,1024]{2,1,0:T(8,128)}, bf16[2,128,1024]{2,1,0:T(8,128)(2,1)}) custom-call(bf16[32,2,16,1024]{3,2,1,0:T(8,128)(2,1)} %bitcast.1.whole, bf16[256,1024]{1,0:T(8,128)(2,1)} %get-tuple-element.16.nf, bf16[256,1024]{1,0:T(8,128)(2,1)} %get-tuple-element.17.nb, bf16[256,1024]{1,0:T(8,128)(2,1)} %get-tuple-element.18.c2, ...), custom_call_target="tpu_custom_call" | custom-call | flops 1342177280 | bytes 8388608 | tf_op jit(solution)/shard_map/pallas_call | solution.py:233
  104.4 2.3 %collective-permute-start.2 = (bf16[2,128,1024]{2,1,0:T(8,128)(2,1)}, bf16[2,128,1024]{2,1,0:T(8,128)(2,1)S(1)}, u32[]{:S(2)}, u32[]{:S(2)}) collective-permute-start(bf16[2,128,1024]{2,1,0:T(8,128)(2,1)} %get-tuple-element.22), channel_id=1, source_target_pairs={{0,1},{1,0},{2,3},{3,2},{4,5},{5,4},{6,7},{7,6},{8,9},{9,8},{10,11... | collective-permute-start | bytes 1572872 | tf_op jit(solution)/shard_map/ppermute | solution.py:31
  106.7 1.8 %collective-permute-done.2 = bf16[2,128,1024]{2,1,0:T(8,128)(2,1)S(1)} collective-permute-done((bf16[2,128,1024]{2,1,0:T(8,128)(2,1)}, bf16[2,128,1024]{2,1,0:T(8,128)(2,1)S(1)}, u32[]{:S(2)}, u32[]{:S(2)}) %collective-permute-start.2) | collective-permute-done | bytes 524320 | tf_op jit(solution)/shard_map/ppermute | solution.py:31
  108.5 1.4 convert_add_fusion
  109.9 0.2 fusion
  110.1 13.6 %all-to-all-done.2.pieces = bf16[8,4,32,1024]{3,2,1,0:T(8,128)(2,1)S(1)} async-done(((bf16[8,4,32,1024]{3,2,1,0:T(8,128)(2,1)}), bf16[8,4,32,1024]{3,2,1,0:T(8,128)(2,1)S(1)}, u32[]{:S(2)}, u32[]{:S(2)}) %all-to-all-start.2) | async-done | bytes 2097184 | tf_op jit(solution)/shard_map/all_to_all | solution.py:45
  123.7 1.0 shard_map.97
  124.7 30.6 %all-to-all-start.3 = ((bf16[4,32,1024]{2,1,0:T(8,128)(2,1)}), bf16[4,32,1024]{2,1,0:T(8,128)(2,1)S(1)}, u32[]{:S(2)}, u32[]{:S(2)}) async-start(bf16[4,32,1024]{2,1,0:T(8,128)(2,1)} %shard_map.97), calls=%async_computation.3 | async-start | bytes 524288 | tf_op jit(solution)/shard_map/all_to_all | solution.py:45
  155.4 1.3 fusion.5
  156.7 6.5 %collective-permute-start.3 = (bf16[128,1024]{1,0:T(8,128)(2,1)S(1)}, bf16[128,1024]{1,0:T(8,128)(2,1)S(1)}, u32[]{:S(2)}, u32[]{:S(2)}) collective-permute-start(bf16[128,1024]{1,0:T(8,128)(2,1)S(1)} %get-tuple-element.31), channel_id=1, source_target_pairs={{0,128},{128,256},{256,384},{384,512},{512,640},{640,768},{768,896... | collective-permute-start | bytes 786440 | tf_op jit(solution)/shard_map/ppermute | solution.py:36
  163.1 5.4 %collective-permute-start.4 = (bf16[128,1024]{1,0:T(8,128)(2,1)S(1)}, bf16[128,1024]{1,0:T(8,128)(2,1)S(1)}, u32[]{:S(2)}, u32[]{:S(2)}) collective-permute-start(bf16[128,1024]{1,0:T(8,128)(2,1)S(1)} %get-tuple-element.30), channel_id=1, source_target_pairs={{0,896},{128,0},{256,128},{384,256},{512,384},{640,512},{768,640},... | collective-permute-start | bytes 786440 | tf_op jit(solution)/shard_map/ppermute | solution.py:36
  168.6 3.4 %collective-permute-done.3.a = bf16[128,1024]{1,0:T(8,128)(2,1)S(1)} collective-permute-done((bf16[128,1024]{1,0:T(8,128)(2,1)S(1)}, bf16[128,1024]{1,0:T(8,128)(2,1)S(1)}, u32[]{:S(2)}, u32[]{:S(2)}) %collective-permute-start.3) | collective-permute-done | bytes 262176 | tf_op jit(solution)/shard_map/ppermute | solution.py:36
  172.0 6.8 %collective-permute-done.4.b = bf16[128,1024]{1,0:T(8,128)(2,1)S(1)} collective-permute-done((bf16[128,1024]{1,0:T(8,128)(2,1)S(1)}, bf16[128,1024]{1,0:T(8,128)(2,1)S(1)}, u32[]{:S(2)}, u32[]{:S(2)}) %collective-permute-start.4) | collective-permute-done | bytes 262176 | tf_op jit(solution)/shard_map/ppermute | solution.py:36
  178.7 0.8 shard_map.95
  179.6 0.7 shard_map.98
  (22 shorter events, 0.1 us)
Async XLA Ops:
  1.5 21.7 %collective-permute-start = (bf16[2,16,1024]{2,1,0:T(8,128)(2,1)S(1)}, bf16[2,16,1024]{2,1,0:T(8,128)(2,1)S(1)}, u32[]{:S(2)}, u32[]{:S(2)}) collective-permute-start(bf16[2,16,1024]{2,1,0:T(8,128)(2,1)S(1)} %pad_maximum_fusion.2), channel_id=1, source_target_pairs={{0,2},{1,3},{2,0},{3,1},{4,6},{5,7},{6,4},{7,5},{8,10},{9,11},{10,... | collective-permute-start | bytes 196616 | tf_op jit(solution)/shard_map/ppermute | solution.py:27
  39.7 4.9 %copy-start = (bf16[1,128,1024]{2,1,0:T(8,128)(2,1)S(1)}, bf16[1,128,1024]{2,1,0:T(8,128)(2,1)}, u32[]{:S(2)}) copy-start(bf16[1,128,1024]{2,1,0:T(8,128)(2,1)} %param.7) | copy-start | bytes 786436
  39.7 4.9 %copy-start.2 = (bf16[1,128,1024]{2,1,0:T(8,128)(2,1)S(1)}, bf16[1,128,1024]{2,1,0:T(8,128)(2,1)}, u32[]{:S(2)}) copy-start(bf16[1,128,1024]{2,1,0:T(8,128)(2,1)} %param.8) | copy-start | bytes 786436
  39.7 17.1 %copy-start.3 = (bf16[1,128,1024]{2,1,0:T(8,128)(2,1)S(1)}, bf16[1,128,1024]{2,1,0:T(8,128)(2,1)}, u32[]{:S(2)}) copy-start(bf16[1,128,1024]{2,1,0:T(8,128)(2,1)} %param.6) | copy-start | bytes 786436
  39.7 52.4 %all-to-all-start.1 = ((bf16[8,4,2,16,1024]{4,3,2,1,0:T(8,128)(2,1)}), bf16[8,4,2,16,1024]{4,3,2,1,0:T(8,128)(2,1)}, u32[]{:S(2)}, u32[]{:S(2)}) async-start(bf16[8,4,2,16,1024]{4,3,2,1,0:T(8,128)(2,1)} %broadcast_in_dim.15), calls=%async_computation.1 | async-start | bytes 4194304 | tf_op jit(solution)/shard_map/all_to_all | solution.py:41
  44.7 21.0 %collective-permute-start.5 = (bf16[256,1024]{1,0:T(8,128)(2,1)S(1)}, bf16[256,1024]{1,0:T(8,128)(2,1)S(1)}, u32[]{:S(2)}, u32[]{:S(2)}) collective-permute-start(bf16[256,1024]{1,0:T(8,128)(2,1)S(1)} %pad_maximum_fusion.1), channel_id=1, source_target_pairs={{0,2},{1,3},{2,0},{3,1},{4,6},{5,7},{6,4},{7,5},{8,10},{9,11},{10,... | collective-permute-start | bytes 1572872 | tf_op jit(solution)/shard_map/ppermute | solution.py:27
  56.9 17.7 %collective-permute-start.1 = (bf16[384,1024]{1,0:T(8,128)(2,1)S(1)}, bf16[384,1024]{1,0:T(8,128)(2,1)S(1)}, u32[]{:S(2)}, u32[]{:S(2)}) collective-permute-start(bf16[384,1024]{1,0:T(8,128)(2,1)S(1)} %pad_maximum_fusion), channel_id=1, source_target_pairs={{0,1},{1,0},{2,3},{3,2},{4,5},{5,4},{6,7},{7,6},{8,9},{9,8},{10,11... | collective-permute-start | bytes 2359304 | tf_op jit(solution)/shard_map/ppermute | solution.py:31
  65.7 19.8 %copy-start.4 = (bf16[256,1024]{1,0:T(8,128)(2,1)}, bf16[256,1024]{1,0:T(8,128)(2,1)S(1)}, u32[]{:S(2)}) copy-start(bf16[256,1024]{1,0:T(8,128)(2,1)S(1)} %collective-permute-done.5.far) | copy-start | bytes 1572868
  65.7 19.8 %collective-permute-start.6 = (bf16[256,1024]{1,0:T(8,128)(2,1)S(1)}, bf16[256,1024]{1,0:T(8,128)(2,1)S(1)}, u32[]{:S(2)}, u32[]{:S(2)}) collective-permute-start(bf16[256,1024]{1,0:T(8,128)(2,1)S(1)} %collective-permute-done.5.far), channel_id=1, source_target_pairs={{0,1},{1,0},{2,3},{3,2},{4,5},{5,4},{6,7},{7,6},{8,9},{9,8},{10,11... | collective-permute-start | bytes 1572872 | tf_op jit(solution)/shard_map/ppermute | solution.py:31
  74.6 1.0 copy-start.7
  85.5 0.8 copy-start.5
  92.1 31.6 %all-to-all-start.2 = ((bf16[8,4,32,1024]{3,2,1,0:T(8,128)(2,1)}), bf16[8,4,32,1024]{3,2,1,0:T(8,128)(2,1)S(1)}, u32[]{:S(2)}, u32[]{:S(2)}) async-start(bf16[8,4,32,1024]{3,2,1,0:T(8,128)(2,1)} %shard_map.96), calls=%async_computation.2 | async-start | bytes 4194304 | tf_op jit(solution)/shard_map/all_to_all | solution.py:45
  104.4 5.5 %copy-start.1 = (bf16[1,128,1024]{2,1,0:T(8,128)(2,1)S(1)}, bf16[1,128,1024]{2,1,0:T(8,128)(2,1)}, u32[]{:S(2)}) copy-start(bf16[1,128,1024]{2,1,0:T(8,128)(2,1)} %param.7) | copy-start | bytes 786436
  104.4 5.5 %copy-start.6 = (f32[1,1024]{1,0:T(1,128)S(1)}, f32[1,1024]{1,0:T(1,128)}, u32[]{:S(2)}) copy-start(f32[1,1024]{1,0:T(1,128)} %gain.3) | copy-start | bytes 12292
  104.4 4.1 %collective-permute-start.2 = (bf16[2,128,1024]{2,1,0:T(8,128)(2,1)}, bf16[2,128,1024]{2,1,0:T(8,128)(2,1)S(1)}, u32[]{:S(2)}, u32[]{:S(2)}) collective-permute-start(bf16[2,128,1024]{2,1,0:T(8,128)(2,1)} %get-tuple-element.22), channel_id=1, source_target_pairs={{0,1},{1,0},{2,3},{3,2},{4,5},{5,4},{6,7},{7,6},{8,9},{9,8},{10,11... | collective-permute-start | bytes 1572872 | tf_op jit(solution)/shard_map/ppermute | solution.py:31
  124.7 54.8 %all-to-all-start.3 = ((bf16[4,32,1024]{2,1,0:T(8,128)(2,1)}), bf16[4,32,1024]{2,1,0:T(8,128)(2,1)S(1)}, u32[]{:S(2)}, u32[]{:S(2)}) async-start(bf16[4,32,1024]{2,1,0:T(8,128)(2,1)} %shard_map.97), calls=%async_computation.3 | async-start | bytes 524288 | tf_op jit(solution)/shard_map/all_to_all | solution.py:45
  156.7 15.3 %collective-permute-start.3 = (bf16[128,1024]{1,0:T(8,128)(2,1)S(1)}, bf16[128,1024]{1,0:T(8,128)(2,1)S(1)}, u32[]{:S(2)}, u32[]{:S(2)}) collective-permute-start(bf16[128,1024]{1,0:T(8,128)(2,1)S(1)} %get-tuple-element.31), channel_id=1, source_target_pairs={{0,128},{128,256},{256,384},{384,512},{512,640},{640,768},{768,896... | collective-permute-start | bytes 786440 | tf_op jit(solution)/shard_map/ppermute | solution.py:36
  163.1 15.6 %collective-permute-start.4 = (bf16[128,1024]{1,0:T(8,128)(2,1)S(1)}, bf16[128,1024]{1,0:T(8,128)(2,1)S(1)}, u32[]{:S(2)}, u32[]{:S(2)}) collective-permute-start(bf16[128,1024]{1,0:T(8,128)(2,1)S(1)} %get-tuple-element.30), channel_id=1, source_target_pairs={{0,896},{128,0},{256,128},{384,256},{512,384},{640,512},{768,640},... | collective-permute-start | bytes 786440 | tf_op jit(solution)/shard_map/ppermute | solution.py:36

commit v5 on v4

--- a/solution.py
+++ b/solution.py
@@ -1,3 +1,5 @@
+import functools
+
 import jax
 import jax.numpy as jnp
 from jax import lax
@@ -19,7 +21,8 @@
 f32, bf16 = jnp.float32, jnp.bfloat16
 vmem = pl.BlockSpec(memory_space=pltpu.VMEM)
 hbm = pl.BlockSpec(memory_space=pltpu.HBM)
-CHUNK = 32
+CHUNK = 16
+EARLY = 16
 TILE = 256
 
 
@@ -36,9 +39,48 @@
     return lax.ppermute(x, axis, [(i, (i + by) % length) for i in range(length)])
 
 
-def gathered(x, groups):
-    copies = jnp.broadcast_to(x, (len(groups[0]), *x.shape))
+def gathered(x, groups, start=0, rows=None):
+    n = len(groups[0])
+    rows = rows or x.shape[-2]
+    shape = (n, *x.shape[:-2], rows, x.shape[-1])
+    (copies,) = pl.pallas_call(
+        functools.partial(copies_kernel, start, rows),
+        out_shape=[jax.ShapeDtypeStruct(shape, x.dtype)],
+        in_specs=[vmem],
+        out_specs=[hbm],
+        scratch_shapes=[pltpu.SemaphoreType.DMA((n,))],
+        compiler_params=pltpu.CompilerParams(vmem_limit_bytes=2 * 2**20),
+        cost_estimate=pl.CostEstimate(flops=2**10, bytes_accessed=2**21, transcendentals=0),
+    )(x)
     return lax.all_to_all(copies, "dp", 0, 0, tiled=True, axis_index_groups=groups)
+
+
+def pack_kernel(part, wi, wo, xb, ct, mine, others, arrived):
+    d = lax.axis_index("dp")
+    at = pl.ds(pl.multiple_of((d % NEAR * FAR + d // NEAR) * part, part), part)
+    later = xb.shape[0] - EARLY
+    pairs = [
+        (wi.at[at], mine.at[:part]),
+        (wo.at[at], mine.at[part : 2 * part]),
+        (xb.at[:EARLY], mine.at[2 * part : 2 * part + EARLY]),
+        (ct.at[:EARLY], mine.at[2 * part + EARLY :]),
+        (xb.at[EARLY:], others.at[:later]),
+        (ct.at[EARLY:], others.at[later:]),
+    ]
+    copies = [pltpu.make_async_copy(a, b, arrived.at[i]) for i, (a, b) in enumerate(pairs)]
+    for copy in copies:
+        copy.start()
+    for copy in copies:
+        copy.wait()
+
+
+def copies_kernel(start, rows, x, out, sent):
+    source = x.at[start : start + rows] if len(x.shape) == 2 else x
+    stores = [pltpu.make_async_copy(source, out.at[k], sent.at[k]) for k in range(out.shape[0])]
+    for store in stores:
+        store.start()
+    for store in stores:
+        store.wait()
 
 
 def exchanged(x, groups):
@@ -77,52 +119,76 @@
     lax.fori_loop(0, rows // CHUNK, step, None)
 
 
-def own_kernel(xf, xb, ct, near, wi, wo, gain, nf, nb, c2, br, dn, p, act_f, act, dp):
+def own_kernel(
+    xf, xb, ct, near, first, wi, wo, gain, nf, nb, c2, br, dn, p, vwi, vwo, vp, act_f, act, dp, arrived, sent
+):
     rows = xf.shape[0]
+    both = 2 * rows
     hid = wi.shape[0]
+    loads = [
+        pltpu.make_async_copy(wi, vwi, arrived.at[0]),
+        pltpu.make_async_copy(wo, vwo, arrived.at[1]),
+    ]
+    for load in loads:
+        load.start()
+    norm_into(xb, 0, gain, nb, 0, rows)
+    norm_into(near, rows, gain, nb, rows, rows)
+    norm_into(first, 2 * EARLY, gain, nb, both, EARLY)
+    norm_into(near, 3 * rows, gain, nb, both + EARLY, EARLY)
     norm_into(xf, 0, gain, nf, 0, rows)
     norm_into(near, 0, gain, nf, rows, rows)
-    norm_into(xb, 0, gain, nb, 0, rows)
-    norm_into(near, rows, gain, nb, rows, rows)
     c2[:rows, :] = ct[...]
-    c2[rows:, :] = near[2 * rows :, :]
+    c2[rows:both, :] = near[2 * rows : 3 * rows, :]
+    c2[both : both + EARLY, :] = first[3 * EARLY :, :]
+    c2[both + EARLY :, :] = near[3 * rows + EARLY :, :]
+    for load in loads:
+        load.wait()
+
+    def hidden(j, _):
+        h = pl.ds(pl.multiple_of(j * TILE, TILE), TILE)
+        value, slope = gelu_both(nt(nb[...], vwi[h, :]))
+        act[:, h] = value.astype(bf16)
+        dp[:, h] = (nt(c2[...], vwo[h, :]) * slope).astype(bf16)
+        value, _ = gelu_both(nt(nf[...], vwi[h, :]))
+        act_f[:, h] = value.astype(bf16)
+
+    lax.fori_loop(0, hid // TILE, hidden, None)
+    stores = []
+    for k in range(FAR):
+        c = slice(k * TILE, (k + 1) * TILE)
+        vp[c, :hid] = tn(nb[:, c], dp[...])
+        vp[c, hid:] = tn(c2[:, c], act[...])
+        store = pltpu.make_async_copy(vp.at[c], p.at[c], sent.at[k])
+        store.start()
+        stores.append(store)
+
+    def back(j, _):
+        c = pl.ds(pl.multiple_of(j * TILE, TILE), TILE)
+        br[:, c] = nn(act_f[...], vwo[:, c])
+        dn[:, c] = nn(dp[:both, :], vwi[:, c])
+
+    lax.fori_loop(0, vwi.shape[1] // TILE, back, None)
+    for store in stores:
+        store.wait()
+
+
+def rest_kernel(whole, nf, nb, c2, br, dn, keep, send, act_f, dp, wi, wo):
+    rows = keep.shape[1]
+    both = 2 * rows
+
+    def split(i, _):
+        r = pl.ds(pl.multiple_of(i * 16, 16), 16)
+        wi[r, :] = whole[i, 0]
+        wo[r, :] = whole[i, 1]
+
+    lax.fori_loop(0, whole.shape[0], split, None)
 
     def hidden(j, _):
         h = pl.ds(pl.multiple_of(j * TILE, TILE), TILE)
         value, _ = gelu_both(nt(nf[...], wi[h, :]))
         act_f[:, h] = value.astype(bf16)
-        value, slope = gelu_both(nt(nb[...], wi[h, :]))
-        act[:, h] = value.astype(bf16)
-        dp[:, h] = (nt(c2[...], wo[h, :]) * slope).astype(bf16)
-
-    lax.fori_loop(0, wi.shape[0] // TILE, hidden, None)
-
-    def back(j, _):
-        c = pl.ds(pl.multiple_of(j * TILE, TILE), TILE)
-        br[:, c] = nn(act_f[...], wo[:, c])
-        dn[:, c] = nn(dp[...], wi[:, c])
-        p[c, :hid] = tn(nb[:, c], dp[...])
-        p[c, hid:] = tn(c2[:, c], act[...])
-
-    lax.fori_loop(0, wi.shape[1] // TILE, back, None)
-
-
-def rest_kernel(whole, nf, nb, c2, br, dn, keep, send, act_f, dp, wi, wo):
-    rows = keep.shape[1]
-
-    def split(i, _):
-        r = pl.ds(pl.multiple_of(i * 16, 16), 16)
-        wi[r, :] = whole[i, 0]
-        wo[r, :] = whole[i, 1]
-
-    lax.fori_loop(0, whole.shape[0], split, None)
-
-    def hidden(j, _):
-        h = pl.ds(pl.multiple_of(j * TILE, TILE), TILE)
-        value, _ = gelu_both(nt(nf[...], wi[h, :]))
-        act_f[:, h] = value.astype(bf16)
-        _, slope = gelu_both(nt(nb[...], wi[h, :]))
-        dp[:, h] = (nt(c2[...], wo[h, :]) * slope).astype(bf16)
+        _, slope = gelu_both(nt(nb[:both, :], wi[h, :]))
+        dp[:, h] = (nt(c2[:both, :], wo[h, :]) * slope).astype(bf16)
 
     lax.fori_loop(0, wi.shape[0] // TILE, hidden, None)
 
@@ -212,23 +278,45 @@
     hid = wi.shape[0]
     both = 2 * rows
     n_dp = lax.axis_size("dp")
-    d = lax.axis_index("dp")
     part = hid // n_dp
-    at = (d % NEAR * FAR + d // NEAR) * part
-    mine = jnp.stack(
-        [lax.dynamic_slice_in_dim(wi, at, part, 0), lax.dynamic_slice_in_dim(wo, at, part, 0)]
-    )
-    piece = to_chip(mine)
-    far = to_chip(jnp.concatenate([xb, ct]))
-    near = to_core(jnp.concatenate([xf, xb, ct]))
+    mine, others = pl.pallas_call(
+        functools.partial(pack_kernel, part),
+        out_shape=[
+            jax.ShapeDtypeStruct((2 * part + 2 * EARLY, dim), bf16),
+            jax.ShapeDtypeStruct((2 * (rows - EARLY), dim), bf16),
+        ],
+        in_specs=[hbm] * 4,
+        out_specs=[vmem] * 2,
+        scratch_shapes=[pltpu.SemaphoreType.DMA((6,))],
+        compiler_params=pltpu.CompilerParams(vmem_limit_bytes=62 * 2**20),
+        cost_estimate=pl.CostEstimate(flops=2**10, bytes_accessed=2**20, transcendentals=0),
+    )(wi, wo, xb, ct)
+    first = to_chip(mine)
+    far = to_chip(others)
+    near = to_core(jnp.concatenate([xf, xb, ct, first[2 * part :]]))
+    more = both + 2 * EARLY
     nf, nb, c2, br, dn, p = local(
         own_kernel,
-        [((both, dim), bf16)] * 3 + [((both, dim), f32)] * 2 + [((dim, 2 * hid), f32)],
-        [((both, hid), bf16)] * 3,
+        [((both, dim), bf16)]
+        + [((more, dim), bf16)] * 2
+        + [((both, dim), f32)] * 2
+        + [((dim, 2 * hid), f32)],
+        [
+            ((hid, dim), bf16),
+            ((hid, dim), bf16),
+            ((dim, 2 * hid), f32),
+            ((both, hid), bf16),
+            ((more, hid), bf16),
+            ((more, hid), bf16),
+            pltpu.SemaphoreType.DMA((2,)),
+            pltpu.SemaphoreType.DMA((FAR,)),
+        ],
         14 * both * hid * dim,
         11 * 2**20,
-    )(xf, xb, ct, near, wi, wo, gain)
-    col = gathered(piece, far_groups)
+        in_specs=[vmem] * 5 + [hbm, hbm, vmem],
+        out_specs=[vmem] * 5 + [hbm],
+    )(xf, xb, ct, near, first, wi, wo, gain)
+    col = gathered(first, far_groups, 0, 2 * part)
     whole = gathered(col, near_groups).reshape(n_dp, 2, part, dim)
     keep, send = local(
         rest_kernel,
@@ -257,10 +345,10 @@
             ((hid, dim), bf16),
             ((dim, 2 * hid), f32),
             ((NEAR, FAR, cut, 2 * hid), bf16),
-            ((both, dim), bf16),
-            ((both, dim), bf16),
-            ((both, hid), bf16),
-            ((both, hid), bf16),
+            ((both - 2 * EARLY, dim), bf16),
+            ((both - 2 * EARLY, dim), bf16),
+            ((both - 2 * EARLY, hid), bf16),
+            ((both - 2 * EARLY, hid), bf16),
             pltpu.SemaphoreType.DMA((3,)),
             pltpu.SemaphoreType.DMA((FAR,)),
         ],

time: 181 us -> 188 us (1.039)
  the two profiles are of different devices: /device:TPU:1 before, /device:TPU:40 now
where the time goes in v5:
time: 188 us; the launch traced here: 187 us
  starting transfers between devices  98.3 us (52%)
  waiting for transfers between devices  41.6 us (22%)
  Pallas kernels  29.7 us (16%)
  blocking collectives  12.9 us (7%)
    ppermute x2, starting transfers between devices, shifted(): lax.ppermute(x, axis, [(i, (i + by) % length) for i in range(length)])  40.8 us
    ppermute x2, starting transfers between devices, to_chip(): return lax.ppermute(x, 'mp', other_chip)  31.7 us
    all_to_all x2, waiting for transfers between devices, exchanged(): return lax.all_to_all(x, 'dp', 0, 0, tiled=True, axis_index_groups=groups)  17.2 us
    ppermute x2, waiting for transfers between devices, to_chip(): return lax.ppermute(x, 'mp', other_chip)  15.5 us
    all_to_all x2, starting transfers between devices, exchanged(): return lax.all_to_all(x, 'dp', 0, 0, tiled=True, axis_index_groups=groups)  13.7 us
    all_to_all x1, blocking collectives, gathered(): lax.all_to_all(copies, 'dp', 0, 0, tiled=True, axis_index_groups=groups)  12.9 us
    pallas_call x1, Pallas kernels, layer(): local(own_kernel, [((both, dim), bf16)] + [((more, dim), bf16)] * 2 + [((...  10.7 us
    ppermute x2, waiting for transfers between devices, shifted(): lax.ppermute(x, axis, [(i, (i + by) % length) for i in range(length)])  8.84 us
  transfers between devices with their start and end apart: 10, of which 5 were waited for; matrix products, arithmetic and copies ran while one was open for 1% of the time, Pallas kernels for 13%

profile of v5, /device:TPU:40, one launch (start us, length us, event | category | flops | bytes accessed | tf_op | source)
XLA Modules:
  0.0 187.1 jit_solution(7525202608066310812)
XLA Ops:
  0.6 2.0 %shard_map.93 = (bf16[64,1024]{1,0:T(8,128)(2,1)}, bf16[224,1024]{1,0:T(8,128)(2,1)}) custom-call(bf16[512,1024]{1,0:T(8,128)(2,1)} %bitcast.35, bf16[512,1024]{1,0:T(8,128)(2,1)} %bitcast.38, bf16[128,1024]{1,0:T(8,128)(2,1)} %bitcast.32, bf16[128,1024]{1,0:T(8,128)(2,1)} %bitcast.41), custom_call_target="tpu_custom_call" | custom-call | flops 1024 | bytes 1048576 | tf_op jit(solution)/shard_map/pallas_call | solution.py:282
  2.7 19.4 %collective-permute-start = (bf16[64,1024]{1,0:T(8,128)(2,1)}, bf16[64,1024]{1,0:T(8,128)(2,1)S(1)}, u32[]{:S(2)}, u32[]{:S(2)}) collective-permute-start(bf16[64,1024]{1,0:T(8,128)(2,1)} %get-tuple-element.18), channel_id=1, source_target_pairs={{0,2},{1,3},{2,0},{3,1},{4,6},{5,7},{6,4},{7,5},{8,10},{9,11},{10,... | collective-permute-start | bytes 393224 | tf_op jit(solution)/shard_map/ppermute | solution.py:30
  22.0 4.0 %collective-permute-done.x.first = bf16[64,1024]{1,0:T(8,128)(2,1)S(1)} collective-permute-done((bf16[64,1024]{1,0:T(8,128)(2,1)}, bf16[64,1024]{1,0:T(8,128)(2,1)S(1)}, u32[]{:S(2)}, u32[]{:S(2)}) %collective-permute-start) | collective-permute-done | bytes 131104 | tf_op jit(solution)/shard_map/ppermute | solution.py:30
  26.0 0.4 shard_map.94
  26.4 12.9 %all_to_all.20.x = bf16[4,32,1024]{2,1,0:T(8,128)(2,1)S(1)} all-to-all(bf16[4,32,1024]{2,1,0:T(8,128)(2,1)S(1)} %shard_map.94), channel_id=1, replica_groups={{0,32,64,96},{4,36,68,100},{8,40,72,104},{12,44,76,108},{16,48,80,112},..., dimensions={0} | all-to-all | bytes 524288 | tf_op jit(solution)/shard_map/all_to_all | solution.py:55
  39.3 1.5 shard_map.95
  40.8 0.0 copy-start.3
  40.8 6.1 %all-to-all-start.1 = ((bf16[8,4,32,1024]{3,2,1,0:T(8,128)(2,1)}), bf16[8,4,32,1024]{3,2,1,0:T(8,128)(2,1)}, u32[]{:S(2)}, u32[]{:S(2)}) async-start(bf16[8,4,32,1024]{3,2,1,0:T(8,128)(2,1)} %shard_map.95), calls=%async_computation.1 | async-start | bytes 4194304 | tf_op jit(solution)/shard_map/all_to_all | solution.py:55
  47.0 0.1 pad_maximum_fusion
  47.0 2.1 %collective-permute-start.1 = (bf16[416,1024]{1,0:T(8,128)(2,1)S(1)}, bf16[416,1024]{1,0:T(8,128)(2,1)S(1)}, u32[]{:S(2)}, u32[]{:S(2)}) collective-permute-start(bf16[416,1024]{1,0:T(8,128)(2,1)S(1)} %pad_maximum_fusion), channel_id=1, source_target_pairs={{0,1},{1,0},{2,3},{3,2},{4,5},{5,4},{6,7},{7,6},{8,9},{9,8},{10,11... | collective-permute-start | bytes 2555912 | tf_op jit(solution)/shard_map/ppermute | solution.py:34
  49.1 12.3 %collective-permute-start.5 = (bf16[224,1024]{1,0:T(8,128)(2,1)S(1)}, bf16[224,1024]{1,0:T(8,128)(2,1)S(1)}, u32[]{:S(2)}, u32[]{:S(2)}) collective-permute-start(bf16[224,1024]{1,0:T(8,128)(2,1)S(1)} %copy-done.12), channel_id=1, source_target_pairs={{0,2},{1,3},{2,0},{3,1},{4,6},{5,7},{6,4},{7,5},{8,10},{9,11},{10,... | collective-permute-start | bytes 1376264 | tf_op jit(solution)/shard_map/ppermute | solution.py:30
  61.4 11.5 %collective-permute-done.5.far = bf16[224,1024]{1,0:T(8,128)(2,1)S(1)} collective-permute-done((bf16[224,1024]{1,0:T(8,128)(2,1)S(1)}, bf16[224,1024]{1,0:T(8,128)(2,1)S(1)}, u32[]{:S(2)}, u32[]{:S(2)}) %collective-permute-start.5) | collective-permute-done | bytes 458784 | tf_op jit(solution)/shard_map/ppermute | solution.py:30
  72.9 1.9 %collective-permute-start.6 = (bf16[224,1024]{1,0:T(8,128)(2,1)S(1)}, bf16[224,1024]{1,0:T(8,128)(2,1)S(1)}, u32[]{:S(2)}, u32[]{:S(2)}) collective-permute-start(bf16[224,1024]{1,0:T(8,128)(2,1)S(1)} %collective-permute-done.5.far), channel_id=1, source_target_pairs={{0,1},{1,0},{2,3},{3,2},{4,5},{5,4},{6,7},{7,6},{8,9},{9,8},{10,11... | collective-permute-start | bytes 1376264 | tf_op jit(solution)/shard_map/ppermute | solution.py:34
  74.9 1.0 copy-done.11
  75.9 10.7 %shard_map.96 = (bf16[256,1024]{1,0:T(8,128)(2,1)}, bf16[288,1024]{1,0:T(8,128)(2,1)}, bf16[288,1024]{1,0:T(8,128)(2,1)}, f32[256,1024]{1,0:T(8,128)}, f32[256,1024]{1,0:T(8,128)}, /*index=5*/f32[1024,1024]{1,0:T(8,128)}) custom-call(bf16[128,1024]{1,0:T(8,128)(2,1)} %bitcast.44, bf16[128,1024]{1,0:T(8,128)(2,1)} %bitcast.33, bf16[128,1024]{1,0:T(8,128)(2,1)} %bitcast.42, ...), custom_call_target="tpu_custom_call" | custom-call | flops 1879048192 | bytes 11534336 | tf_op jit(solution)/shard_map/pallas_call | solution.py:298
  86.6 0.8 copy-done.9
  87.4 5.8 %shard_map.99 = bf16[8,4,32,1024]{3,2,1,0:T(8,128)(2,1)} custom-call(bf16[224,1024]{1,0:T(8,128)(2,1)} %copy-done.8, bf16[224,1024]{1,0:T(8,128)(2,1)} %copy-done.9, bf16[512,1024]{1,0:T(8,128)(2,1)} %bitcast.37, bf16[512,1024]{1,0:T(8,128)(2,1)} %bitcast.40, f32[1,1024]{1,0:T(1,128)} %gain.3, f32[1024,1024]{1,0:T(8,128)} %get-tuple-element.29.p), custom_call_target="tpu_custom_call" | custom-call | flops 1073741824 | bytes 9437184 | tf_op jit(solution)/shard_map/pallas_call | solution.py:340
  93.2 5.7 %all-to-all-start.2 = ((bf16[8,4,32,1024]{3,2,1,0:T(8,128)(2,1)}), bf16[8,4,32,1024]{3,2,1,0:T(8,128)(2,1)S(1)}, u32[]{:S(2)}, u32[]{:S(2)}) async-start(bf16[8,4,32,1024]{3,2,1,0:T(8,128)(2,1)} %shard_map.99), calls=%async_computation.2 | async-start | bytes 4194304 | tf_op jit(solution)/shard_map/all_to_all | solution.py:87
  98.9 6.9 %shard_map.97 = (f32[2,128,1024]{2,1,0:T(8,128)}, bf16[2,128,1024]{2,1,0:T(8,128)(2,1)}) custom-call(bf16[32,2,16,1024]{3,2,1,0:T(8,128)(2,1)} %bitcast.5.whole, bf16[256,1024]{1,0:T(8,128)(2,1)} %get-tuple-element.19.nf, bf16[288,1024]{1,0:T(8,128)(2,1)} %get-tuple-element.20.nb, bf16[288,1024]{1,0:T(8,128)(2,1)} %get-tuple-element.21.c2, ...), custom_call_target="tpu_custom_call" | custom-call | flops 1342177280 | bytes 8388608 | tf_op jit(solution)/shard_map/pallas_call | solution.py:321
  105.8 2.0 %collective-permute-start.2 = (bf16[2,128,1024]{2,1,0:T(8,128)(2,1)}, bf16[2,128,1024]{2,1,0:T(8,128)(2,1)}, u32[]{:S(2)}, u32[]{:S(2)}) collective-permute-start(bf16[2,128,1024]{2,1,0:T(8,128)(2,1)} %get-tuple-element.25), channel_id=1, source_target_pairs={{0,1},{1,0},{2,3},{3,2},{4,5},{5,4},{6,7},{7,6},{8,9},{9,8},{10,11... | collective-permute-start | bytes 1572872 | tf_op jit(solution)/shard_map/ppermute | solution.py:34
  107.8 17.2 %all-to-all-done.2.pieces = bf16[8,4,32,1024]{3,2,1,0:T(8,128)(2,1)S(1)} async-done(((bf16[8,4,32,1024]{3,2,1,0:T(8,128)(2,1)}), bf16[8,4,32,1024]{3,2,1,0:T(8,128)(2,1)S(1)}, u32[]{:S(2)}, u32[]{:S(2)}) %all-to-all-start.2) | async-done | bytes 2097184 | tf_op jit(solution)/shard_map/all_to_all | solution.py:87
  125.1 1.0 shard_map.100
  126.1 8.0 %all-to-all-start.3 = ((bf16[4,32,1024]{2,1,0:T(8,128)(2,1)}), bf16[4,32,1024]{2,1,0:T(8,128)(2,1)S(1)}, u32[]{:S(2)}, u32[]{:S(2)}) async-start(bf16[4,32,1024]{2,1,0:T(8,128)(2,1)} %shard_map.100), calls=%async_computation.3 | async-start | bytes 524288 | tf_op jit(solution)/shard_map/all_to_all | solution.py:87
  134.1 1.3 convert_add_fusion
  135.4 0.2 fusion
  135.6 0.3 fusion.5
  135.9 38.9 %collective-permute-start.3 = (bf16[128,1024]{1,0:T(8,128)(2,1)S(1)}, bf16[128,1024]{1,0:T(8,128)(2,1)S(1)}, u32[]{:S(2)}, u32[]{:S(2)}) collective-permute-start(bf16[128,1024]{1,0:T(8,128)(2,1)S(1)} %get-tuple-element.35), channel_id=1, source_target_pairs={{0,128},{128,256},{256,384},{384,512},{512,640},{640,768},{768,896... | collective-permute-start | bytes 786440 | tf_op jit(solution)/shard_map/ppermute | solution.py:39
  174.8 1.9 %collective-permute-start.4 = (bf16[128,1024]{1,0:T(8,128)(2,1)S(1)}, bf16[128,1024]{1,0:T(8,128)(2,1)S(1)}, u32[]{:S(2)}, u32[]{:S(2)}) collective-permute-start(bf16[128,1024]{1,0:T(8,128)(2,1)S(1)} %get-tuple-element.34), channel_id=1, source_target_pairs={{0,896},{128,0},{256,128},{384,256},{512,384},{640,512},{768,640},... | collective-permute-start | bytes 786440 | tf_op jit(solution)/shard_map/ppermute | solution.py:39
  176.7 4.7 %collective-permute-done.3.a = bf16[128,1024]{1,0:T(8,128)(2,1)S(1)} collective-permute-done((bf16[128,1024]{1,0:T(8,128)(2,1)S(1)}, bf16[128,1024]{1,0:T(8,128)(2,1)S(1)}, u32[]{:S(2)}, u32[]{:S(2)}) %collective-permute-start.3) | collective-permute-done | bytes 262176 | tf_op jit(solution)/shard_map/ppermute | solution.py:39
  181.5 4.1 %collective-permute-done.4.b = bf16[128,1024]{1,0:T(8,128)(2,1)S(1)} collective-permute-done((bf16[128,1024]{1,0:T(8,128)(2,1)S(1)}, bf16[128,1024]{1,0:T(8,128)(2,1)S(1)}, u32[]{:S(2)}, u32[]{:S(2)}) %collective-permute-start.4) | collective-permute-done | bytes 262176 | tf_op jit(solution)/shard_map/ppermute | solution.py:39
  185.6 0.8 shard_map.98
  186.4 0.7 shard_map.101
  (30 shorter events, 0.1 us)
Async XLA Ops:
  2.7 23.4 %collective-permute-start = (bf16[64,1024]{1,0:T(8,128)(2,1)}, bf16[64,1024]{1,0:T(8,128)(2,1)S(1)}, u32[]{:S(2)}, u32[]{:S(2)}) collective-permute-start(bf16[64,1024]{1,0:T(8,128)(2,1)} %get-tuple-element.18), channel_id=1, source_target_pairs={{0,2},{1,3},{2,0},{3,1},{4,6},{5,7},{6,4},{7,5},{8,10},{9,11},{10,... | collective-permute-start | bytes 393224 | tf_op jit(solution)/shard_map/ppermute | solution.py:30
  26.0 20.9 %copy-start = (bf16[64,1024]{1,0:T(8,128)(2,1)}, bf16[64,1024]{1,0:T(8,128)(2,1)S(1)}, u32[]{:S(2)}) copy-start(bf16[64,1024]{1,0:T(8,128)(2,1)S(1)} %collective-permute-done.x.first) | copy-start | bytes 393220
  40.8 6.2 %copy-start.1 = (bf16[1,128,1024]{2,1,0:T(8,128)(2,1)S(1)}, bf16[1,128,1024]{2,1,0:T(8,128)(2,1)}, u32[]{:S(2)}) copy-start(bf16[1,128,1024]{2,1,0:T(8,128)(2,1)} %param.7) | copy-start | bytes 786436
  40.8 6.2 %copy-start.3 = (bf16[1,128,1024]{2,1,0:T(8,128)(2,1)S(1)}, bf16[1,128,1024]{2,1,0:T(8,128)(2,1)}, u32[]{:S(2)}) copy-start(bf16[1,128,1024]{2,1,0:T(8,128)(2,1)} %param.8) | copy-start | bytes 786436
  40.8 6.2 %copy-start.6 = (bf16[1,128,1024]{2,1,0:T(8,128)(2,1)S(1)}, bf16[1,128,1024]{2,1,0:T(8,128)(2,1)}, u32[]{:S(2)}) copy-start(bf16[1,128,1024]{2,1,0:T(8,128)(2,1)} %param.6) | copy-start | bytes 786436
  40.8 52.4 %all-to-all-start.1 = ((bf16[8,4,32,1024]{3,2,1,0:T(8,128)(2,1)}), bf16[8,4,32,1024]{3,2,1,0:T(8,128)(2,1)}, u32[]{:S(2)}, u32[]{:S(2)}) async-start(bf16[8,4,32,1024]{3,2,1,0:T(8,128)(2,1)} %shard_map.95), calls=%async_computation.1 | async-start | bytes 4194304 | tf_op jit(solution)/shard_map/all_to_all | solution.py:55
  46.9 2.2 %copy-start.12 = (bf16[224,1024]{1,0:T(8,128)(2,1)S(1)}, bf16[224,1024]{1,0:T(8,128)(2,1)}, u32[]{:S(2)}) copy-start(bf16[224,1024]{1,0:T(8,128)(2,1)} %get-tuple-element.28) | copy-start | bytes 1376260
  47.0 27.8 %collective-permute-start.1 = (bf16[416,1024]{1,0:T(8,128)(2,1)S(1)}, bf16[416,1024]{1,0:T(8,128)(2,1)S(1)}, u32[]{:S(2)}, u32[]{:S(2)}) collective-permute-start(bf16[416,1024]{1,0:T(8,128)(2,1)S(1)} %pad_maximum_fusion), channel_id=1, source_target_pairs={{0,1},{1,0},{2,3},{3,2},{4,5},{5,4},{6,7},{7,6},{8,9},{9,8},{10,11... | collective-permute-start | bytes 2555912 | tf_op jit(solution)/shard_map/ppermute | solution.py:34
  49.1 23.8 %collective-permute-start.5 = (bf16[224,1024]{1,0:T(8,128)(2,1)S(1)}, bf16[224,1024]{1,0:T(8,128)(2,1)S(1)}, u32[]{:S(2)}, u32[]{:S(2)}) collective-permute-start(bf16[224,1024]{1,0:T(8,128)(2,1)S(1)} %copy-done.12), channel_id=1, source_target_pairs={{0,2},{1,3},{2,0},{3,1},{4,6},{5,7},{6,4},{7,5},{8,10},{9,11},{10,... | collective-permute-start | bytes 1376264 | tf_op jit(solution)/shard_map/ppermute | solution.py:30
  72.9 13.7 %copy-start.8 = (bf16[224,1024]{1,0:T(8,128)(2,1)}, bf16[224,1024]{1,0:T(8,128)(2,1)S(1)}, u32[]{:S(2)}) copy-start(bf16[224,1024]{1,0:T(8,128)(2,1)S(1)} %collective-permute-done.5.far) | copy-start | bytes 1376260
  72.9 13.7 %collective-permute-start.6 = (bf16[224,1024]{1,0:T(8,128)(2,1)S(1)}, bf16[224,1024]{1,0:T(8,128)(2,1)S(1)}, u32[]{:S(2)}, u32[]{:S(2)}) collective-permute-start(bf16[224,1024]{1,0:T(8,128)(2,1)S(1)} %collective-permute-done.5.far), channel_id=1, source_target_pairs={{0,1},{1,0},{2,3},{3,2},{4,5},{5,4},{6,7},{7,6},{8,9},{9,8},{10,11... | collective-permute-start | bytes 1376264 | tf_op jit(solution)/shard_map/ppermute | solution.py:34
  74.9 1.0 copy-start.11
  86.6 0.8 copy-start.9
  93.2 31.8 %all-to-all-start.2 = ((bf16[8,4,32,1024]{3,2,1,0:T(8,128)(2,1)}), bf16[8,4,32,1024]{3,2,1,0:T(8,128)(2,1)S(1)}, u32[]{:S(2)}, u32[]{:S(2)}) async-start(bf16[8,4,32,1024]{3,2,1,0:T(8,128)(2,1)} %shard_map.99), calls=%async_computation.2 | async-start | bytes 4194304 | tf_op jit(solution)/shard_map/all_to_all | solution.py:87
  105.8 28.3 %copy-start.5 = (f32[2,128,1024]{2,1,0:T(8,128)S(1)}, f32[2,128,1024]{2,1,0:T(8,128)}, u32[]{:S(2)}) copy-start(f32[2,128,1024]{2,1,0:T(8,128)} %get-tuple-element.24) | copy-start | bytes 3145732
  105.8 28.3 %collective-permute-start.2 = (bf16[2,128,1024]{2,1,0:T(8,128)(2,1)}, bf16[2,128,1024]{2,1,0:T(8,128)(2,1)}, u32[]{:S(2)}, u32[]{:S(2)}) collective-permute-start(bf16[2,128,1024]{2,1,0:T(8,128)(2,1)} %get-tuple-element.25), channel_id=1, source_target_pairs={{0,1},{1,0},{2,3},{3,2},{4,5},{5,4},{6,7},{7,6},{8,9},{9,8},{10,11... | collective-permute-start | bytes 1572872 | tf_op jit(solution)/shard_map/ppermute | solution.py:34
  126.1 9.3 %copy-start.2 = (bf16[1,128,1024]{2,1,0:T(8,128)(2,1)S(1)}, bf16[1,128,1024]{2,1,0:T(8,128)(2,1)}, u32[]{:S(2)}) copy-start(bf16[1,128,1024]{2,1,0:T(8,128)(2,1)} %param.7) | copy-start | bytes 786436
  126.1 9.3 %copy-start.10 = (f32[1,1024]{1,0:T(1,128)S(1)}, f32[1,1024]{1,0:T(1,128)}, u32[]{:S(2)}) copy-start(f32[1,1024]{1,0:T(1,128)} %gain.3) | copy-start | bytes 12292
  126.1 60.4 %all-to-all-start.3 = ((bf16[4,32,1024]{2,1,0:T(8,128)(2,1)}), bf16[4,32,1024]{2,1,0:T(8,128)(2,1)S(1)}, u32[]{:S(2)}, u32[]{:S(2)}) async-start(bf16[4,32,1024]{2,1,0:T(8,128)(2,1)} %shard_map.100), calls=%async_computation.3 | async-start | bytes 524288 | tf_op jit(solution)/shard_map/all_to_all | solution.py:87
  134.1 1.5 copy-start.4
  134.1 1.5 copy-start.7
  135.9 45.6 %collective-permute-start.3 = (bf16[128,1024]{1,0:T(8,128)(2,1)S(1)}, bf16[128,1024]{1,0:T(8,128)(2,1)S(1)}, u32[]{:S(2)}, u32[]{:S(2)}) collective-permute-start(bf16[128,1024]{1,0:T(8,128)(2,1)S(1)} %get-tuple-element.35), channel_id=1, source_target_pairs={{0,128},{128,256},{256,384},{384,512},{512,640},{640,768},{768,896... | collective-permute-start | bytes 786440 | tf_op jit(solution)/shard_map/ppermute | solution.py:39
  174.8 10.8 %collective-permute-start.4 = (bf16[128,1024]{1,0:T(8,128)(2,1)S(1)}, bf16[128,1024]{1,0:T(8,128)(2,1)S(1)}, u32[]{:S(2)}, u32[]{:S(2)}) collective-permute-start(bf16[128,1024]{1,0:T(8,128)(2,1)S(1)} %get-tuple-element.34), channel_id=1, source_target_pairs={{0,896},{128,0},{256,128},{384,256},{512,384},{640,512},{768,640},... | collective-permute-start | bytes 786440 | tf_op jit(solution)/shard_map/ppermute | solution.py:39

commit v6 on v4

--- a/solution.py
+++ b/solution.py
@@ -138,35 +138,48 @@
     lax.fori_loop(0, wi.shape[1] // TILE, back, None)
 
 
-def grad_kernel(far, far2, wi, wo, gain, p, g, vwi, vwo, vp, vg, nb3, c3, act3, dp3, arrived, sent):
-    rows = far.shape[0] // 2
-    hid = wi.shape[0]
-    loads = [
-        pltpu.make_async_copy(src, dst, arrived.at[i])
-        for i, (src, dst) in enumerate([(wi, vwi), (wo, vwo), (p, vp)])
-    ]
+def half_kernel(far, far2, wi, gain, nbt, act, slope, nb):
+    rows = far.shape[0]
+    for k, part in enumerate((far, far2)):
+        norm_into(part, 0, gain, nb, k * rows, rows)
+
+    def hidden(j, _):
+        h = pl.ds(pl.multiple_of(j * TILE, TILE), TILE)
+        value, down = gelu_both(nt(nb[...], wi[h, :]))
+        act[:, h] = value.astype(bf16)
+        slope[:, h] = down
+        for k in range(2):
+            c = pl.ds(pl.multiple_of((2 * j + k) * TILE, TILE), TILE)
+            nbt[c, :] = nb[:, c].T
+
+    lax.fori_loop(0, wi.shape[0] // TILE, hidden, None)
+
+
+def grad_kernel(far, far2, wo, nbt, act, slope, p, g, vwo, vnbt, vact, vslope, vp, vg, c3, dp3, arrived, sent):
+    rows = far.shape[0]
+    hid = wo.shape[0]
+    pairs = [(wo, vwo), (slope, vslope), (nbt, vnbt), (act, vact), (p, vp)]
+    loads = [pltpu.make_async_copy(a, b, arrived.at[i]) for i, (a, b) in enumerate(pairs)]
     for load in loads:
         load.start()
-    for k, half in enumerate((far, far2)):
-        norm_into(half, 0, gain, nb3, k * rows, rows)
-        c3[k * rows : (k + 1) * rows, :] = half[rows:, :]
+    c3[:rows, :] = far[...]
+    c3[rows:, :] = far2[...]
     loads[0].wait()
     loads[1].wait()
 
     def hidden(j, _):
         h = pl.ds(pl.multiple_of(j * TILE, TILE), TILE)
-        value, slope = gelu_both(nt(nb3[...], vwi[h, :]))
-        act3[:, h] = value.astype(bf16)
-        dp3[:, h] = (nt(c3[...], vwo[h, :]) * slope).astype(bf16)
+        dp3[:, h] = (nt(c3[...], vwo[h, :]) * vslope[:, h]).astype(bf16)
 
     lax.fori_loop(0, hid // TILE, hidden, None)
-    loads[2].wait()
+    for load in loads[2:]:
+        load.wait()
     stores = []
     for k in range(FAR):
         c = slice(k * TILE, (k + 1) * TILE)
-        gi = vp[c, :hid] + tn(nb3[:, c], dp3[...])
+        gi = vp[c, :hid] + nn(vnbt[c, :], dp3[...])
         vg[:, k, :, :hid] = gi.astype(bf16).reshape(NEAR, -1, hid)
-        go = vp[c, hid:] + tn(c3[:, c], act3[...])
+        go = vp[c, hid:] + tn(c3[:, c], vact[...])
         vg[:, k, :, hid:] = go.astype(bf16).reshape(NEAR, -1, hid)
         store = pltpu.make_async_copy(vg.at[:, k], g.at[:, k], sent.at[k])
         store.start()
@@ -219,7 +232,8 @@
         [lax.dynamic_slice_in_dim(wi, at, part, 0), lax.dynamic_slice_in_dim(wo, at, part, 0)]
     )
     piece = to_chip(mine)
-    far = to_chip(jnp.concatenate([xb, ct]))
+    far_s = to_chip(xb)
+    far_c = to_chip(ct)
     near = to_core(jnp.concatenate([xf, xb, ct]))
     nf, nb, c2, br, dn, p = local(
         own_kernel,
@@ -247,29 +261,36 @@
     mixed = jnp.mean(shard_x * push, axis=-1, keepdims=True)
     dx = ct.astype(f32) + scale * push - shard_x * scale * scale * scale * mixed
     passed_grad = shifted(dx.astype(bf16), "section", -1)
-    far2 = to_core(far)
+    far_s2 = to_core(far_s)
+    nbt3, act3, slope3 = local(
+        half_kernel,
+        [((dim, both), bf16), ((both, hid), bf16), ((both, hid), f32)],
+        [((both, dim), bf16)],
+        2 * both * hid * dim,
+        4 * 2**20,
+    )(far_s, far_s2, wi, gain)
+    far_c2 = to_core(far_c)
     cut = dim // n_dp
     (g,) = local(
         grad_kernel,
         [((NEAR, FAR, cut, 2 * hid), bf16)],
         [
             ((hid, dim), bf16),
-            ((hid, dim), bf16),
+            ((dim, both), bf16),
+            ((both, hid), bf16),
+            ((both, hid), f32),
             ((dim, 2 * hid), f32),
             ((NEAR, FAR, cut, 2 * hid), bf16),
             ((both, dim), bf16),
-            ((both, dim), bf16),
             ((both, hid), bf16),
-            ((both, hid), bf16),
-            pltpu.SemaphoreType.DMA((3,)),
+            pltpu.SemaphoreType.DMA((5,)),
             pltpu.SemaphoreType.DMA((FAR,)),
         ],
-        8 * both * hid * dim,
+        6 * both * hid * dim,
         9 * 2**20,
-        mib=60,
-        in_specs=[vmem, vmem, hbm, hbm, vmem, hbm],
+        in_specs=[vmem, vmem, hbm, hbm, hbm, hbm, hbm],
         out_specs=[hbm],
-    )(far, far2, wi, wo, gain, p)
+    )(far_c, far_c2, wo, nbt3, act3, slope3, p)
     g = exchanged(g, near_groups)
     (g,) = local(sum_kernel, [(g.shape[1:], bf16)], [], 2**21, 2**21, mib=16)(g)
     g = exchanged(g, far_groups)

time: 181 us -> 187 us (1.033)
  the two profiles are of different devices: /device:TPU:1 before, /device:TPU:40 now
where the time goes in v6:
time: 187 us; the launch traced here: 186 us
  starting transfers between devices  86.6 us (46%)
  waiting for transfers between devices  51.6 us (28%)
  Pallas kernels  29.2 us (16%)
  blocking collectives  11.5 us (6%)
  local copies, waits for them, and re-layouts  4.63 us (2%)
    ppermute x3, starting transfers between devices, to_chip(): return lax.ppermute(x, 'mp', other_chip)  34.5 us
    ppermute x3, waiting for transfers between devices, to_chip(): return lax.ppermute(x, 'mp', other_chip)  26.2 us
    ppermute x2, starting transfers between devices, shifted(): lax.ppermute(x, axis, [(i, (i + by) % length) for i in range(length)])  23.2 us
    all_to_all x2, waiting for transfers between devices, exchanged(): return lax.all_to_all(x, 'dp', 0, 0, tiled=True, axis_index_groups=groups)  17.3 us
    all_to_all x2, starting transfers between devices, exchanged(): return lax.all_to_all(x, 'dp', 0, 0, tiled=True, axis_index_groups=groups)  14.8 us
    all_to_all x1, blocking collectives, gathered(): lax.all_to_all(copies, 'dp', 0, 0, tiled=True, axis_index_groups=groups)  11.5 us
    pallas_call x1, Pallas kernels, layer(): local(own_kernel, [((both, dim), bf16)] * 3 + [((both, dim), f32)] * 2 +...  9.96 us
    ppermute x2, waiting for transfers between devices, shifted(): lax.ppermute(x, axis, [(i, (i + by) % length) for i in range(length)])  8.17 us
  transfers between devices with their start and end apart: 12, of which 6 were waited for; matrix products, arithmetic and copies ran while one was open for 1% of the time, Pallas kernels for 15%

profile of v6, /device:TPU:40, one launch (start us, length us, event | category | flops | bytes accessed | tf_op | source)
XLA Modules:
  0.0 186.3 jit_solution(9909109141452454977)
XLA Ops:
  0.7 0.8 constant_dynamic-slice_fusion
  1.4 0.8 constant_dynamic-slice_fusion.1
  2.2 19.4 %collective-permute-start = (bf16[2,16,1024]{2,1,0:T(8,128)(2,1)S(1)}, bf16[2,16,1024]{2,1,0:T(8,128)(2,1)S(1)}, u32[]{:S(2)}, u32[]{:S(2)}) collective-permute-start(bf16[2,16,1024]{2,1,0:T(8,128)(2,1)S(1)} %pad_maximum_fusion.1), channel_id=1, source_target_pairs={{0,2},{1,3},{2,0},{3,1},{4,6},{5,7},{6,4},{7,5},{8,10},{9,11},{10,... | collective-permute-start | bytes 196616 | tf_op jit(solution)/shard_map/ppermute | solution.py:27
  21.6 4.6 %collective-permute-done = bf16[2,16,1024]{2,1,0:T(8,128)(2,1)S(1)} collective-permute-done((bf16[2,16,1024]{2,1,0:T(8,128)(2,1)S(1)}, bf16[2,16,1024]{2,1,0:T(8,128)(2,1)S(1)}, u32[]{:S(2)}, u32[]{:S(2)}) %collective-permute-start) | collective-permute-done | bytes 65568 | tf_op jit(solution)/shard_map/ppermute | solution.py:27
  26.2 11.5 %all_to_all.20 = bf16[4,2,16,1024]{3,2,1,0:T(8,128)(2,1)S(1)} all-to-all(bf16[4,2,16,1024]{3,2,1,0:T(8,128)(2,1)S(1)} %broadcast_in_dim.14), channel_id=1, replica_groups={{0,32,64,96},{4,36,68,100},{8,40,72,104},{12,44,76,108},{16,48,80,112},..., dimensions={0} | all-to-all | bytes 524288 | tf_op jit(solution)/shard_map/all_to_all | solution.py:41
  37.7 1.7 broadcast_in_dim.15
  39.4 6.3 %all-to-all-start.1 = ((bf16[8,4,2,16,1024]{4,3,2,1,0:T(8,128)(2,1)}), bf16[8,4,2,16,1024]{4,3,2,1,0:T(8,128)(2,1)}, u32[]{:S(2)}, u32[]{:S(2)}) async-start(bf16[8,4,2,16,1024]{4,3,2,1,0:T(8,128)(2,1)} %broadcast_in_dim.15), calls=%async_computation.1 | async-start | bytes 4194304 | tf_op jit(solution)/shard_map/all_to_all | solution.py:41
  45.7 1.9 %collective-permute-start.1 = (bf16[384,1024]{1,0:T(8,128)(2,1)S(1)}, bf16[384,1024]{1,0:T(8,128)(2,1)}, u32[]{:S(2)}, u32[]{:S(2)}) collective-permute-start(bf16[384,1024]{1,0:T(8,128)(2,1)S(1)} %pad_maximum_fusion), channel_id=1, source_target_pairs={{0,1},{1,0},{2,3},{3,2},{4,5},{5,4},{6,7},{7,6},{8,9},{9,8},{10,11... | collective-permute-start | bytes 2359304 | tf_op jit(solution)/shard_map/ppermute | solution.py:31
  47.7 13.3 %collective-permute-start.7 = (bf16[128,1024]{1,0:T(8,128)(2,1)S(1)}, bf16[128,1024]{1,0:T(8,128)(2,1)S(1)}, u32[]{:S(2)}, u32[]{:S(2)}) collective-permute-start(bf16[128,1024]{1,0:T(8,128)(2,1)S(1)} %bitcast.34), channel_id=1, source_target_pairs={{0,2},{1,3},{2,0},{3,1},{4,6},{5,7},{6,4},{7,5},{8,10},{9,11},{10,... | collective-permute-start | bytes 786440 | tf_op jit(solution)/shard_map/ppermute | solution.py:27
  60.9 1.9 %collective-permute-start.5 = (bf16[128,1024]{1,0:T(8,128)(2,1)S(1)}, bf16[128,1024]{1,0:T(8,128)(2,1)S(1)}, u32[]{:S(2)}, u32[]{:S(2)}) collective-permute-start(bf16[128,1024]{1,0:T(8,128)(2,1)S(1)} %bitcast.43), channel_id=1, source_target_pairs={{0,2},{1,3},{2,0},{3,1},{4,6},{5,7},{6,4},{7,5},{8,10},{9,11},{10,... | collective-permute-start | bytes 786440 | tf_op jit(solution)/shard_map/ppermute | solution.py:27
  62.9 11.1 %collective-permute-done.7.far = bf16[128,1024]{1,0:T(8,128)(2,1)S(1)} collective-permute-done((bf16[128,1024]{1,0:T(8,128)(2,1)S(1)}, bf16[128,1024]{1,0:T(8,128)(2,1)S(1)}, u32[]{:S(2)}, u32[]{:S(2)}) %collective-permute-start.7) | collective-permute-done | bytes 262176 | tf_op jit(solution)/shard_map/ppermute | solution.py:27
  73.9 1.9 %collective-permute-start.8 = (bf16[128,1024]{1,0:T(8,128)(2,1)S(1)}, bf16[128,1024]{1,0:T(8,128)(2,1)S(1)}, u32[]{:S(2)}, u32[]{:S(2)}) collective-permute-start(bf16[128,1024]{1,0:T(8,128)(2,1)S(1)} %collective-permute-done.7.far), channel_id=1, source_target_pairs={{0,1},{1,0},{2,3},{3,2},{4,5},{5,4},{6,7},{7,6},{8,9},{9,8},{10,11... | collective-permute-start | bytes 786440 | tf_op jit(solution)/shard_map/ppermute | solution.py:31
  75.8 10.5 %collective-permute-done.5.far = bf16[128,1024]{1,0:T(8,128)(2,1)S(1)} collective-permute-done((bf16[128,1024]{1,0:T(8,128)(2,1)S(1)}, bf16[128,1024]{1,0:T(8,128)(2,1)S(1)}, u32[]{:S(2)}, u32[]{:S(2)}) %collective-permute-start.5) | collective-permute-done | bytes 262176 | tf_op jit(solution)/shard_map/ppermute | solution.py:27
  86.4 1.9 %collective-permute-start.6 = (bf16[128,1024]{1,0:T(8,128)(2,1)S(1)}, bf16[128,1024]{1,0:T(8,128)(2,1)S(1)}, u32[]{:S(2)}, u32[]{:S(2)}) collective-permute-start(bf16[128,1024]{1,0:T(8,128)(2,1)S(1)} %collective-permute-done.5.far), channel_id=1, source_target_pairs={{0,1},{1,0},{2,3},{3,2},{4,5},{5,4},{6,7},{7,6},{8,9},{9,8},{10,11... | collective-permute-start | bytes 786440 | tf_op jit(solution)/shard_map/ppermute | solution.py:31
  88.3 0.7 copy-done.10
  89.0 4.3 %shard_map.96 = (bf16[1024,256]{1,0:T(8,128)(2,1)}, bf16[256,512]{1,0:T(8,128)(2,1)}, f32[256,512]{1,0:T(8,128)}) custom-call(bf16[128,1024]{1,0:T(8,128)(2,1)} %copy-done.9, bf16[128,1024]{1,0:T(8,128)(2,1)} %copy-done.10, bf16[512,1024]{1,0:T(8,128)(2,1)} %bitcast.37, f32[1,1024]{1,0:T(1,128)} %gain.3), custom_call_target="tpu_custom_call" | custom-call | flops 268435456 | bytes 4194304 | tf_op jit(solution)/shard_map/pallas_call | solution.py:265
  93.3 10.0 %shard_map.93 = (bf16[256,1024]{1,0:T(8,128)(2,1)}, bf16[256,1024]{1,0:T(8,128)(2,1)}, bf16[256,1024]{1,0:T(8,128)(2,1)}, f32[256,1024]{1,0:T(8,128)}, f32[256,1024]{1,0:T(8,128)}, /*index=5*/f32[1024,1024]{1,0:T(8,128)}) custom-call(bf16[128,1024]{1,0:T(8,128)(2,1)} %bitcast.39, bf16[128,1024]{1,0:T(8,128)(2,1)} %bitcast.32, bf16[128,1024]{1,0:T(8,128)(2,1)} %bitcast.41, ...), custom_call_target="tpu_custom_call" | custom-call | flops 1879048192 | bytes 11534336 | tf_op jit(solution)/shard_map/pallas_call | solution.py:238
  103.2 0.7 copy-done.8
  103.9 5.7 %shard_map.97 = bf16[8,4,32,1024]{3,2,1,0:T(8,128)(2,1)} custom-call(bf16[128,1024]{1,0:T(8,128)(2,1)} %copy-done.7, bf16[128,1024]{1,0:T(8,128)(2,1)} %copy-done.8, bf16[512,1024]{1,0:T(8,128)(2,1)} %bitcast.36, bf16[1024,256]{1,0:T(8,128)(2,1)} %get-tuple-element.28.nbt, bf16[256,512]{1,0:T(8,128)(2,1)} %get-tuple-element.29.act, ...), custom_call_target="tpu_custom_call" | custom-call | flops 805306368 | bytes 9437184 | tf_op jit(solution)/shard_map/pallas_call | solution.py:274
  109.7 5.7 %all-to-all-start.2 = ((bf16[8,4,32,1024]{3,2,1,0:T(8,128)(2,1)}), bf16[8,4,32,1024]{3,2,1,0:T(8,128)(2,1)S(1)}, u32[]{:S(2)}, u32[]{:S(2)}) async-start(bf16[8,4,32,1024]{3,2,1,0:T(8,128)(2,1)} %shard_map.97), calls=%async_computation.2 | async-start | bytes 4194304 | tf_op jit(solution)/shard_map/all_to_all | solution.py:45
  115.4 6.8 %shard_map.94 = (f32[2,128,1024]{2,1,0:T(8,128)}, bf16[2,128,1024]{2,1,0:T(8,128)(2,1)}) custom-call(bf16[32,2,16,1024]{3,2,1,0:T(8,128)(2,1)} %bitcast.1.whole, bf16[256,1024]{1,0:T(8,128)(2,1)} %get-tuple-element.19.nf, bf16[256,1024]{1,0:T(8,128)(2,1)} %get-tuple-element.20.nb, bf16[256,1024]{1,0:T(8,128)(2,1)} %get-tuple-element.21.c2, ...), custom_call_target="tpu_custom_call" | custom-call | flops 1342177280 | bytes 8388608 | tf_op jit(solution)/shard_map/pallas_call | solution.py:247
  122.2 2.0 %collective-permute-start.2 = (bf16[2,128,1024]{2,1,0:T(8,128)(2,1)}, bf16[2,128,1024]{2,1,0:T(8,128)(2,1)}, u32[]{:S(2)}, u32[]{:S(2)}) collective-permute-start(bf16[2,128,1024]{2,1,0:T(8,128)(2,1)} %get-tuple-element.25), channel_id=1, source_target_pairs={{0,1},{1,0},{2,3},{3,2},{4,5},{5,4},{6,7},{7,6},{8,9},{9,8},{10,11... | collective-permute-start | bytes 1572872 | tf_op jit(solution)/shard_map/ppermute | solution.py:31
  124.2 17.3 %all-to-all-done.2.pieces = bf16[8,4,32,1024]{3,2,1,0:T(8,128)(2,1)S(1)} async-done(((bf16[8,4,32,1024]{3,2,1,0:T(8,128)(2,1)}), bf16[8,4,32,1024]{3,2,1,0:T(8,128)(2,1)S(1)}, u32[]{:S(2)}, u32[]{:S(2)}) %all-to-all-start.2) | async-done | bytes 2097184 | tf_op jit(solution)/shard_map/all_to_all | solution.py:45
  141.5 1.0 shard_map.98
  142.5 9.1 %all-to-all-start.3 = ((bf16[4,32,1024]{2,1,0:T(8,128)(2,1)}), bf16[4,32,1024]{2,1,0:T(8,128)(2,1)S(1)}, u32[]{:S(2)}, u32[]{:S(2)}) async-start(bf16[4,32,1024]{2,1,0:T(8,128)(2,1)} %shard_map.98), calls=%async_computation.3 | async-start | bytes 524288 | tf_op jit(solution)/shard_map/all_to_all | solution.py:45
  151.7 1.2 convert_add_fusion
  153.4 21.3 %collective-permute-start.3 = (bf16[128,1024]{1,0:T(8,128)(2,1)S(1)}, bf16[128,1024]{1,0:T(8,128)(2,1)S(1)}, u32[]{:S(2)}, u32[]{:S(2)}) collective-permute-start(bf16[128,1024]{1,0:T(8,128)(2,1)S(1)} %get-tuple-element.37), channel_id=1, source_target_pairs={{0,128},{128,256},{256,384},{384,512},{512,640},{640,768},{768,896... | collective-permute-start | bytes 786440 | tf_op jit(solution)/shard_map/ppermute | solution.py:36
  174.7 1.9 %collective-permute-start.4 = (bf16[128,1024]{1,0:T(8,128)(2,1)S(1)}, bf16[128,1024]{1,0:T(8,128)(2,1)S(1)}, u32[]{:S(2)}, u32[]{:S(2)}) collective-permute-start(bf16[128,1024]{1,0:T(8,128)(2,1)S(1)} %get-tuple-element.36), channel_id=1, source_target_pairs={{0,896},{128,0},{256,128},{384,256},{512,384},{640,512},{768,640},... | collective-permute-start | bytes 786440 | tf_op jit(solution)/shard_map/ppermute | solution.py:36
  176.6 0.7 shard_map.99
  177.3 4.1 %collective-permute-done.3.a = bf16[128,1024]{1,0:T(8,128)(2,1)S(1)} collective-permute-done((bf16[128,1024]{1,0:T(8,128)(2,1)S(1)}, bf16[128,1024]{1,0:T(8,128)(2,1)S(1)}, u32[]{:S(2)}, u32[]{:S(2)}) %collective-permute-start.3) | collective-permute-done | bytes 262176 | tf_op jit(solution)/shard_map/ppermute | solution.py:36
  181.4 4.1 %collective-permute-done.4.b = bf16[128,1024]{1,0:T(8,128)(2,1)S(1)} collective-permute-done((bf16[128,1024]{1,0:T(8,128)(2,1)S(1)}, bf16[128,1024]{1,0:T(8,128)(2,1)S(1)}, u32[]{:S(2)}, u32[]{:S(2)}) %collective-permute-start.4) | collective-permute-done | bytes 262176 | tf_op jit(solution)/shard_map/ppermute | solution.py:36
  185.5 0.8 shard_map.95
  (34 shorter events, 0.6 us)
Async XLA Ops:
  2.2 23.9 %collective-permute-start = (bf16[2,16,1024]{2,1,0:T(8,128)(2,1)S(1)}, bf16[2,16,1024]{2,1,0:T(8,128)(2,1)S(1)}, u32[]{:S(2)}, u32[]{:S(2)}) collective-permute-start(bf16[2,16,1024]{2,1,0:T(8,128)(2,1)S(1)} %pad_maximum_fusion.1), channel_id=1, source_target_pairs={{0,2},{1,3},{2,0},{3,1},{4,6},{5,7},{6,4},{7,5},{8,10},{9,11},{10,... | collective-permute-start | bytes 196616 | tf_op jit(solution)/shard_map/ppermute | solution.py:27
  39.4 6.3 %copy-start = (bf16[1,128,1024]{2,1,0:T(8,128)(2,1)S(1)}, bf16[1,128,1024]{2,1,0:T(8,128)(2,1)}, u32[]{:S(2)}) copy-start(bf16[1,128,1024]{2,1,0:T(8,128)(2,1)} %param.7) | copy-start | bytes 786436
  39.4 6.3 %copy-start.3 = (bf16[1,128,1024]{2,1,0:T(8,128)(2,1)S(1)}, bf16[1,128,1024]{2,1,0:T(8,128)(2,1)}, u32[]{:S(2)}) copy-start(bf16[1,128,1024]{2,1,0:T(8,128)(2,1)} %param.6) | copy-start | bytes 786436
  39.4 6.3 %copy-start.5 = (bf16[1,128,1024]{2,1,0:T(8,128)(2,1)S(1)}, bf16[1,128,1024]{2,1,0:T(8,128)(2,1)}, u32[]{:S(2)}) copy-start(bf16[1,128,1024]{2,1,0:T(8,128)(2,1)} %param.8) | copy-start | bytes 786436
  39.4 70.3 %all-to-all-start.1 = ((bf16[8,4,2,16,1024]{4,3,2,1,0:T(8,128)(2,1)}), bf16[8,4,2,16,1024]{4,3,2,1,0:T(8,128)(2,1)}, u32[]{:S(2)}, u32[]{:S(2)}) async-start(bf16[8,4,2,16,1024]{4,3,2,1,0:T(8,128)(2,1)} %broadcast_in_dim.15), calls=%async_computation.1 | async-start | bytes 4194304 | tf_op jit(solution)/shard_map/all_to_all | solution.py:41
  45.7 47.5 %collective-permute-start.1 = (bf16[384,1024]{1,0:T(8,128)(2,1)S(1)}, bf16[384,1024]{1,0:T(8,128)(2,1)}, u32[]{:S(2)}, u32[]{:S(2)}) collective-permute-start(bf16[384,1024]{1,0:T(8,128)(2,1)S(1)} %pad_maximum_fusion), channel_id=1, source_target_pairs={{0,1},{1,0},{2,3},{3,2},{4,5},{5,4},{6,7},{7,6},{8,9},{9,8},{10,11... | collective-permute-start | bytes 2359304 | tf_op jit(solution)/shard_map/ppermute | solution.py:31
  47.7 26.3 %collective-permute-start.7 = (bf16[128,1024]{1,0:T(8,128)(2,1)S(1)}, bf16[128,1024]{1,0:T(8,128)(2,1)S(1)}, u32[]{:S(2)}, u32[]{:S(2)}) collective-permute-start(bf16[128,1024]{1,0:T(8,128)(2,1)S(1)} %bitcast.34), channel_id=1, source_target_pairs={{0,2},{1,3},{2,0},{3,1},{4,6},{5,7},{6,4},{7,5},{8,10},{9,11},{10,... | collective-permute-start | bytes 786440 | tf_op jit(solution)/shard_map/ppermute | solution.py:27
  60.9 25.4 %collective-permute-start.5 = (bf16[128,1024]{1,0:T(8,128)(2,1)S(1)}, bf16[128,1024]{1,0:T(8,128)(2,1)S(1)}, u32[]{:S(2)}, u32[]{:S(2)}) collective-permute-start(bf16[128,1024]{1,0:T(8,128)(2,1)S(1)} %bitcast.43), channel_id=1, source_target_pairs={{0,2},{1,3},{2,0},{3,1},{4,6},{5,7},{6,4},{7,5},{8,10},{9,11},{10,... | collective-permute-start | bytes 786440 | tf_op jit(solution)/shard_map/ppermute | solution.py:27
  73.9 14.4 %copy-start.9 = (bf16[128,1024]{1,0:T(8,128)(2,1)}, bf16[128,1024]{1,0:T(8,128)(2,1)S(1)}, u32[]{:S(2)}) copy-start(bf16[128,1024]{1,0:T(8,128)(2,1)S(1)} %collective-permute-done.7.far) | copy-start | bytes 786436
  73.9 14.4 %collective-permute-start.8 = (bf16[128,1024]{1,0:T(8,128)(2,1)S(1)}, bf16[128,1024]{1,0:T(8,128)(2,1)S(1)}, u32[]{:S(2)}, u32[]{:S(2)}) collective-permute-start(bf16[128,1024]{1,0:T(8,128)(2,1)S(1)} %collective-permute-done.7.far), channel_id=1, source_target_pairs={{0,1},{1,0},{2,3},{3,2},{4,5},{5,4},{6,7},{7,6},{8,9},{9,8},{10,11... | collective-permute-start | bytes 786440 | tf_op jit(solution)/shard_map/ppermute | solution.py:31
  86.4 16.9 %copy-start.7 = (bf16[128,1024]{1,0:T(8,128)(2,1)}, bf16[128,1024]{1,0:T(8,128)(2,1)S(1)}, u32[]{:S(2)}) copy-start(bf16[128,1024]{1,0:T(8,128)(2,1)S(1)} %collective-permute-done.5.far) | copy-start | bytes 786436
  86.4 16.9 %collective-permute-start.6 = (bf16[128,1024]{1,0:T(8,128)(2,1)S(1)}, bf16[128,1024]{1,0:T(8,128)(2,1)S(1)}, u32[]{:S(2)}, u32[]{:S(2)}) collective-permute-start(bf16[128,1024]{1,0:T(8,128)(2,1)S(1)} %collective-permute-done.5.far), channel_id=1, source_target_pairs={{0,1},{1,0},{2,3},{3,2},{4,5},{5,4},{6,7},{7,6},{8,9},{9,8},{10,11... | collective-permute-start | bytes 786440 | tf_op jit(solution)/shard_map/ppermute | solution.py:31
  88.3 0.7 copy-start.10
  103.2 0.7 copy-start.8
  109.7 31.9 %all-to-all-start.2 = ((bf16[8,4,32,1024]{3,2,1,0:T(8,128)(2,1)}), bf16[8,4,32,1024]{3,2,1,0:T(8,128)(2,1)S(1)}, u32[]{:S(2)}, u32[]{:S(2)}) async-start(bf16[8,4,32,1024]{3,2,1,0:T(8,128)(2,1)} %shard_map.97), calls=%async_computation.2 | async-start | bytes 4194304 | tf_op jit(solution)/shard_map/all_to_all | solution.py:45
  122.2 29.5 %copy-start.2 = (f32[2,128,1024]{2,1,0:T(8,128)S(1)}, f32[2,128,1024]{2,1,0:T(8,128)}, u32[]{:S(2)}) copy-start(f32[2,128,1024]{2,1,0:T(8,128)} %get-tuple-element.24) | copy-start | bytes 3145732
  122.2 29.5 %collective-permute-start.2 = (bf16[2,128,1024]{2,1,0:T(8,128)(2,1)}, bf16[2,128,1024]{2,1,0:T(8,128)(2,1)}, u32[]{:S(2)}, u32[]{:S(2)}) collective-permute-start(bf16[2,128,1024]{2,1,0:T(8,128)(2,1)} %get-tuple-element.25), channel_id=1, source_target_pairs={{0,1},{1,0},{2,3},{3,2},{4,5},{5,4},{6,7},{7,6},{8,9},{9,8},{10,11... | collective-permute-start | bytes 1572872 | tf_op jit(solution)/shard_map/ppermute | solution.py:31
  142.5 10.4 %copy-start.1 = (bf16[1,128,1024]{2,1,0:T(8,128)(2,1)S(1)}, bf16[1,128,1024]{2,1,0:T(8,128)(2,1)}, u32[]{:S(2)}) copy-start(bf16[1,128,1024]{2,1,0:T(8,128)(2,1)} %param.7) | copy-start | bytes 786436
  142.5 10.4 %copy-start.11 = (f32[1,1024]{1,0:T(1,128)S(1)}, f32[1,1024]{1,0:T(1,128)}, u32[]{:S(2)}) copy-start(f32[1,1024]{1,0:T(1,128)} %gain.3) | copy-start | bytes 12292
  142.5 10.6 %copy-start.4 = (bf16[1,128,1024]{2,1,0:T(8,128)(2,1)S(1)}, bf16[1,128,1024]{2,1,0:T(8,128)(2,1)}, u32[]{:S(2)}) copy-start(bf16[1,128,1024]{2,1,0:T(8,128)(2,1)} %param.6) | copy-start | bytes 786436
  142.5 10.6 %copy-start.6 = (bf16[1,128,1024]{2,1,0:T(8,128)(2,1)S(1)}, bf16[1,128,1024]{2,1,0:T(8,128)(2,1)}, u32[]{:S(2)}) copy-start(bf16[1,128,1024]{2,1,0:T(8,128)(2,1)} %param.8) | copy-start | bytes 786436
  142.5 34.1 %all-to-all-start.3 = ((bf16[4,32,1024]{2,1,0:T(8,128)(2,1)}), bf16[4,32,1024]{2,1,0:T(8,128)(2,1)S(1)}, u32[]{:S(2)}, u32[]{:S(2)}) async-start(bf16[4,32,1024]{2,1,0:T(8,128)(2,1)} %shard_map.98), calls=%async_computation.3 | async-start | bytes 524288 | tf_op jit(solution)/shard_map/all_to_all | solution.py:45
  153.4 28.0 %collective-permute-start.3 = (bf16[128,1024]{1,0:T(8,128)(2,1)S(1)}, bf16[128,1024]{1,0:T(8,128)(2,1)S(1)}, u32[]{:S(2)}, u32[]{:S(2)}) collective-permute-start(bf16[128,1024]{1,0:T(8,128)(2,1)S(1)} %get-tuple-element.37), channel_id=1, source_target_pairs={{0,128},{128,256},{256,384},{384,512},{512,640},{640,768},{768,896... | collective-permute-start | bytes 786440 | tf_op jit(solution)/shard_map/ppermute | solution.py:36
  174.7 10.8 %collective-permute-start.4 = (bf16[128,1024]{1,0:T(8,128)(2,1)S(1)}, bf16[128,1024]{1,0:T(8,128)(2,1)S(1)}, u32[]{:S(2)}, u32[]{:S(2)}) collective-permute-start(bf16[128,1024]{1,0:T(8,128)(2,1)S(1)} %get-tuple-element.36), channel_id=1, source_target_pairs={{0,896},{128,0},{256,128},{384,256},{512,384},{640,512},{768,640},... | collective-permute-start | bytes 786440 | tf_op jit(solution)/shard_map/ppermute | solution.py:36

commit v7 on v6

--- a/solution.py
+++ b/solution.py
@@ -69,42 +69,66 @@
 
 
 def norm_into(src, at, gain, dst, to, rows):
-    def step(i, _):
-        r = pl.multiple_of(i * CHUNK, CHUNK)
-        x = src[pl.ds(at + r, CHUNK), :].astype(f32)
-        dst[pl.ds(to + r, CHUNK), :] = (x * scale_of(x) * gain[...]).astype(bf16)
-
-    lax.fori_loop(0, rows // CHUNK, step, None)
-
-
-def own_kernel(xf, xb, ct, near, wi, wo, gain, nf, nb, c2, br, dn, p, act_f, act, dp):
-    rows = xf.shape[0]
+    for r in range(0, rows, CHUNK):
+        x = src[at + r : at + r + CHUNK, :].astype(f32)
+        dst[to + r : to + r + CHUNK, :] = (x * scale_of(x) * gain[...]).astype(bf16)
+
+
+def own_kernel(xb, ct, near, wi, wo, gain, nb, c2, dp, p, vwi, vwo, vp, act, arrived, sent):
+    rows = xb.shape[0]
     hid = wi.shape[0]
-    norm_into(xf, 0, gain, nf, 0, rows)
-    norm_into(near, 0, gain, nf, rows, rows)
+    loads = [
+        pltpu.make_async_copy(wi, vwi, arrived.at[0]),
+        pltpu.make_async_copy(wo, vwo, arrived.at[1]),
+    ]
+    for load in loads:
+        load.start()
     norm_into(xb, 0, gain, nb, 0, rows)
     norm_into(near, rows, gain, nb, rows, rows)
     c2[:rows, :] = ct[...]
     c2[rows:, :] = near[2 * rows :, :]
+    for load in loads:
+        load.wait()
+
+    def hidden(j, _):
+        h = pl.ds(pl.multiple_of(j * TILE, TILE), TILE)
+        value, slope = gelu_both(nt(nb[...], vwi[h, :]))
+        act[:, h] = value.astype(bf16)
+        dp[:, h] = (nt(c2[...], vwo[h, :]) * slope).astype(bf16)
+
+    lax.fori_loop(0, hid // TILE, hidden, None)
+    stores = []
+    for k in range(FAR):
+        c = slice(k * TILE, (k + 1) * TILE)
+        vp[c, :hid] = tn(nb[:, c], dp[...])
+        vp[c, hid:] = tn(c2[:, c], act[...])
+        store = pltpu.make_async_copy(vp.at[c], p.at[c], sent.at[k])
+        store.start()
+        stores.append(store)
+    for store in stores:
+        store.wait()
+
+
+def forward_kernel(xf, near, wi, wo, gain, nf, br, act):
+    rows = xf.shape[0]
+    norm_into(xf, 0, gain, nf, 0, rows)
+    norm_into(near, 0, gain, nf, rows, rows)
 
     def hidden(j, _):
         h = pl.ds(pl.multiple_of(j * TILE, TILE), TILE)
         value, _ = gelu_both(nt(nf[...], wi[h, :]))
-        act_f[:, h] = value.astype(bf16)
-        value, slope = gelu_both(nt(nb[...], wi[h, :]))
         act[:, h] = value.astype(bf16)
-        dp[:, h] = (nt(c2[...], wo[h, :]) * slope).astype(bf16)
 
     lax.fori_loop(0, wi.shape[0] // TILE, hidden, None)
-
+    times_kernel(act, wo, br)
+
+
+def times_kernel(a, w, total):
     def back(j, _):
         c = pl.ds(pl.multiple_of(j * TILE, TILE), TILE)
-        br[:, c] = nn(act_f[...], wo[:, c])
-        dn[:, c] = nn(dp[...], wi[:, c])
-        p[c, :hid] = tn(nb[:, c], dp[...])
-        p[c, hid:] = tn(c2[:, c], act[...])
-
-    lax.fori_loop(0, wi.shape[1] // TILE, back, None)
+        total[:, c] = nn(a[...], w[:, c])
+
+    lax.fori_loop(0, w.shape[1] // TILE, back, None)
 
 
 def rest_kernel(whole, nf, nb, c2, br, dn, keep, send, act_f, dp, wi, wo):
@@ -235,13 +259,30 @@
     far_s = to_chip(xb)
     far_c = to_chip(ct)
     near = to_core(jnp.concatenate([xf, xb, ct]))
-    nf, nb, c2, br, dn, p = local(
+    nb, c2, dp, p = local(
         own_kernel,
-        [((both, dim), bf16)] * 3 + [((both, dim), f32)] * 2 + [((dim, 2 * hid), f32)],
-        [((both, hid), bf16)] * 3,
-        14 * both * hid * dim,
-        11 * 2**20,
-    )(xf, xb, ct, near, wi, wo, gain)
+        [((both, dim), bf16)] * 2 + [((both, hid), bf16), ((dim, 2 * hid), f32)],
+        [
+            ((hid, dim), bf16),
+            ((hid, dim), bf16),
+            ((dim, 2 * hid), f32),
+            ((both, hid), bf16),
+            pltpu.SemaphoreType.DMA((2,)),
+            pltpu.SemaphoreType.DMA((FAR,)),
+        ],
+        8 * both * hid * dim,
+        9 * 2**20,
+        in_specs=[vmem] * 3 + [hbm, hbm, vmem],
+        out_specs=[vmem] * 3 + [hbm],
+    )(xb, ct, near, wi, wo, gain)
+    nf, br = local(
+        forward_kernel,
+        [((both, dim), bf16), ((both, dim), f32)],
+        [((both, hid), bf16)],
+        4 * both * hid * dim,
+        4 * 2**20,
+    )(xf, near, wi, wo, gain)
+    (dn,) = local(times_kernel, [((both, dim), f32)], [], 2 * both * hid * dim, 2**21)(dp, wi)
     col = gathered(piece, far_groups)
     whole = gathered(col, near_groups).reshape(n_dp, 2, part, dim)
     keep, send = local(

time: 187 us -> 185 us (0.989)
  waiting for transfers between devices: 51.6 us -> 43.7 us
  Pallas kernels: 29.2 us -> 35.7 us
    all_to_all x2, waiting for transfers between devices: 17.3 us -> 9.31 us  [exchanged(): return lax.all_to_all(x, 'dp', 0, 0, tiled=True, axis_index_groups=groups)]
    pallas_call x1 -> x3, Pallas kernels: 9.96 us -> 15.5 us  [the longest x1 7.43 us: layer(): local(own_kernel, [((both, dim), bf16)] * 2 + [((both, hid), bf16), ((dim...]
  transfers between devices with their start and end apart: 12 -> 12, of which waited for: 6 -> 6; matrix products, arithmetic and copies ran while one was open for 1% -> 0% of each run, Pallas kernels for 15% -> 19%
where the time goes in v7:
time: 185 us; the launch traced here: 184 us
  starting transfers between devices  86.6 us (47%)
  waiting for transfers between devices  43.7 us (24%)
  Pallas kernels  35.7 us (19%)
  blocking collectives  11.5 us (6%)
  local copies, waits for them, and re-layouts  4.61 us (2%)
    ppermute x3, starting transfers between devices, to_chip(): return lax.ppermute(x, 'mp', other_chip)  34.5 us
    ppermute x3, waiting for transfers between devices, to_chip(): return lax.ppermute(x, 'mp', other_chip)  26.2 us
    ppermute x2, starting transfers between devices, shifted(): lax.ppermute(x, axis, [(i, (i + by) % length) for i in range(length)])  23.2 us
    all_to_all x2, starting transfers between devices, exchanged(): return lax.all_to_all(x, 'dp', 0, 0, tiled=True, axis_index_groups=groups)  14.8 us
    all_to_all x1, blocking collectives, gathered(): lax.all_to_all(copies, 'dp', 0, 0, tiled=True, axis_index_groups=groups)  11.5 us
    all_to_all x2, waiting for transfers between devices, exchanged(): return lax.all_to_all(x, 'dp', 0, 0, tiled=True, axis_index_groups=groups)  9.31 us
    ppermute x2, waiting for transfers between devices, shifted(): lax.ppermute(x, axis, [(i, (i + by) % length) for i in range(length)])  8.17 us
    ppermute x4, starting transfers between devices, to_core(): return lax.ppermute(x, 'mp', other_core)  7.78 us
  transfers between devices with their start and end apart: 12, of which 6 were waited for; matrix products, arithmetic and copies ran while one was open for 0% of the time, Pallas kernels for 19%

profile of v7, /device:TPU:40, one launch (start us, length us, event | category | flops | bytes accessed | tf_op | source)
XLA Modules:
  0.0 183.7 jit_solution(5090379666765839734)
XLA Ops:
  0.7 0.8 constant_dynamic-slice_fusion
  1.4 0.8 constant_dynamic-slice_fusion.1
  2.2 19.4 %collective-permute-start = (bf16[2,16,1024]{2,1,0:T(8,128)(2,1)S(1)}, bf16[2,16,1024]{2,1,0:T(8,128)(2,1)S(1)}, u32[]{:S(2)}, u32[]{:S(2)}) collective-permute-start(bf16[2,16,1024]{2,1,0:T(8,128)(2,1)S(1)} %pad_maximum_fusion.1), channel_id=1, source_target_pairs={{0,2},{1,3},{2,0},{3,1},{4,6},{5,7},{6,4},{7,5},{8,10},{9,11},{10,... | collective-permute-start | bytes 196616 | tf_op jit(solution)/shard_map/ppermute | solution.py:27
  21.6 4.6 %collective-permute-done = bf16[2,16,1024]{2,1,0:T(8,128)(2,1)S(1)} collective-permute-done((bf16[2,16,1024]{2,1,0:T(8,128)(2,1)S(1)}, bf16[2,16,1024]{2,1,0:T(8,128)(2,1)S(1)}, u32[]{:S(2)}, u32[]{:S(2)}) %collective-permute-start) | collective-permute-done | bytes 65568 | tf_op jit(solution)/shard_map/ppermute | solution.py:27
  26.2 11.5 %all_to_all.20 = bf16[4,2,16,1024]{3,2,1,0:T(8,128)(2,1)S(1)} all-to-all(bf16[4,2,16,1024]{3,2,1,0:T(8,128)(2,1)S(1)} %broadcast_in_dim.14), channel_id=1, replica_groups={{0,32,64,96},{4,36,68,100},{8,40,72,104},{12,44,76,108},{16,48,80,112},..., dimensions={0} | all-to-all | bytes 524288 | tf_op jit(solution)/shard_map/all_to_all | solution.py:41
  37.7 1.6 broadcast_in_dim.15
  39.4 6.3 %all-to-all-start.1 = ((bf16[8,4,2,16,1024]{4,3,2,1,0:T(8,128)(2,1)}), bf16[8,4,2,16,1024]{4,3,2,1,0:T(8,128)(2,1)}, u32[]{:S(2)}, u32[]{:S(2)}) async-start(bf16[8,4,2,16,1024]{4,3,2,1,0:T(8,128)(2,1)} %broadcast_in_dim.15), calls=%async_computation.1 | async-start | bytes 4194304 | tf_op jit(solution)/shard_map/all_to_all | solution.py:41
  45.7 1.9 %collective-permute-start.1 = (bf16[384,1024]{1,0:T(8,128)(2,1)S(1)}, bf16[384,1024]{1,0:T(8,128)(2,1)}, u32[]{:S(2)}, u32[]{:S(2)}) collective-permute-start(bf16[384,1024]{1,0:T(8,128)(2,1)S(1)} %pad_maximum_fusion), channel_id=1, source_target_pairs={{0,1},{1,0},{2,3},{3,2},{4,5},{5,4},{6,7},{7,6},{8,9},{9,8},{10,11... | collective-permute-start | bytes 2359304 | tf_op jit(solution)/shard_map/ppermute | solution.py:31
  47.6 13.3 %collective-permute-start.7 = (bf16[128,1024]{1,0:T(8,128)(2,1)S(1)}, bf16[128,1024]{1,0:T(8,128)(2,1)S(1)}, u32[]{:S(2)}, u32[]{:S(2)}) collective-permute-start(bf16[128,1024]{1,0:T(8,128)(2,1)S(1)} %bitcast.43), channel_id=1, source_target_pairs={{0,2},{1,3},{2,0},{3,1},{4,6},{5,7},{6,4},{7,5},{8,10},{9,11},{10,... | collective-permute-start | bytes 786440 | tf_op jit(solution)/shard_map/ppermute | solution.py:27
  60.9 1.9 %collective-permute-start.5 = (bf16[128,1024]{1,0:T(8,128)(2,1)S(1)}, bf16[128,1024]{1,0:T(8,128)(2,1)S(1)}, u32[]{:S(2)}, u32[]{:S(2)}) collective-permute-start(bf16[128,1024]{1,0:T(8,128)(2,1)S(1)} %bitcast.46), channel_id=1, source_target_pairs={{0,2},{1,3},{2,0},{3,1},{4,6},{5,7},{6,4},{7,5},{8,10},{9,11},{10,... | collective-permute-start | bytes 786440 | tf_op jit(solution)/shard_map/ppermute | solution.py:27
  62.8 11.1 %collective-permute-done.7.far = bf16[128,1024]{1,0:T(8,128)(2,1)S(1)} collective-permute-done((bf16[128,1024]{1,0:T(8,128)(2,1)S(1)}, bf16[128,1024]{1,0:T(8,128)(2,1)S(1)}, u32[]{:S(2)}, u32[]{:S(2)}) %collective-permute-start.7) | collective-permute-done | bytes 262176 | tf_op jit(solution)/shard_map/ppermute | solution.py:27
  73.9 1.9 %collective-permute-start.8 = (bf16[128,1024]{1,0:T(8,128)(2,1)S(1)}, bf16[128,1024]{1,0:T(8,128)(2,1)S(1)}, u32[]{:S(2)}, u32[]{:S(2)}) collective-permute-start(bf16[128,1024]{1,0:T(8,128)(2,1)S(1)} %collective-permute-done.7.far), channel_id=1, source_target_pairs={{0,1},{1,0},{2,3},{3,2},{4,5},{5,4},{6,7},{7,6},{8,9},{9,8},{10,11... | collective-permute-start | bytes 786440 | tf_op jit(solution)/shard_map/ppermute | solution.py:31
  75.8 10.5 %collective-permute-done.5.far = bf16[128,1024]{1,0:T(8,128)(2,1)S(1)} collective-permute-done((bf16[128,1024]{1,0:T(8,128)(2,1)S(1)}, bf16[128,1024]{1,0:T(8,128)(2,1)S(1)}, u32[]{:S(2)}, u32[]{:S(2)}) %collective-permute-start.5) | collective-permute-done | bytes 262176 | tf_op jit(solution)/shard_map/ppermute | solution.py:27
  86.3 1.9 %collective-permute-start.6 = (bf16[128,1024]{1,0:T(8,128)(2,1)S(1)}, bf16[128,1024]{1,0:T(8,128)(2,1)S(1)}, u32[]{:S(2)}, u32[]{:S(2)}) collective-permute-start(bf16[128,1024]{1,0:T(8,128)(2,1)S(1)} %collective-permute-done.5.far), channel_id=1, source_target_pairs={{0,1},{1,0},{2,3},{3,2},{4,5},{5,4},{6,7},{7,6},{8,9},{9,8},{10,11... | collective-permute-start | bytes 786440 | tf_op jit(solution)/shard_map/ppermute | solution.py:31
  88.3 0.7 copy-done.10
  89.0 3.6 %shard_map.98 = (bf16[1024,256]{1,0:T(8,128)(2,1)}, bf16[256,512]{1,0:T(8,128)(2,1)}, f32[256,512]{1,0:T(8,128)}) custom-call(bf16[128,1024]{1,0:T(8,128)(2,1)} %copy-done.9, bf16[128,1024]{1,0:T(8,128)(2,1)} %copy-done.10, bf16[512,1024]{1,0:T(8,128)(2,1)} %bitcast.32, f32[1,1024]{1,0:T(1,128)} %gain.5), custom_call_target="tpu_custom_call" | custom-call | flops 268435456 | bytes 4194304 | tf_op jit(solution)/shard_map/pallas_call | solution.py:306
  92.6 7.4 %shard_map.94 = (bf16[256,1024]{1,0:T(8,128)(2,1)}, bf16[256,1024]{1,0:T(8,128)(2,1)}, bf16[256,512]{1,0:T(8,128)(2,1)}, f32[1024,1024]{1,0:T(8,128)}) custom-call(bf16[128,1024]{1,0:T(8,128)(2,1)} %bitcast.41, bf16[128,1024]{1,0:T(8,128)(2,1)} %bitcast.44, bf16[384,1024]{1,0:T(8,128)(2,1)} %collective-permute-done.1.near, bf16[512,1024]{1,0:T(8,128)(2,1)} %bitcast.33, ...), custom_call_target="tpu_custom_call" | custom-call | flops 1073741824 | bytes 9437184 | tf_op jit(solution)/shard_map/pallas_call | solution.py:262
  100.1 0.7 copy-done.8
  100.8 5.7 %shard_map.99 = bf16[8,4,32,1024]{3,2,1,0:T(8,128)(2,1)} custom-call(bf16[128,1024]{1,0:T(8,128)(2,1)} %copy-done.7, bf16[128,1024]{1,0:T(8,128)(2,1)} %copy-done.8, bf16[512,1024]{1,0:T(8,128)(2,1)} %bitcast.37, bf16[1024,256]{1,0:T(8,128)(2,1)} %get-tuple-element.28.nbt, bf16[256,512]{1,0:T(8,128)(2,1)} %get-tuple-element.29.act, ...), custom_call_target="tpu_custom_call" | custom-call | flops 805306368 | bytes 9437184 | tf_op jit(solution)/shard_map/pallas_call | solution.py:315
  106.5 5.7 %all-to-all-start.2 = ((bf16[8,4,32,1024]{3,2,1,0:T(8,128)(2,1)}), bf16[8,4,32,1024]{3,2,1,0:T(8,128)(2,1)}, u32[]{:S(2)}, u32[]{:S(2)}) async-start(bf16[8,4,32,1024]{3,2,1,0:T(8,128)(2,1)} %shard_map.99), calls=%async_computation.2 | async-start | bytes 4194304 | tf_op jit(solution)/shard_map/all_to_all | solution.py:45
  112.2 3.3 %shard_map.95.dn = f32[256,1024]{1,0:T(8,128)} custom-call(bf16[256,512]{1,0:T(8,128)(2,1)} %get-tuple-element.23.a, bf16[512,1024]{1,0:T(8,128)(2,1)} %bitcast.34), custom_call_target="tpu_custom_call" | custom-call | flops 268435456 | bytes 2097152 | tf_op jit(solution)/shard_map/pallas_call | solution.py:285
  115.5 4.7 %shard_map.93 = (bf16[256,1024]{1,0:T(8,128)(2,1)}, f32[256,1024]{1,0:T(8,128)}) custom-call(bf16[128,1024]{1,0:T(8,128)(2,1)} %bitcast.39, bf16[384,1024]{1,0:T(8,128)(2,1)} %collective-permute-done.1.near, bf16[512,1024]{1,0:T(8,128)(2,1)} %bitcast.35, bf16[512,1024]{1,0:T(8,128)(2,1)} %bitcast.38, f32[1,1024]{1,0:T(1,128)} %gain.5), custom_call_target="tpu_custom_call" | custom-call | flops 536870912 | bytes 4194304 | tf_op jit(solution)/shard_map/pallas_call | solution.py:278
  120.2 6.8 %shard_map.96 = (f32[2,128,1024]{2,1,0:T(8,128)}, bf16[2,128,1024]{2,1,0:T(8,128)(2,1)}) custom-call(bf16[32,2,16,1024]{3,2,1,0:T(8,128)(2,1)} %bitcast.1.whole, bf16[256,1024]{1,0:T(8,128)(2,1)} %get-tuple-element.19.nf, bf16[256,1024]{1,0:T(8,128)(2,1)} %get-tuple-element.20.nb, bf16[256,1024]{1,0:T(8,128)(2,1)} %get-tuple-element.21.c2, ...), custom_call_target="tpu_custom_call" | custom-call | flops 1342177280 | bytes 8388608 | tf_op jit(solution)/shard_map/pallas_call | solution.py:288
  127.1 2.0 %collective-permute-start.2 = (bf16[2,128,1024]{2,1,0:T(8,128)(2,1)}, bf16[2,128,1024]{2,1,0:T(8,128)(2,1)S(1)}, u32[]{:S(2)}, u32[]{:S(2)}) collective-permute-start(bf16[2,128,1024]{2,1,0:T(8,128)(2,1)} %get-tuple-element.25), channel_id=1, source_target_pairs={{0,1},{1,0},{2,3},{3,2},{4,5},{5,4},{6,7},{7,6},{8,9},{9,8},{10,11... | collective-permute-start | bytes 1572872 | tf_op jit(solution)/shard_map/ppermute | solution.py:31
  129.1 9.3 %all-to-all-done.2.pieces = bf16[8,4,32,1024]{3,2,1,0:T(8,128)(2,1)} async-done(((bf16[8,4,32,1024]{3,2,1,0:T(8,128)(2,1)}), bf16[8,4,32,1024]{3,2,1,0:T(8,128)(2,1)}, u32[]{:S(2)}, u32[]{:S(2)}) %all-to-all-start.2) | async-done | bytes 2097184 | tf_op jit(solution)/shard_map/all_to_all | solution.py:45
  138.4 2.6 %shard_map.100 = bf16[4,32,1024]{2,1,0:T(8,128)(2,1)} custom-call(bf16[8,4,32,1024]{3,2,1,0:T(8,128)(2,1)} %all-to-all-done.2.pieces), custom_call_target="tpu_custom_call" | custom-call | flops 2097152 | bytes 2097152 | tf_op jit(solution)/shard_map/pallas_call | solution.py:336
  141.0 9.1 %all-to-all-start.3 = ((bf16[4,32,1024]{2,1,0:T(8,128)(2,1)}), bf16[4,32,1024]{2,1,0:T(8,128)(2,1)S(1)}, u32[]{:S(2)}, u32[]{:S(2)}) async-start(bf16[4,32,1024]{2,1,0:T(8,128)(2,1)} %shard_map.100), calls=%async_computation.3 | async-start | bytes 524288 | tf_op jit(solution)/shard_map/all_to_all | solution.py:45
  150.9 21.3 %collective-permute-start.3 = (bf16[128,1024]{1,0:T(8,128)(2,1)S(1)}, bf16[128,1024]{1,0:T(8,128)(2,1)S(1)}, u32[]{:S(2)}, u32[]{:S(2)}) collective-permute-start(bf16[128,1024]{1,0:T(8,128)(2,1)S(1)} %get-tuple-element.37), channel_id=1, source_target_pairs={{0,128},{128,256},{256,384},{384,512},{512,640},{640,768},{768,896... | collective-permute-start | bytes 786440 | tf_op jit(solution)/shard_map/ppermute | solution.py:36
  172.1 1.9 %collective-permute-start.4 = (bf16[128,1024]{1,0:T(8,128)(2,1)S(1)}, bf16[128,1024]{1,0:T(8,128)(2,1)S(1)}, u32[]{:S(2)}, u32[]{:S(2)}) collective-permute-start(bf16[128,1024]{1,0:T(8,128)(2,1)S(1)} %get-tuple-element.36), channel_id=1, source_target_pairs={{0,896},{128,0},{256,128},{384,256},{512,384},{640,512},{768,640},... | collective-permute-start | bytes 786440 | tf_op jit(solution)/shard_map/ppermute | solution.py:36
  174.7 4.1 %collective-permute-done.3.a = bf16[128,1024]{1,0:T(8,128)(2,1)S(1)} collective-permute-done((bf16[128,1024]{1,0:T(8,128)(2,1)S(1)}, bf16[128,1024]{1,0:T(8,128)(2,1)S(1)}, u32[]{:S(2)}, u32[]{:S(2)}) %collective-permute-start.3) | collective-permute-done | bytes 262176 | tf_op jit(solution)/shard_map/ppermute | solution.py:36
  178.8 4.1 %collective-permute-done.4.b = bf16[128,1024]{1,0:T(8,128)(2,1)S(1)} collective-permute-done((bf16[128,1024]{1,0:T(8,128)(2,1)S(1)}, bf16[128,1024]{1,0:T(8,128)(2,1)S(1)}, u32[]{:S(2)}, u32[]{:S(2)}) %collective-permute-start.4) | collective-permute-done | bytes 262176 | tf_op jit(solution)/shard_map/ppermute | solution.py:36
  182.9 0.8 shard_map.97
  (36 shorter events, 1.4 us)
Async XLA Ops:
  2.2 23.9 %collective-permute-start = (bf16[2,16,1024]{2,1,0:T(8,128)(2,1)S(1)}, bf16[2,16,1024]{2,1,0:T(8,128)(2,1)S(1)}, u32[]{:S(2)}, u32[]{:S(2)}) collective-permute-start(bf16[2,16,1024]{2,1,0:T(8,128)(2,1)S(1)} %pad_maximum_fusion.1), channel_id=1, source_target_pairs={{0,2},{1,3},{2,0},{3,1},{4,6},{5,7},{6,4},{7,5},{8,10},{9,11},{10,... | collective-permute-start | bytes 196616 | tf_op jit(solution)/shard_map/ppermute | solution.py:27
  39.4 6.3 %copy-start = (bf16[1,128,1024]{2,1,0:T(8,128)(2,1)S(1)}, bf16[1,128,1024]{2,1,0:T(8,128)(2,1)}, u32[]{:S(2)}) copy-start(bf16[1,128,1024]{2,1,0:T(8,128)(2,1)} %param.6) | copy-start | bytes 786436
  39.4 6.3 %copy-start.2 = (bf16[1,128,1024]{2,1,0:T(8,128)(2,1)S(1)}, bf16[1,128,1024]{2,1,0:T(8,128)(2,1)}, u32[]{:S(2)}) copy-start(bf16[1,128,1024]{2,1,0:T(8,128)(2,1)} %param.7) | copy-start | bytes 786436
  39.4 6.3 %copy-start.5 = (bf16[1,128,1024]{2,1,0:T(8,128)(2,1)S(1)}, bf16[1,128,1024]{2,1,0:T(8,128)(2,1)}, u32[]{:S(2)}) copy-start(bf16[1,128,1024]{2,1,0:T(8,128)(2,1)} %param.8) | copy-start | bytes 786436
  39.4 67.1 %all-to-all-start.1 = ((bf16[8,4,2,16,1024]{4,3,2,1,0:T(8,128)(2,1)}), bf16[8,4,2,16,1024]{4,3,2,1,0:T(8,128)(2,1)}, u32[]{:S(2)}, u32[]{:S(2)}) async-start(bf16[8,4,2,16,1024]{4,3,2,1,0:T(8,128)(2,1)} %broadcast_in_dim.15), calls=%async_computation.1 | async-start | bytes 4194304 | tf_op jit(solution)/shard_map/all_to_all | solution.py:41
  45.7 46.9 %collective-permute-start.1 = (bf16[384,1024]{1,0:T(8,128)(2,1)S(1)}, bf16[384,1024]{1,0:T(8,128)(2,1)}, u32[]{:S(2)}, u32[]{:S(2)}) collective-permute-start(bf16[384,1024]{1,0:T(8,128)(2,1)S(1)} %pad_maximum_fusion), channel_id=1, source_target_pairs={{0,1},{1,0},{2,3},{3,2},{4,5},{5,4},{6,7},{7,6},{8,9},{9,8},{10,11... | collective-permute-start | bytes 2359304 | tf_op jit(solution)/shard_map/ppermute | solution.py:31
  47.6 26.3 %collective-permute-start.7 = (bf16[128,1024]{1,0:T(8,128)(2,1)S(1)}, bf16[128,1024]{1,0:T(8,128)(2,1)S(1)}, u32[]{:S(2)}, u32[]{:S(2)}) collective-permute-start(bf16[128,1024]{1,0:T(8,128)(2,1)S(1)} %bitcast.43), channel_id=1, source_target_pairs={{0,2},{1,3},{2,0},{3,1},{4,6},{5,7},{6,4},{7,5},{8,10},{9,11},{10,... | collective-permute-start | bytes 786440 | tf_op jit(solution)/shard_map/ppermute | solution.py:27
  60.9 25.4 %collective-permute-start.5 = (bf16[128,1024]{1,0:T(8,128)(2,1)S(1)}, bf16[128,1024]{1,0:T(8,128)(2,1)S(1)}, u32[]{:S(2)}, u32[]{:S(2)}) collective-permute-start(bf16[128,1024]{1,0:T(8,128)(2,1)S(1)} %bitcast.46), channel_id=1, source_target_pairs={{0,2},{1,3},{2,0},{3,1},{4,6},{5,7},{6,4},{7,5},{8,10},{9,11},{10,... | collective-permute-start | bytes 786440 | tf_op jit(solution)/shard_map/ppermute | solution.py:27
  73.9 15.1 %copy-start.9 = (bf16[128,1024]{1,0:T(8,128)(2,1)}, bf16[128,1024]{1,0:T(8,128)(2,1)S(1)}, u32[]{:S(2)}) copy-start(bf16[128,1024]{1,0:T(8,128)(2,1)S(1)} %collective-permute-done.7.far) | copy-start | bytes 786436
  73.9 14.4 %collective-permute-start.8 = (bf16[128,1024]{1,0:T(8,128)(2,1)S(1)}, bf16[128,1024]{1,0:T(8,128)(2,1)S(1)}, u32[]{:S(2)}, u32[]{:S(2)}) collective-permute-start(bf16[128,1024]{1,0:T(8,128)(2,1)S(1)} %collective-permute-done.7.far), channel_id=1, source_target_pairs={{0,1},{1,0},{2,3},{3,2},{4,5},{5,4},{6,7},{7,6},{8,9},{9,8},{10,11... | collective-permute-start | bytes 786440 | tf_op jit(solution)/shard_map/ppermute | solution.py:31
  86.3 13.7 %copy-start.7 = (bf16[128,1024]{1,0:T(8,128)(2,1)}, bf16[128,1024]{1,0:T(8,128)(2,1)S(1)}, u32[]{:S(2)}) copy-start(bf16[128,1024]{1,0:T(8,128)(2,1)S(1)} %collective-permute-done.5.far) | copy-start | bytes 786436
  86.3 13.7 %collective-permute-start.6 = (bf16[128,1024]{1,0:T(8,128)(2,1)S(1)}, bf16[128,1024]{1,0:T(8,128)(2,1)S(1)}, u32[]{:S(2)}, u32[]{:S(2)}) collective-permute-start(bf16[128,1024]{1,0:T(8,128)(2,1)S(1)} %collective-permute-done.5.far), channel_id=1, source_target_pairs={{0,1},{1,0},{2,3},{3,2},{4,5},{5,4},{6,7},{7,6},{8,9},{9,8},{10,11... | collective-permute-start | bytes 786440 | tf_op jit(solution)/shard_map/ppermute | solution.py:31
  88.3 0.7 copy-start.10
  100.1 0.7 copy-start.8
  106.5 31.9 %all-to-all-start.2 = ((bf16[8,4,32,1024]{3,2,1,0:T(8,128)(2,1)}), bf16[8,4,32,1024]{3,2,1,0:T(8,128)(2,1)}, u32[]{:S(2)}, u32[]{:S(2)}) async-start(bf16[8,4,32,1024]{3,2,1,0:T(8,128)(2,1)} %shard_map.99), calls=%async_computation.2 | async-start | bytes 4194304 | tf_op jit(solution)/shard_map/all_to_all | solution.py:45
  127.1 23.1 %copy-start.4 = (f32[2,128,1024]{2,1,0:T(8,128)S(1)}, f32[2,128,1024]{2,1,0:T(8,128)}, u32[]{:S(2)}) copy-start(f32[2,128,1024]{2,1,0:T(8,128)} %get-tuple-element.24) | copy-start | bytes 3145732
  127.1 23.1 %collective-permute-start.2 = (bf16[2,128,1024]{2,1,0:T(8,128)(2,1)}, bf16[2,128,1024]{2,1,0:T(8,128)(2,1)S(1)}, u32[]{:S(2)}, u32[]{:S(2)}) collective-permute-start(bf16[2,128,1024]{2,1,0:T(8,128)(2,1)} %get-tuple-element.25), channel_id=1, source_target_pairs={{0,1},{1,0},{2,3},{3,2},{4,5},{5,4},{6,7},{7,6},{8,9},{9,8},{10,11... | collective-permute-start | bytes 1572872 | tf_op jit(solution)/shard_map/ppermute | solution.py:31
  141.0 9.4 %copy-start.3 = (bf16[1,128,1024]{2,1,0:T(8,128)(2,1)S(1)}, bf16[1,128,1024]{2,1,0:T(8,128)(2,1)}, u32[]{:S(2)}) copy-start(bf16[1,128,1024]{2,1,0:T(8,128)(2,1)} %param.7) | copy-start | bytes 786436
  141.0 9.4 %copy-start.11 = (f32[1,1024]{1,0:T(1,128)S(1)}, f32[1,1024]{1,0:T(1,128)}, u32[]{:S(2)}) copy-start(f32[1,1024]{1,0:T(1,128)} %gain.5) | copy-start | bytes 12292
  141.0 9.6 %copy-start.1 = (bf16[1,128,1024]{2,1,0:T(8,128)(2,1)S(1)}, bf16[1,128,1024]{2,1,0:T(8,128)(2,1)}, u32[]{:S(2)}) copy-start(bf16[1,128,1024]{2,1,0:T(8,128)(2,1)} %param.6) | copy-start | bytes 786436
  141.0 9.6 %copy-start.6 = (bf16[1,128,1024]{2,1,0:T(8,128)(2,1)S(1)}, bf16[1,128,1024]{2,1,0:T(8,128)(2,1)}, u32[]{:S(2)}) copy-start(bf16[1,128,1024]{2,1,0:T(8,128)(2,1)} %param.8) | copy-start | bytes 786436
  141.0 33.1 %all-to-all-start.3 = ((bf16[4,32,1024]{2,1,0:T(8,128)(2,1)}), bf16[4,32,1024]{2,1,0:T(8,128)(2,1)S(1)}, u32[]{:S(2)}, u32[]{:S(2)}) async-start(bf16[4,32,1024]{2,1,0:T(8,128)(2,1)} %shard_map.100), calls=%async_computation.3 | async-start | bytes 524288 | tf_op jit(solution)/shard_map/all_to_all | solution.py:45
  150.9 27.9 %collective-permute-start.3 = (bf16[128,1024]{1,0:T(8,128)(2,1)S(1)}, bf16[128,1024]{1,0:T(8,128)(2,1)S(1)}, u32[]{:S(2)}, u32[]{:S(2)}) collective-permute-start(bf16[128,1024]{1,0:T(8,128)(2,1)S(1)} %get-tuple-element.37), channel_id=1, source_target_pairs={{0,128},{128,256},{256,384},{384,512},{512,640},{640,768},{768,896... | collective-permute-start | bytes 786440 | tf_op jit(solution)/shard_map/ppermute | solution.py:36
  172.1 10.8 %collective-permute-start.4 = (bf16[128,1024]{1,0:T(8,128)(2,1)S(1)}, bf16[128,1024]{1,0:T(8,128)(2,1)S(1)}, u32[]{:S(2)}, u32[]{:S(2)}) collective-permute-start(bf16[128,1024]{1,0:T(8,128)(2,1)S(1)} %get-tuple-element.36), channel_id=1, source_target_pairs={{0,896},{128,0},{256,128},{384,256},{512,384},{640,512},{768,640},... | collective-permute-start | bytes 786440 | tf_op jit(solution)/shard_map/ppermute | solution.py:36

commit v8 on v6

--- a/solution.py
+++ b/solution.py
@@ -69,42 +69,62 @@
 
 
 def norm_into(src, at, gain, dst, to, rows):
-    def step(i, _):
-        r = pl.multiple_of(i * CHUNK, CHUNK)
-        x = src[pl.ds(at + r, CHUNK), :].astype(f32)
-        dst[pl.ds(to + r, CHUNK), :] = (x * scale_of(x) * gain[...]).astype(bf16)
-
-    lax.fori_loop(0, rows // CHUNK, step, None)
-
-
-def own_kernel(xf, xb, ct, near, wi, wo, gain, nf, nb, c2, br, dn, p, act_f, act, dp):
+    for r in range(0, rows, CHUNK):
+        x = src[at + r : at + r + CHUNK, :].astype(f32)
+        dst[to + r : to + r + CHUNK, :] = (x * scale_of(x) * gain[...]).astype(bf16)
+
+
+def copies_of(pairs, sems):
+    copies = [pltpu.make_async_copy(a, b, sems.at[i]) for i, (a, b) in enumerate(pairs)]
+    for copy in copies:
+        copy.start()
+    return copies
+
+
+def own_kernel(
+    xf, xb, ct, near, wi, wo, gain, nf, nb, c2, br, dn, p,
+    vx, vnear, vwi, vwo, vbr, vdn, vp, act_f, act, dp, arrived, sent,
+):
     rows = xf.shape[0]
     hid = wi.shape[0]
-    norm_into(xf, 0, gain, nf, 0, rows)
-    norm_into(near, 0, gain, nf, rows, rows)
-    norm_into(xb, 0, gain, nb, 0, rows)
-    norm_into(near, rows, gain, nb, rows, rows)
-    c2[:rows, :] = ct[...]
-    c2[rows:, :] = near[2 * rows :, :]
+    loads = copies_of(
+        [(near, vnear), (xb, vx.at[0]), (xf, vx.at[1]), (ct, c2.at[:rows]), (wi, vwi), (wo, vwo)],
+        arrived,
+    )
+    loads[0].wait()
+    norm_into(vnear, rows, gain, nb, rows, rows)
+    norm_into(vnear, 0, gain, nf, rows, rows)
+    c2[rows:, :] = vnear[2 * rows :, :]
+    for load in loads[1:]:
+        load.wait()
+    norm_into(vx.at[0], 0, gain, nb, 0, rows)
+    norm_into(vx.at[1], 0, gain, nf, 0, rows)
 
     def hidden(j, _):
         h = pl.ds(pl.multiple_of(j * TILE, TILE), TILE)
-        value, _ = gelu_both(nt(nf[...], wi[h, :]))
+        value, _ = gelu_both(nt(nf[...], vwi[h, :]))
         act_f[:, h] = value.astype(bf16)
-        value, slope = gelu_both(nt(nb[...], wi[h, :]))
+        value, slope = gelu_both(nt(nb[...], vwi[h, :]))
         act[:, h] = value.astype(bf16)
-        dp[:, h] = (nt(c2[...], wo[h, :]) * slope).astype(bf16)
-
-    lax.fori_loop(0, wi.shape[0] // TILE, hidden, None)
-
-    def back(j, _):
-        c = pl.ds(pl.multiple_of(j * TILE, TILE), TILE)
-        br[:, c] = nn(act_f[...], wo[:, c])
-        dn[:, c] = nn(dp[...], wi[:, c])
-        p[c, :hid] = tn(nb[:, c], dp[...])
-        p[c, hid:] = tn(c2[:, c], act[...])
-
-    lax.fori_loop(0, wi.shape[1] // TILE, back, None)
+        dp[:, h] = (nt(c2[...], vwo[h, :]) * slope).astype(bf16)
+
+    lax.fori_loop(0, hid // TILE, hidden, None)
+    stores = []
+    for k in range(FAR):
+        c = slice(k * TILE, (k + 1) * TILE)
+        vp[c, :hid] = tn(nb[:, c], dp[...]).astype(bf16)
+        vp[c, hid:] = tn(c2[:, c], act[...]).astype(bf16)
+        store = pltpu.make_async_copy(vp.at[c], p.at[c], sent.at[k])
+        store.start()
+        stores.append(store)
+    for k, (a, w, v, out) in enumerate(((act_f, vwo, vbr, br), (dp, vwi, vdn, dn))):
+        for t in range(0, w.shape[1], 2 * TILE):
+            v[:, t : t + 2 * TILE] = nn(a[...], w[:, t : t + 2 * TILE]).astype(bf16)
+        store = pltpu.make_async_copy(v, out, sent.at[FAR + k])
+        store.start()
+        stores.append(store)
+    for store in stores:
+        store.wait()
 
 
 def rest_kernel(whole, nf, nb, c2, br, dn, keep, send, act_f, dp, wi, wo):
@@ -128,24 +148,27 @@
 
     def back(j, _):
         c = pl.ds(pl.multiple_of(j * TILE, TILE), TILE)
-        b = br[:, c] + nn(act_f[...], wo[:, c])
+        b = br[:, c].astype(f32) + nn(act_f[...], wo[:, c])
         keep[0, :, c] = b[:rows]
         send[0, :, c] = b[rows:].astype(bf16)
-        g = dn[:, c] + nn(dp[...], wi[:, c])
+        g = dn[:, c].astype(f32) + nn(dp[...], wi[:, c])
         keep[1, :, c] = g[:rows]
         send[1, :, c] = g[rows:].astype(bf16)
 
     lax.fori_loop(0, wi.shape[1] // TILE, back, None)
 
 
-def half_kernel(far, far2, wi, gain, nbt, act, slope, nb):
+def half_kernel(far, far2, wi, gain, nbt, act, slope, vfar, vwi, nb, arrived):
     rows = far.shape[0]
-    for k, part in enumerate((far, far2)):
-        norm_into(part, 0, gain, nb, k * rows, rows)
+    loads = copies_of([(far, vfar.at[0]), (far2, vfar.at[1]), (wi, vwi)], arrived)
+    for k in range(2):
+        loads[k].wait()
+        norm_into(vfar.at[k], 0, gain, nb, k * rows, rows)
+    loads[2].wait()
 
     def hidden(j, _):
         h = pl.ds(pl.multiple_of(j * TILE, TILE), TILE)
-        value, down = gelu_both(nt(nb[...], wi[h, :]))
+        value, down = gelu_both(nt(nb[...], vwi[h, :]))
         act[:, h] = value.astype(bf16)
         slope[:, h] = down
         for k in range(2):
@@ -155,31 +178,37 @@
     lax.fori_loop(0, wi.shape[0] // TILE, hidden, None)
 
 
-def grad_kernel(far, far2, wo, nbt, act, slope, p, g, vwo, vnbt, vact, vslope, vp, vg, c3, dp3, arrived, sent):
+def grad_kernel(far, far2, wo, nbt, act, slope, p, g, c3, vwo, vnbt, vact, vslope, vp, vg, dp3, arrived, sent):
     rows = far.shape[0]
     hid = wo.shape[0]
-    pairs = [(wo, vwo), (slope, vslope), (nbt, vnbt), (act, vact), (p, vp)]
-    loads = [pltpu.make_async_copy(a, b, arrived.at[i]) for i, (a, b) in enumerate(pairs)]
-    for load in loads:
-        load.start()
-    c3[:rows, :] = far[...]
-    c3[rows:, :] = far2[...]
-    loads[0].wait()
-    loads[1].wait()
+    loads = copies_of(
+        [
+            (far, c3.at[:rows]),
+            (far2, c3.at[rows:]),
+            (wo, vwo),
+            (slope, vslope),
+            (act, vact),
+            (nbt, vnbt),
+            (p, vp),
+        ],
+        arrived,
+    )
+    for load in loads[:4]:
+        load.wait()
 
     def hidden(j, _):
         h = pl.ds(pl.multiple_of(j * TILE, TILE), TILE)
         dp3[:, h] = (nt(c3[...], vwo[h, :]) * vslope[:, h]).astype(bf16)
 
     lax.fori_loop(0, hid // TILE, hidden, None)
-    for load in loads[2:]:
+    for load in loads[4:]:
         load.wait()
     stores = []
     for k in range(FAR):
         c = slice(k * TILE, (k + 1) * TILE)
-        gi = vp[c, :hid] + nn(vnbt[c, :], dp3[...])
+        gi = vp[c, :hid].astype(f32) + nn(vnbt[c, :], dp3[...])
         vg[:, k, :, :hid] = gi.astype(bf16).reshape(NEAR, -1, hid)
-        go = vp[c, hid:] + tn(c3[:, c], vact[...])
+        go = vp[c, hid:].astype(f32) + tn(c3[:, c], vact[...])
         vg[:, k, :, hid:] = go.astype(bf16).reshape(NEAR, -1, hid)
         store = pltpu.make_async_copy(vg.at[:, k], g.at[:, k], sent.at[k])
         store.start()
@@ -235,12 +264,28 @@
     far_s = to_chip(xb)
     far_c = to_chip(ct)
     near = to_core(jnp.concatenate([xf, xb, ct]))
+    dma = pltpu.SemaphoreType.DMA
     nf, nb, c2, br, dn, p = local(
         own_kernel,
-        [((both, dim), bf16)] * 3 + [((both, dim), f32)] * 2 + [((dim, 2 * hid), f32)],
-        [((both, hid), bf16)] * 3,
+        [((both, dim), bf16)] * 5 + [((dim, 2 * hid), bf16)],
+        [
+            ((2, rows, dim), bf16),
+            ((3 * rows, dim), bf16),
+            ((hid, dim), bf16),
+            ((hid, dim), bf16),
+            ((both, dim), bf16),
+            ((both, dim), bf16),
+            ((dim, 2 * hid), bf16),
+            ((both, hid), bf16),
+            ((both, hid), bf16),
+            ((both, hid), bf16),
+            dma((6,)),
+            dma((FAR + 2,)),
+        ],
         14 * both * hid * dim,
-        11 * 2**20,
+        8 * 2**20,
+        in_specs=[hbm] * 6 + [vmem],
+        out_specs=[vmem] * 3 + [hbm] * 3,
     )(xf, xb, ct, near, wi, wo, gain)
     col = gathered(piece, far_groups)
     whole = gathered(col, near_groups).reshape(n_dp, 2, part, dim)
@@ -265,9 +310,11 @@
     nbt3, act3, slope3 = local(
         half_kernel,
         [((dim, both), bf16), ((both, hid), bf16), ((both, hid), f32)],
-        [((both, dim), bf16)],
+        [((2, rows, dim), bf16), ((hid, dim), bf16), ((both, dim), bf16), dma((3,))],
         2 * both * hid * dim,
         4 * 2**20,
+        in_specs=[hbm] * 3 + [vmem],
+        out_specs=[vmem] * 3,
     )(far_s, far_s2, wi, gain)
     far_c2 = to_core(far_c)
     cut = dim // n_dp
@@ -275,20 +322,20 @@
         grad_kernel,
         [((NEAR, FAR, cut, 2 * hid), bf16)],
         [
+            ((both, dim), bf16),
             ((hid, dim), bf16),
             ((dim, both), bf16),
             ((both, hid), bf16),
             ((both, hid), f32),
-            ((dim, 2 * hid), f32),
+            ((dim, 2 * hid), bf16),
             ((NEAR, FAR, cut, 2 * hid), bf16),
-            ((both, dim), bf16),
-            ((both, hid), bf16),
-            pltpu.SemaphoreType.DMA((5,)),
-            pltpu.SemaphoreType.DMA((FAR,)),
+            ((both, hid), bf16),
+            dma((7,)),
+            dma((FAR,)),
         ],
         6 * both * hid * dim,
-        9 * 2**20,
-        in_specs=[vmem, vmem, hbm, hbm, hbm, hbm, hbm],
+        7 * 2**20,
+        in_specs=[hbm] * 7,
         out_specs=[hbm],
     )(far_c, far_c2, wo, nbt3, act3, slope3, p)
     g = exchanged(g, near_groups)
@@ -316,4 +363,6 @@
         P("section", "mp", "dp"),
         P("section", "mp", "dp"),
     )
-    return jax.shard_map(layer, mesh=mesh, in_specs=in_specs, out_specs=out_specs, check_vma=False)
+    return jax.shard_map(
+        layer, mesh=mesh, in_specs=in_specs, out_specs=out_specs, check_vma=False
+    )

time: 187 us -> 184 us (0.984)
  Pallas kernels: 29.2 us -> 25.2 us
    pallas_call x2, Pallas kernels: 15.7 us -> 12.2 us  [the longest x1 7.97 us: layer(): local(own_kernel, [((both, dim), bf16)] * 5 + [((dim, 2 * hid), bf16)], [...]
  transfers between devices with their start and end apart: 12 -> 12, of which waited for: 6 -> 6; matrix products, arithmetic and copies ran while one was open for 1% -> 1% of each run, Pallas kernels for 15% -> 13%
where the time goes in v8:
time: 184 us; the launch traced here: 183 us
  starting transfers between devices  86.6 us (47%)
  waiting for transfers between devices  52 us (28%)
  Pallas kernels  25.2 us (14%)
  blocking collectives  11.5 us (6%)
  local copies, waits for them, and re-layouts  4.54 us (2%)
    ppermute x3, starting transfers between devices, to_chip(): return lax.ppermute(x, 'mp', other_chip)  34.5 us
    ppermute x3, waiting for transfers between devices, to_chip(): return lax.ppermute(x, 'mp', other_chip)  26.2 us
    ppermute x2, starting transfers between devices, shifted(): lax.ppermute(x, axis, [(i, (i + by) % length) for i in range(length)])  23.2 us
    all_to_all x2, waiting for transfers between devices, exchanged(): return lax.all_to_all(x, 'dp', 0, 0, tiled=True, axis_index_groups=groups)  17.6 us
    all_to_all x2, starting transfers between devices, exchanged(): return lax.all_to_all(x, 'dp', 0, 0, tiled=True, axis_index_groups=groups)  14.8 us
    all_to_all x1, blocking collectives, gathered(): lax.all_to_all(copies, 'dp', 0, 0, tiled=True, axis_index_groups=groups)  11.5 us
    ppermute x2, waiting for transfers between devices, shifted(): lax.ppermute(x, axis, [(i, (i + by) % length) for i in range(length)])  8.17 us
    pallas_call x1, Pallas kernels, layer(): local(own_kernel, [((both, dim), bf16)] * 5 + [((dim, 2 * hid), bf16)], [...  7.97 us
  transfers between devices with their start and end apart: 12, of which 6 were waited for; matrix products, arithmetic and copies ran while one was open for 1% of the time, Pallas kernels for 13%

profile of v8, /device:TPU:40, one launch (start us, length us, event | category | flops | bytes accessed | tf_op | source)
XLA Modules:
  0.0 182.6 jit_solution(16018337409718916667)
XLA Ops:
  0.7 0.8 constant_dynamic-slice_fusion
  1.4 0.8 constant_dynamic-slice_fusion.1
  2.2 19.4 %collective-permute-start = (bf16[2,16,1024]{2,1,0:T(8,128)(2,1)S(1)}, bf16[2,16,1024]{2,1,0:T(8,128)(2,1)S(1)}, u32[]{:S(2)}, u32[]{:S(2)}) collective-permute-start(bf16[2,16,1024]{2,1,0:T(8,128)(2,1)S(1)} %pad_maximum_fusion.1), channel_id=1, source_target_pairs={{0,2},{1,3},{2,0},{3,1},{4,6},{5,7},{6,4},{7,5},{8,10},{9,11},{10,... | collective-permute-start | bytes 196616 | tf_op jit(solution)/shard_map/ppermute | solution.py:27
  21.6 4.6 %collective-permute-done = bf16[2,16,1024]{2,1,0:T(8,128)(2,1)S(1)} collective-permute-done((bf16[2,16,1024]{2,1,0:T(8,128)(2,1)S(1)}, bf16[2,16,1024]{2,1,0:T(8,128)(2,1)S(1)}, u32[]{:S(2)}, u32[]{:S(2)}) %collective-permute-start) | collective-permute-done | bytes 65568 | tf_op jit(solution)/shard_map/ppermute | solution.py:27
  26.2 11.5 %all_to_all.20 = bf16[4,2,16,1024]{3,2,1,0:T(8,128)(2,1)S(1)} all-to-all(bf16[4,2,16,1024]{3,2,1,0:T(8,128)(2,1)S(1)} %broadcast_in_dim.14), channel_id=1, replica_groups={{0,32,64,96},{4,36,68,100},{8,40,72,104},{12,44,76,108},{16,48,80,112},..., dimensions={0} | all-to-all | bytes 524288 | tf_op jit(solution)/shard_map/all_to_all | solution.py:41
  37.7 1.6 broadcast_in_dim.15
  39.3 6.3 %all-to-all-start.1 = ((bf16[8,4,2,16,1024]{4,3,2,1,0:T(8,128)(2,1)}), bf16[8,4,2,16,1024]{4,3,2,1,0:T(8,128)(2,1)}, u32[]{:S(2)}, u32[]{:S(2)}) async-start(bf16[8,4,2,16,1024]{4,3,2,1,0:T(8,128)(2,1)} %broadcast_in_dim.15), calls=%async_computation.1 | async-start | bytes 4194304 | tf_op jit(solution)/shard_map/all_to_all | solution.py:41
  45.6 1.9 %collective-permute-start.1 = (bf16[384,1024]{1,0:T(8,128)(2,1)S(1)}, bf16[384,1024]{1,0:T(8,128)(2,1)}, u32[]{:S(2)}, u32[]{:S(2)}) collective-permute-start(bf16[384,1024]{1,0:T(8,128)(2,1)S(1)} %pad_maximum_fusion), channel_id=1, source_target_pairs={{0,1},{1,0},{2,3},{3,2},{4,5},{5,4},{6,7},{7,6},{8,9},{9,8},{10,11... | collective-permute-start | bytes 2359304 | tf_op jit(solution)/shard_map/ppermute | solution.py:31
  47.6 13.3 %collective-permute-start.7 = (bf16[128,1024]{1,0:T(8,128)(2,1)S(1)}, bf16[128,1024]{1,0:T(8,128)(2,1)S(1)}, u32[]{:S(2)}, u32[]{:S(2)}) collective-permute-start(bf16[128,1024]{1,0:T(8,128)(2,1)S(1)} %bitcast.34), channel_id=1, source_target_pairs={{0,2},{1,3},{2,0},{3,1},{4,6},{5,7},{6,4},{7,5},{8,10},{9,11},{10,... | collective-permute-start | bytes 786440 | tf_op jit(solution)/shard_map/ppermute | solution.py:27
  60.8 1.9 %collective-permute-start.5 = (bf16[128,1024]{1,0:T(8,128)(2,1)S(1)}, bf16[128,1024]{1,0:T(8,128)(2,1)S(1)}, u32[]{:S(2)}, u32[]{:S(2)}) collective-permute-start(bf16[128,1024]{1,0:T(8,128)(2,1)S(1)} %bitcast.43), channel_id=1, source_target_pairs={{0,2},{1,3},{2,0},{3,1},{4,6},{5,7},{6,4},{7,5},{8,10},{9,11},{10,... | collective-permute-start | bytes 786440 | tf_op jit(solution)/shard_map/ppermute | solution.py:27
  62.8 11.1 %collective-permute-done.7.far = bf16[128,1024]{1,0:T(8,128)(2,1)S(1)} collective-permute-done((bf16[128,1024]{1,0:T(8,128)(2,1)S(1)}, bf16[128,1024]{1,0:T(8,128)(2,1)S(1)}, u32[]{:S(2)}, u32[]{:S(2)}) %collective-permute-start.7) | collective-permute-done | bytes 262176 | tf_op jit(solution)/shard_map/ppermute | solution.py:27
  73.8 1.9 %collective-permute-start.8 = (bf16[128,1024]{1,0:T(8,128)(2,1)S(1)}, bf16[128,1024]{1,0:T(8,128)(2,1)S(1)}, u32[]{:S(2)}, u32[]{:S(2)}) collective-permute-start(bf16[128,1024]{1,0:T(8,128)(2,1)S(1)} %collective-permute-done.7.far), channel_id=1, source_target_pairs={{0,1},{1,0},{2,3},{3,2},{4,5},{5,4},{6,7},{7,6},{8,9},{9,8},{10,11... | collective-permute-start | bytes 786440 | tf_op jit(solution)/shard_map/ppermute | solution.py:31
  75.7 10.5 %collective-permute-done.5.far = bf16[128,1024]{1,0:T(8,128)(2,1)S(1)} collective-permute-done((bf16[128,1024]{1,0:T(8,128)(2,1)S(1)}, bf16[128,1024]{1,0:T(8,128)(2,1)S(1)}, u32[]{:S(2)}, u32[]{:S(2)}) %collective-permute-start.5) | collective-permute-done | bytes 262176 | tf_op jit(solution)/shard_map/ppermute | solution.py:27
  86.3 1.9 %collective-permute-start.6 = (bf16[128,1024]{1,0:T(8,128)(2,1)S(1)}, bf16[128,1024]{1,0:T(8,128)(2,1)S(1)}, u32[]{:S(2)}, u32[]{:S(2)}) collective-permute-start(bf16[128,1024]{1,0:T(8,128)(2,1)S(1)} %collective-permute-done.5.far), channel_id=1, source_target_pairs={{0,1},{1,0},{2,3},{3,2},{4,5},{5,4},{6,7},{7,6},{8,9},{9,8},{10,11... | collective-permute-start | bytes 786440 | tf_op jit(solution)/shard_map/ppermute | solution.py:31
  88.2 0.7 copy-done.10
  88.9 4.1 %shard_map.96 = (bf16[1024,256]{1,0:T(8,128)(2,1)}, bf16[256,512]{1,0:T(8,128)(2,1)}, f32[256,512]{1,0:T(8,128)}) custom-call(bf16[128,1024]{1,0:T(8,128)(2,1)} %copy-done.9, bf16[128,1024]{1,0:T(8,128)(2,1)} %copy-done.10, bf16[512,1024]{1,0:T(8,128)(2,1)} %bitcast.37, f32[1,1024]{1,0:T(1,128)} %gain.3), custom_call_target="tpu_custom_call" | custom-call | flops 268435456 | bytes 4194304 | tf_op jit(solution)/shard_map/pallas_call | solution.py:310
  93.0 8.0 %shard_map.93 = (bf16[256,1024]{1,0:T(8,128)(2,1)}, bf16[256,1024]{1,0:T(8,128)(2,1)}, bf16[256,1024]{1,0:T(8,128)(2,1)}, bf16[256,1024]{1,0:T(8,128)(2,1)}, bf1...) custom-call(bf16[128,1024]{1,0:T(8,128)(2,1)} %bitcast.39, bf16[128,1024]{1,0:T(8,128)(2,1)} %bitcast.32, ...), custom_call_target="tpu_custom_call" | custom-call | flops 1879048192 | bytes 8388608 | tf_op jit(solution)/shard_map/pallas_call | solution.py:268
  101.1 0.7 copy-done.8
  101.7 4.2 %shard_map.97 = bf16[8,4,32,1024]{3,2,1,0:T(8,128)(2,1)} custom-call(bf16[128,1024]{1,0:T(8,128)(2,1)} %copy-done.7, bf16[128,1024]{1,0:T(8,128)(2,1)} %copy-done.8, bf16[512,1024]{1,0:T(8,128)(2,1)} %bitcast.36, bf16[1024,256]{1,0:T(8,128)(2,1)} %get-tuple-element.28.nbt, bf16[256,512]{1,0:T(8,128)(2,1)} %get-tuple-element.29.act, ...), custom_call_target="tpu_custom_call" | custom-call | flops 805306368 | bytes 7340032 | tf_op jit(solution)/shard_map/pallas_call | solution.py:321
  106.0 5.7 %all-to-all-start.2 = ((bf16[8,4,32,1024]{3,2,1,0:T(8,128)(2,1)}), bf16[8,4,32,1024]{3,2,1,0:T(8,128)(2,1)S(1)}, u32[]{:S(2)}, u32[]{:S(2)}) async-start(bf16[8,4,32,1024]{3,2,1,0:T(8,128)(2,1)} %shard_map.97), calls=%async_computation.2 | async-start | bytes 4194304 | tf_op jit(solution)/shard_map/all_to_all | solution.py:45
  111.7 6.4 %shard_map.94 = (f32[2,128,1024]{2,1,0:T(8,128)}, bf16[2,128,1024]{2,1,0:T(8,128)(2,1)}) custom-call(bf16[32,2,16,1024]{3,2,1,0:T(8,128)(2,1)} %bitcast.1.whole, bf16[256,1024]{1,0:T(8,128)(2,1)} %get-tuple-element.19.nf, bf16[256,1024]{1,0:T(8,128)(2,1)} %get-tuple-element.20.nb, bf16[256,1024]{1,0:T(8,128)(2,1)} %get-tuple-element.21.c2, ...), custom_call_target="tpu_custom_call" | custom-call | flops 1342177280 | bytes 8388608 | tf_op jit(solution)/shard_map/pallas_call | solution.py:292
  118.2 2.0 %collective-permute-start.2 = (bf16[2,128,1024]{2,1,0:T(8,128)(2,1)}, bf16[2,128,1024]{2,1,0:T(8,128)(2,1)}, u32[]{:S(2)}, u32[]{:S(2)}) collective-permute-start(bf16[2,128,1024]{2,1,0:T(8,128)(2,1)} %get-tuple-element.25), channel_id=1, source_target_pairs={{0,1},{1,0},{2,3},{3,2},{4,5},{5,4},{6,7},{7,6},{8,9},{9,8},{10,11... | collective-permute-start | bytes 1572872 | tf_op jit(solution)/shard_map/ppermute | solution.py:31
  120.2 17.6 %all-to-all-done.2.pieces = bf16[8,4,32,1024]{3,2,1,0:T(8,128)(2,1)S(1)} async-done(((bf16[8,4,32,1024]{3,2,1,0:T(8,128)(2,1)}), bf16[8,4,32,1024]{3,2,1,0:T(8,128)(2,1)S(1)}, u32[]{:S(2)}, u32[]{:S(2)}) %all-to-all-start.2) | async-done | bytes 2097184 | tf_op jit(solution)/shard_map/all_to_all | solution.py:45
  137.9 1.0 shard_map.98
  138.9 9.1 %all-to-all-start.3 = ((bf16[4,32,1024]{2,1,0:T(8,128)(2,1)}), bf16[4,32,1024]{2,1,0:T(8,128)(2,1)S(1)}, u32[]{:S(2)}, u32[]{:S(2)}) async-start(bf16[4,32,1024]{2,1,0:T(8,128)(2,1)} %shard_map.98), calls=%async_computation.3 | async-start | bytes 524288 | tf_op jit(solution)/shard_map/all_to_all | solution.py:45
  148.0 1.2 convert_add_fusion
  149.8 21.3 %collective-permute-start.3 = (bf16[128,1024]{1,0:T(8,128)(2,1)S(1)}, bf16[128,1024]{1,0:T(8,128)(2,1)S(1)}, u32[]{:S(2)}, u32[]{:S(2)}) collective-permute-start(bf16[128,1024]{1,0:T(8,128)(2,1)S(1)} %get-tuple-element.37), channel_id=1, source_target_pairs={{0,128},{128,256},{256,384},{384,512},{512,640},{640,768},{768,896... | collective-permute-start | bytes 786440 | tf_op jit(solution)/shard_map/ppermute | solution.py:36
  171.1 1.9 %collective-permute-start.4 = (bf16[128,1024]{1,0:T(8,128)(2,1)S(1)}, bf16[128,1024]{1,0:T(8,128)(2,1)S(1)}, u32[]{:S(2)}, u32[]{:S(2)}) collective-permute-start(bf16[128,1024]{1,0:T(8,128)(2,1)S(1)} %get-tuple-element.36), channel_id=1, source_target_pairs={{0,896},{128,0},{256,128},{384,256},{512,384},{640,512},{768,640},... | collective-permute-start | bytes 786440 | tf_op jit(solution)/shard_map/ppermute | solution.py:36
  173.0 0.7 shard_map.99
  173.6 4.1 %collective-permute-done.3.a = bf16[128,1024]{1,0:T(8,128)(2,1)S(1)} collective-permute-done((bf16[128,1024]{1,0:T(8,128)(2,1)S(1)}, bf16[128,1024]{1,0:T(8,128)(2,1)S(1)}, u32[]{:S(2)}, u32[]{:S(2)}) %collective-permute-start.3) | collective-permute-done | bytes 262176 | tf_op jit(solution)/shard_map/ppermute | solution.py:36
  177.7 4.1 %collective-permute-done.4.b = bf16[128,1024]{1,0:T(8,128)(2,1)S(1)} collective-permute-done((bf16[128,1024]{1,0:T(8,128)(2,1)S(1)}, bf16[128,1024]{1,0:T(8,128)(2,1)S(1)}, u32[]{:S(2)}, u32[]{:S(2)}) %collective-permute-start.4) | collective-permute-done | bytes 262176 | tf_op jit(solution)/shard_map/ppermute | solution.py:36
  181.8 0.8 shard_map.95
  (34 shorter events, 0.6 us)
Async XLA Ops:
  2.2 23.9 %collective-permute-start = (bf16[2,16,1024]{2,1,0:T(8,128)(2,1)S(1)}, bf16[2,16,1024]{2,1,0:T(8,128)(2,1)S(1)}, u32[]{:S(2)}, u32[]{:S(2)}) collective-permute-start(bf16[2,16,1024]{2,1,0:T(8,128)(2,1)S(1)} %pad_maximum_fusion.1), channel_id=1, source_target_pairs={{0,2},{1,3},{2,0},{3,1},{4,6},{5,7},{6,4},{7,5},{8,10},{9,11},{10,... | collective-permute-start | bytes 196616 | tf_op jit(solution)/shard_map/ppermute | solution.py:27
  39.3 6.3 %copy-start = (bf16[1,128,1024]{2,1,0:T(8,128)(2,1)S(1)}, bf16[1,128,1024]{2,1,0:T(8,128)(2,1)}, u32[]{:S(2)}) copy-start(bf16[1,128,1024]{2,1,0:T(8,128)(2,1)} %param.7) | copy-start | bytes 786436
  39.3 6.3 %copy-start.3 = (bf16[1,128,1024]{2,1,0:T(8,128)(2,1)S(1)}, bf16[1,128,1024]{2,1,0:T(8,128)(2,1)}, u32[]{:S(2)}) copy-start(bf16[1,128,1024]{2,1,0:T(8,128)(2,1)} %param.6) | copy-start | bytes 786436
  39.3 6.3 %copy-start.5 = (bf16[1,128,1024]{2,1,0:T(8,128)(2,1)S(1)}, bf16[1,128,1024]{2,1,0:T(8,128)(2,1)}, u32[]{:S(2)}) copy-start(bf16[1,128,1024]{2,1,0:T(8,128)(2,1)} %param.8) | copy-start | bytes 786436
  39.3 66.7 %all-to-all-start.1 = ((bf16[8,4,2,16,1024]{4,3,2,1,0:T(8,128)(2,1)}), bf16[8,4,2,16,1024]{4,3,2,1,0:T(8,128)(2,1)}, u32[]{:S(2)}, u32[]{:S(2)}) async-start(bf16[8,4,2,16,1024]{4,3,2,1,0:T(8,128)(2,1)} %broadcast_in_dim.15), calls=%async_computation.1 | async-start | bytes 4194304 | tf_op jit(solution)/shard_map/all_to_all | solution.py:41
  45.6 47.4 %collective-permute-start.1 = (bf16[384,1024]{1,0:T(8,128)(2,1)S(1)}, bf16[384,1024]{1,0:T(8,128)(2,1)}, u32[]{:S(2)}, u32[]{:S(2)}) collective-permute-start(bf16[384,1024]{1,0:T(8,128)(2,1)S(1)} %pad_maximum_fusion), channel_id=1, source_target_pairs={{0,1},{1,0},{2,3},{3,2},{4,5},{5,4},{6,7},{7,6},{8,9},{9,8},{10,11... | collective-permute-start | bytes 2359304 | tf_op jit(solution)/shard_map/ppermute | solution.py:31
  47.6 26.3 %collective-permute-start.7 = (bf16[128,1024]{1,0:T(8,128)(2,1)S(1)}, bf16[128,1024]{1,0:T(8,128)(2,1)S(1)}, u32[]{:S(2)}, u32[]{:S(2)}) collective-permute-start(bf16[128,1024]{1,0:T(8,128)(2,1)S(1)} %bitcast.34), channel_id=1, source_target_pairs={{0,2},{1,3},{2,0},{3,1},{4,6},{5,7},{6,4},{7,5},{8,10},{9,11},{10,... | collective-permute-start | bytes 786440 | tf_op jit(solution)/shard_map/ppermute | solution.py:27
  60.8 25.4 %collective-permute-start.5 = (bf16[128,1024]{1,0:T(8,128)(2,1)S(1)}, bf16[128,1024]{1,0:T(8,128)(2,1)S(1)}, u32[]{:S(2)}, u32[]{:S(2)}) collective-permute-start(bf16[128,1024]{1,0:T(8,128)(2,1)S(1)} %bitcast.43), channel_id=1, source_target_pairs={{0,2},{1,3},{2,0},{3,1},{4,6},{5,7},{6,4},{7,5},{8,10},{9,11},{10,... | collective-permute-start | bytes 786440 | tf_op jit(solution)/shard_map/ppermute | solution.py:27
  73.8 14.4 %copy-start.9 = (bf16[128,1024]{1,0:T(8,128)(2,1)}, bf16[128,1024]{1,0:T(8,128)(2,1)S(1)}, u32[]{:S(2)}) copy-start(bf16[128,1024]{1,0:T(8,128)(2,1)S(1)} %collective-permute-done.7.far) | copy-start | bytes 786436
  73.8 14.4 %collective-permute-start.8 = (bf16[128,1024]{1,0:T(8,128)(2,1)S(1)}, bf16[128,1024]{1,0:T(8,128)(2,1)S(1)}, u32[]{:S(2)}, u32[]{:S(2)}) collective-permute-start(bf16[128,1024]{1,0:T(8,128)(2,1)S(1)} %collective-permute-done.7.far), channel_id=1, source_target_pairs={{0,1},{1,0},{2,3},{3,2},{4,5},{5,4},{6,7},{7,6},{8,9},{9,8},{10,11... | collective-permute-start | bytes 786440 | tf_op jit(solution)/shard_map/ppermute | solution.py:31
  86.3 14.8 %copy-start.7 = (bf16[128,1024]{1,0:T(8,128)(2,1)}, bf16[128,1024]{1,0:T(8,128)(2,1)S(1)}, u32[]{:S(2)}) copy-start(bf16[128,1024]{1,0:T(8,128)(2,1)S(1)} %collective-permute-done.5.far) | copy-start | bytes 786436
  86.3 14.8 %collective-permute-start.6 = (bf16[128,1024]{1,0:T(8,128)(2,1)S(1)}, bf16[128,1024]{1,0:T(8,128)(2,1)S(1)}, u32[]{:S(2)}, u32[]{:S(2)}) collective-permute-start(bf16[128,1024]{1,0:T(8,128)(2,1)S(1)} %collective-permute-done.5.far), channel_id=1, source_target_pairs={{0,1},{1,0},{2,3},{3,2},{4,5},{5,4},{6,7},{7,6},{8,9},{9,8},{10,11... | collective-permute-start | bytes 786440 | tf_op jit(solution)/shard_map/ppermute | solution.py:31
  88.2 0.7 copy-start.10
  101.0 0.7 copy-start.8
  106.0 31.9 %all-to-all-start.2 = ((bf16[8,4,32,1024]{3,2,1,0:T(8,128)(2,1)}), bf16[8,4,32,1024]{3,2,1,0:T(8,128)(2,1)S(1)}, u32[]{:S(2)}, u32[]{:S(2)}) async-start(bf16[8,4,32,1024]{3,2,1,0:T(8,128)(2,1)} %shard_map.97), calls=%async_computation.2 | async-start | bytes 4194304 | tf_op jit(solution)/shard_map/all_to_all | solution.py:45
  118.2 29.8 %copy-start.2 = (f32[2,128,1024]{2,1,0:T(8,128)S(1)}, f32[2,128,1024]{2,1,0:T(8,128)}, u32[]{:S(2)}) copy-start(f32[2,128,1024]{2,1,0:T(8,128)} %get-tuple-element.24) | copy-start | bytes 3145732
  118.2 29.8 %collective-permute-start.2 = (bf16[2,128,1024]{2,1,0:T(8,128)(2,1)}, bf16[2,128,1024]{2,1,0:T(8,128)(2,1)}, u32[]{:S(2)}, u32[]{:S(2)}) collective-permute-start(bf16[2,128,1024]{2,1,0:T(8,128)(2,1)} %get-tuple-element.25), channel_id=1, source_target_pairs={{0,1},{1,0},{2,3},{3,2},{4,5},{5,4},{6,7},{7,6},{8,9},{9,8},{10,11... | collective-permute-start | bytes 1572872 | tf_op jit(solution)/shard_map/ppermute | solution.py:31
  138.9 10.4 %copy-start.1 = (bf16[1,128,1024]{2,1,0:T(8,128)(2,1)S(1)}, bf16[1,128,1024]{2,1,0:T(8,128)(2,1)}, u32[]{:S(2)}) copy-start(bf16[1,128,1024]{2,1,0:T(8,128)(2,1)} %param.7) | copy-start | bytes 786436
  138.9 10.4 %copy-start.11 = (f32[1,1024]{1,0:T(1,128)S(1)}, f32[1,1024]{1,0:T(1,128)}, u32[]{:S(2)}) copy-start(f32[1,1024]{1,0:T(1,128)} %gain.3) | copy-start | bytes 12292
  138.9 10.6 %copy-start.4 = (bf16[1,128,1024]{2,1,0:T(8,128)(2,1)S(1)}, bf16[1,128,1024]{2,1,0:T(8,128)(2,1)}, u32[]{:S(2)}) copy-start(bf16[1,128,1024]{2,1,0:T(8,128)(2,1)} %param.6) | copy-start | bytes 786436
  138.9 10.6 %copy-start.6 = (bf16[1,128,1024]{2,1,0:T(8,128)(2,1)S(1)}, bf16[1,128,1024]{2,1,0:T(8,128)(2,1)}, u32[]{:S(2)}) copy-start(bf16[1,128,1024]{2,1,0:T(8,128)(2,1)} %param.8) | copy-start | bytes 786436
  138.9 34.1 %all-to-all-start.3 = ((bf16[4,32,1024]{2,1,0:T(8,128)(2,1)}), bf16[4,32,1024]{2,1,0:T(8,128)(2,1)S(1)}, u32[]{:S(2)}, u32[]{:S(2)}) async-start(bf16[4,32,1024]{2,1,0:T(8,128)(2,1)} %shard_map.98), calls=%async_computation.3 | async-start | bytes 524288 | tf_op jit(solution)/shard_map/all_to_all | solution.py:45
  149.8 28.0 %collective-permute-start.3 = (bf16[128,1024]{1,0:T(8,128)(2,1)S(1)}, bf16[128,1024]{1,0:T(8,128)(2,1)S(1)}, u32[]{:S(2)}, u32[]{:S(2)}) collective-permute-start(bf16[128,1024]{1,0:T(8,128)(2,1)S(1)} %get-tuple-element.37), channel_id=1, source_target_pairs={{0,128},{128,256},{256,384},{384,512},{512,640},{640,768},{768,896... | collective-permute-start | bytes 786440 | tf_op jit(solution)/shard_map/ppermute | solution.py:36
  171.1 10.8 %collective-permute-start.4 = (bf16[128,1024]{1,0:T(8,128)(2,1)S(1)}, bf16[128,1024]{1,0:T(8,128)(2,1)S(1)}, u32[]{:S(2)}, u32[]{:S(2)}) collective-permute-start(bf16[128,1024]{1,0:T(8,128)(2,1)S(1)} %get-tuple-element.36), channel_id=1, source_target_pairs={{0,896},{128,0},{256,128},{384,256},{512,384},{640,512},{768,640},... | collective-permute-start | bytes 786440 | tf_op jit(solution)/shard_map/ppermute | solution.py:36

commit v9 on v8

--- a/solution.py
+++ b/solution.py
@@ -127,35 +127,47 @@
         store.wait()
 
 
-def rest_kernel(whole, nf, nb, c2, br, dn, keep, send, act_f, dp, wi, wo):
+def rest_kernel(
+    whole, nf, nb, c2, br, dn, keep, send, vwi, vwo, vnf, vnb, vc2, vbr, vdn, act_f, dp, arrived
+):
     rows = keep.shape[1]
-
-    def split(i, _):
-        r = pl.ds(pl.multiple_of(i * 16, 16), 16)
-        wi[r, :] = whole[i, 0]
-        wo[r, :] = whole[i, 1]
-
-    lax.fori_loop(0, whole.shape[0], split, None)
+    blocks, part, dim = vwi.shape
+    hid = blocks * part
+    loads = copies_of(
+        [
+            (whole.at[:, 0], vwi),
+            (nf, vnf),
+            (nb, vnb),
+            (whole.at[:, 1], vwo),
+            (c2, vc2),
+            (br, vbr),
+            (dn, vdn),
+        ],
+        arrived,
+    )
+    for load in loads[:5]:
+        load.wait()
 
     def hidden(j, _):
         h = pl.ds(pl.multiple_of(j * TILE, TILE), TILE)
-        value, _ = gelu_both(nt(nf[...], wi[h, :]))
+        of = pl.ds(pl.multiple_of(j * (TILE // part), TILE // part), TILE // part)
+        wi = vwi[of].reshape(TILE, dim)
+        value, _ = gelu_both(nt(vnf[...], wi))
         act_f[:, h] = value.astype(bf16)
-        _, slope = gelu_both(nt(nb[...], wi[h, :]))
-        dp[:, h] = (nt(c2[...], wo[h, :]) * slope).astype(bf16)
-
-    lax.fori_loop(0, wi.shape[0] // TILE, hidden, None)
-
-    def back(j, _):
-        c = pl.ds(pl.multiple_of(j * TILE, TILE), TILE)
-        b = br[:, c].astype(f32) + nn(act_f[...], wo[:, c])
+        _, slope = gelu_both(nt(vnb[...], wi))
+        dp[:, h] = (nt(vc2[...], vwo[of].reshape(TILE, dim)) * slope).astype(bf16)
+
+    lax.fori_loop(0, hid // TILE, hidden, None)
+    for load in loads[5:]:
+        load.wait()
+    for t in range(0, dim, 2 * TILE):
+        c = slice(t, t + 2 * TILE)
+        b = vbr[:, c].astype(f32) + nn(act_f[...], vwo[:, :, c].reshape(hid, 2 * TILE))
         keep[0, :, c] = b[:rows]
         send[0, :, c] = b[rows:].astype(bf16)
-        g = dn[:, c].astype(f32) + nn(dp[...], wi[:, c])
+        g = vdn[:, c].astype(f32) + nn(dp[...], vwi[:, :, c].reshape(hid, 2 * TILE))
         keep[1, :, c] = g[:rows]
         send[1, :, c] = g[rows:].astype(bf16)
-
-    lax.fori_loop(0, wi.shape[1] // TILE, back, None)
 
 
 def half_kernel(far, far2, wi, gain, nbt, act, slope, vfar, vwi, nb, arrived):
@@ -292,10 +304,15 @@
     keep, send = local(
         rest_kernel,
         [((2, rows, dim), f32), ((2, rows, dim), bf16)],
-        [((both, hid), bf16)] * 2 + [((hid, dim), bf16)] * 2,
+        [((n_dp, part, dim), bf16)] * 2
+        + [((both, dim), bf16)] * 5
+        + [((both, hid), bf16)] * 2
+        + [dma((7,))],
         10 * both * hid * dim,
         8 * 2**20,
         mib=56,
+        in_specs=[hbm] * 6,
+        out_specs=[vmem] * 2,
     )(whole, nf, nb, c2, br, dn)
     sums = keep + to_core(send).astype(f32)
     out = (xf.astype(f32) + sums[0]).astype(bf16)
@@ -363,6 +380,4 @@
         P("section", "mp", "dp"),
         P("section", "mp", "dp"),
     )
-    return jax.shard_map(
-        layer, mesh=mesh, in_specs=in_specs, out_specs=out_specs, check_vma=False
-    )
+    return jax.shard_map(layer, mesh=mesh, in_specs=in_specs, out_specs=out_specs, check_vma=False)

time: 184 us -> 184 us (level)
  no operation moved by 1% of the time
where the time goes in v9:
time: 184 us; the launch traced here: 183 us
  starting transfers between devices  86.6 us (47%)
  waiting for transfers between devices  53 us (29%)
  Pallas kernels  24.2 us (13%)
  blocking collectives  11.5 us (6%)
  local copies, waits for them, and re-layouts  4.54 us (2%)
    ppermute x3, starting transfers between devices, to_chip(): return lax.ppermute(x, 'mp', other_chip)  34.5 us
    ppermute x3, waiting for transfers between devices, to_chip(): return lax.ppermute(x, 'mp', other_chip)  26.2 us
    ppermute x2, starting transfers between devices, shifted(): lax.ppermute(x, axis, [(i, (i + by) % length) for i in range(length)])  23.2 us
    all_to_all x2, waiting for transfers between devices, exchanged(): return lax.all_to_all(x, 'dp', 0, 0, tiled=True, axis_index_groups=groups)  18.7 us
    all_to_all x2, starting transfers between devices, exchanged(): return lax.all_to_all(x, 'dp', 0, 0, tiled=True, axis_index_groups=groups)  14.8 us
    all_to_all x1, blocking collectives, gathered(): lax.all_to_all(copies, 'dp', 0, 0, tiled=True, axis_index_groups=groups)  11.5 us
    ppermute x2, waiting for transfers between devices, shifted(): lax.ppermute(x, axis, [(i, (i + by) % length) for i in range(length)])  8.17 us
    pallas_call x1, Pallas kernels, layer(): local(own_kernel, [((both, dim), bf16)] * 5 + [((dim, 2 * hid), bf16)], [...  7.97 us
  transfers between devices with their start and end apart: 12, of which 6 were waited for; matrix products, arithmetic and copies ran while one was open for 1% of the time, Pallas kernels for 13%

profile of v9, /device:TPU:40, one launch (start us, length us, event | category | flops | bytes accessed | tf_op | source)
XLA Modules:
  0.0 182.6 jit_solution(14764936812714712794)
XLA Ops:
  0.7 0.8 constant_dynamic-slice_fusion
  1.4 0.8 constant_dynamic-slice_fusion.1
  2.2 19.4 %collective-permute-start = (bf16[2,16,1024]{2,1,0:T(8,128)(2,1)S(1)}, bf16[2,16,1024]{2,1,0:T(8,128)(2,1)S(1)}, u32[]{:S(2)}, u32[]{:S(2)}) collective-permute-start(bf16[2,16,1024]{2,1,0:T(8,128)(2,1)S(1)} %pad_maximum_fusion.1), channel_id=1, source_target_pairs={{0,2},{1,3},{2,0},{3,1},{4,6},{5,7},{6,4},{7,5},{8,10},{9,11},{10,... | collective-permute-start | bytes 196616 | tf_op jit(solution)/shard_map/ppermute | solution.py:27
  21.6 4.6 %collective-permute-done = bf16[2,16,1024]{2,1,0:T(8,128)(2,1)S(1)} collective-permute-done((bf16[2,16,1024]{2,1,0:T(8,128)(2,1)S(1)}, bf16[2,16,1024]{2,1,0:T(8,128)(2,1)S(1)}, u32[]{:S(2)}, u32[]{:S(2)}) %collective-permute-start) | collective-permute-done | bytes 65568 | tf_op jit(solution)/shard_map/ppermute | solution.py:27
  26.2 11.5 %all_to_all.20 = bf16[4,2,16,1024]{3,2,1,0:T(8,128)(2,1)S(1)} all-to-all(bf16[4,2,16,1024]{3,2,1,0:T(8,128)(2,1)S(1)} %broadcast_in_dim.14), channel_id=1, replica_groups={{0,32,64,96},{4,36,68,100},{8,40,72,104},{12,44,76,108},{16,48,80,112},..., dimensions={0} | all-to-all | bytes 524288 | tf_op jit(solution)/shard_map/all_to_all | solution.py:41
  37.7 1.6 broadcast_in_dim.15
  39.3 6.3 %all-to-all-start.1 = ((bf16[8,4,2,16,1024]{4,3,2,1,0:T(8,128)(2,1)}), bf16[8,4,2,16,1024]{4,3,2,1,0:T(8,128)(2,1)}, u32[]{:S(2)}, u32[]{:S(2)}) async-start(bf16[8,4,2,16,1024]{4,3,2,1,0:T(8,128)(2,1)} %broadcast_in_dim.15), calls=%async_computation.1 | async-start | bytes 4194304 | tf_op jit(solution)/shard_map/all_to_all | solution.py:41
  45.6 1.9 %collective-permute-start.1 = (bf16[384,1024]{1,0:T(8,128)(2,1)S(1)}, bf16[384,1024]{1,0:T(8,128)(2,1)}, u32[]{:S(2)}, u32[]{:S(2)}) collective-permute-start(bf16[384,1024]{1,0:T(8,128)(2,1)S(1)} %pad_maximum_fusion), channel_id=1, source_target_pairs={{0,1},{1,0},{2,3},{3,2},{4,5},{5,4},{6,7},{7,6},{8,9},{9,8},{10,11... | collective-permute-start | bytes 2359304 | tf_op jit(solution)/shard_map/ppermute | solution.py:31
  47.6 13.3 %collective-permute-start.7 = (bf16[128,1024]{1,0:T(8,128)(2,1)S(1)}, bf16[128,1024]{1,0:T(8,128)(2,1)S(1)}, u32[]{:S(2)}, u32[]{:S(2)}) collective-permute-start(bf16[128,1024]{1,0:T(8,128)(2,1)S(1)} %bitcast.34), channel_id=1, source_target_pairs={{0,2},{1,3},{2,0},{3,1},{4,6},{5,7},{6,4},{7,5},{8,10},{9,11},{10,... | collective-permute-start | bytes 786440 | tf_op jit(solution)/shard_map/ppermute | solution.py:27
  60.8 1.9 %collective-permute-start.5 = (bf16[128,1024]{1,0:T(8,128)(2,1)S(1)}, bf16[128,1024]{1,0:T(8,128)(2,1)S(1)}, u32[]{:S(2)}, u32[]{:S(2)}) collective-permute-start(bf16[128,1024]{1,0:T(8,128)(2,1)S(1)} %bitcast.43), channel_id=1, source_target_pairs={{0,2},{1,3},{2,0},{3,1},{4,6},{5,7},{6,4},{7,5},{8,10},{9,11},{10,... | collective-permute-start | bytes 786440 | tf_op jit(solution)/shard_map/ppermute | solution.py:27
  62.8 11.1 %collective-permute-done.7.far = bf16[128,1024]{1,0:T(8,128)(2,1)S(1)} collective-permute-done((bf16[128,1024]{1,0:T(8,128)(2,1)S(1)}, bf16[128,1024]{1,0:T(8,128)(2,1)S(1)}, u32[]{:S(2)}, u32[]{:S(2)}) %collective-permute-start.7) | collective-permute-done | bytes 262176 | tf_op jit(solution)/shard_map/ppermute | solution.py:27
  73.8 1.9 %collective-permute-start.8 = (bf16[128,1024]{1,0:T(8,128)(2,1)S(1)}, bf16[128,1024]{1,0:T(8,128)(2,1)S(1)}, u32[]{:S(2)}, u32[]{:S(2)}) collective-permute-start(bf16[128,1024]{1,0:T(8,128)(2,1)S(1)} %collective-permute-done.7.far), channel_id=1, source_target_pairs={{0,1},{1,0},{2,3},{3,2},{4,5},{5,4},{6,7},{7,6},{8,9},{9,8},{10,11... | collective-permute-start | bytes 786440 | tf_op jit(solution)/shard_map/ppermute | solution.py:31
  75.7 10.5 %collective-permute-done.5.far = bf16[128,1024]{1,0:T(8,128)(2,1)S(1)} collective-permute-done((bf16[128,1024]{1,0:T(8,128)(2,1)S(1)}, bf16[128,1024]{1,0:T(8,128)(2,1)S(1)}, u32[]{:S(2)}, u32[]{:S(2)}) %collective-permute-start.5) | collective-permute-done | bytes 262176 | tf_op jit(solution)/shard_map/ppermute | solution.py:27
  86.3 1.9 %collective-permute-start.6 = (bf16[128,1024]{1,0:T(8,128)(2,1)S(1)}, bf16[128,1024]{1,0:T(8,128)(2,1)S(1)}, u32[]{:S(2)}, u32[]{:S(2)}) collective-permute-start(bf16[128,1024]{1,0:T(8,128)(2,1)S(1)} %collective-permute-done.5.far), channel_id=1, source_target_pairs={{0,1},{1,0},{2,3},{3,2},{4,5},{5,4},{6,7},{7,6},{8,9},{9,8},{10,11... | collective-permute-start | bytes 786440 | tf_op jit(solution)/shard_map/ppermute | solution.py:31
  88.2 0.7 copy-done.10
  88.9 4.1 %shard_map.96 = (bf16[1024,256]{1,0:T(8,128)(2,1)}, bf16[256,512]{1,0:T(8,128)(2,1)}, f32[256,512]{1,0:T(8,128)}) custom-call(bf16[128,1024]{1,0:T(8,128)(2,1)} %copy-done.9, bf16[128,1024]{1,0:T(8,128)(2,1)} %copy-done.10, bf16[512,1024]{1,0:T(8,128)(2,1)} %bitcast.37, f32[1,1024]{1,0:T(1,128)} %gain.3), custom_call_target="tpu_custom_call" | custom-call | flops 268435456 | bytes 4194304 | tf_op jit(solution)/shard_map/pallas_call | solution.py:327
  93.0 8.0 %shard_map.93 = (bf16[256,1024]{1,0:T(8,128)(2,1)}, bf16[256,1024]{1,0:T(8,128)(2,1)}, bf16[256,1024]{1,0:T(8,128)(2,1)}, bf16[256,1024]{1,0:T(8,128)(2,1)}, bf1...) custom-call(bf16[128,1024]{1,0:T(8,128)(2,1)} %bitcast.39, bf16[128,1024]{1,0:T(8,128)(2,1)} %bitcast.32, ...), custom_call_target="tpu_custom_call" | custom-call | flops 1879048192 | bytes 8388608 | tf_op jit(solution)/shard_map/pallas_call | solution.py:280
  101.1 0.7 copy-done.8
  101.7 4.2 %shard_map.97 = bf16[8,4,32,1024]{3,2,1,0:T(8,128)(2,1)} custom-call(bf16[128,1024]{1,0:T(8,128)(2,1)} %copy-done.7, bf16[128,1024]{1,0:T(8,128)(2,1)} %copy-done.8, bf16[512,1024]{1,0:T(8,128)(2,1)} %bitcast.36, bf16[1024,256]{1,0:T(8,128)(2,1)} %get-tuple-element.28.nbt, bf16[256,512]{1,0:T(8,128)(2,1)} %get-tuple-element.29.act, ...), custom_call_target="tpu_custom_call" | custom-call | flops 805306368 | bytes 7340032 | tf_op jit(solution)/shard_map/pallas_call | solution.py:338
  106.0 5.7 %all-to-all-start.2 = ((bf16[8,4,32,1024]{3,2,1,0:T(8,128)(2,1)}), bf16[8,4,32,1024]{3,2,1,0:T(8,128)(2,1)S(1)}, u32[]{:S(2)}, u32[]{:S(2)}) async-start(bf16[8,4,32,1024]{3,2,1,0:T(8,128)(2,1)} %shard_map.97), calls=%async_computation.2 | async-start | bytes 4194304 | tf_op jit(solution)/shard_map/all_to_all | solution.py:45
  111.7 5.4 %shard_map.94 = (f32[2,128,1024]{2,1,0:T(8,128)}, bf16[2,128,1024]{2,1,0:T(8,128)(2,1)}) custom-call(bf16[32,2,16,1024]{3,2,1,0:T(8,128)(2,1)} %bitcast.1.whole, bf16[256,1024]{1,0:T(8,128)(2,1)} %get-tuple-element.19.nf, bf16[256,1024]{1,0:T(8,128)(2,1)} %get-tuple-element.20.nb, bf16[256,1024]{1,0:T(8,128)(2,1)} %get-tuple-element.21.c2, ...), custom_call_target="tpu_custom_call" | custom-call | flops 1342177280 | bytes 8388608 | tf_op jit(solution)/shard_map/pallas_call | solution.py:304
  117.1 2.1 %collective-permute-start.2 = (bf16[2,128,1024]{2,1,0:T(8,128)(2,1)}, bf16[2,128,1024]{2,1,0:T(8,128)(2,1)}, u32[]{:S(2)}, u32[]{:S(2)}) collective-permute-start(bf16[2,128,1024]{2,1,0:T(8,128)(2,1)} %get-tuple-element.25), channel_id=1, source_target_pairs={{0,1},{1,0},{2,3},{3,2},{4,5},{5,4},{6,7},{7,6},{8,9},{9,8},{10,11... | collective-permute-start | bytes 1572872 | tf_op jit(solution)/shard_map/ppermute | solution.py:31
  119.2 18.7 %all-to-all-done.2.pieces = bf16[8,4,32,1024]{3,2,1,0:T(8,128)(2,1)S(1)} async-done(((bf16[8,4,32,1024]{3,2,1,0:T(8,128)(2,1)}), bf16[8,4,32,1024]{3,2,1,0:T(8,128)(2,1)S(1)}, u32[]{:S(2)}, u32[]{:S(2)}) %all-to-all-start.2) | async-done | bytes 2097184 | tf_op jit(solution)/shard_map/all_to_all | solution.py:45
  137.9 1.0 shard_map.98
  138.9 9.1 %all-to-all-start.3 = ((bf16[4,32,1024]{2,1,0:T(8,128)(2,1)}), bf16[4,32,1024]{2,1,0:T(8,128)(2,1)S(1)}, u32[]{:S(2)}, u32[]{:S(2)}) async-start(bf16[4,32,1024]{2,1,0:T(8,128)(2,1)} %shard_map.98), calls=%async_computation.3 | async-start | bytes 524288 | tf_op jit(solution)/shard_map/all_to_all | solution.py:45
  148.0 1.2 convert_add_fusion
  149.8 21.3 %collective-permute-start.3 = (bf16[128,1024]{1,0:T(8,128)(2,1)S(1)}, bf16[128,1024]{1,0:T(8,128)(2,1)S(1)}, u32[]{:S(2)}, u32[]{:S(2)}) collective-permute-start(bf16[128,1024]{1,0:T(8,128)(2,1)S(1)} %get-tuple-element.37), channel_id=1, source_target_pairs={{0,128},{128,256},{256,384},{384,512},{512,640},{640,768},{768,896... | collective-permute-start | bytes 786440 | tf_op jit(solution)/shard_map/ppermute | solution.py:36
  171.1 1.9 %collective-permute-start.4 = (bf16[128,1024]{1,0:T(8,128)(2,1)S(1)}, bf16[128,1024]{1,0:T(8,128)(2,1)S(1)}, u32[]{:S(2)}, u32[]{:S(2)}) collective-permute-start(bf16[128,1024]{1,0:T(8,128)(2,1)S(1)} %get-tuple-element.36), channel_id=1, source_target_pairs={{0,896},{128,0},{256,128},{384,256},{512,384},{640,512},{768,640},... | collective-permute-start | bytes 786440 | tf_op jit(solution)/shard_map/ppermute | solution.py:36
  173.0 0.7 shard_map.99
  173.6 4.1 %collective-permute-done.3.a = bf16[128,1024]{1,0:T(8,128)(2,1)S(1)} collective-permute-done((bf16[128,1024]{1,0:T(8,128)(2,1)S(1)}, bf16[128,1024]{1,0:T(8,128)(2,1)S(1)}, u32[]{:S(2)}, u32[]{:S(2)}) %collective-permute-start.3) | collective-permute-done | bytes 262176 | tf_op jit(solution)/shard_map/ppermute | solution.py:36
  177.7 4.1 %collective-permute-done.4.b = bf16[128,1024]{1,0:T(8,128)(2,1)S(1)} collective-permute-done((bf16[128,1024]{1,0:T(8,128)(2,1)S(1)}, bf16[128,1024]{1,0:T(8,128)(2,1)S(1)}, u32[]{:S(2)}, u32[]{:S(2)}) %collective-permute-start.4) | collective-permute-done | bytes 262176 | tf_op jit(solution)/shard_map/ppermute | solution.py:36
  181.8 0.8 shard_map.95
  (34 shorter events, 0.6 us)
Async XLA Ops:
  2.2 23.9 %collective-permute-start = (bf16[2,16,1024]{2,1,0:T(8,128)(2,1)S(1)}, bf16[2,16,1024]{2,1,0:T(8,128)(2,1)S(1)}, u32[]{:S(2)}, u32[]{:S(2)}) collective-permute-start(bf16[2,16,1024]{2,1,0:T(8,128)(2,1)S(1)} %pad_maximum_fusion.1), channel_id=1, source_target_pairs={{0,2},{1,3},{2,0},{3,1},{4,6},{5,7},{6,4},{7,5},{8,10},{9,11},{10,... | collective-permute-start | bytes 196616 | tf_op jit(solution)/shard_map/ppermute | solution.py:27
  39.3 6.3 %copy-start = (bf16[1,128,1024]{2,1,0:T(8,128)(2,1)S(1)}, bf16[1,128,1024]{2,1,0:T(8,128)(2,1)}, u32[]{:S(2)}) copy-start(bf16[1,128,1024]{2,1,0:T(8,128)(2,1)} %param.7) | copy-start | bytes 786436
  39.3 6.3 %copy-start.3 = (bf16[1,128,1024]{2,1,0:T(8,128)(2,1)S(1)}, bf16[1,128,1024]{2,1,0:T(8,128)(2,1)}, u32[]{:S(2)}) copy-start(bf16[1,128,1024]{2,1,0:T(8,128)(2,1)} %param.6) | copy-start | bytes 786436
  39.3 6.3 %copy-start.5 = (bf16[1,128,1024]{2,1,0:T(8,128)(2,1)S(1)}, bf16[1,128,1024]{2,1,0:T(8,128)(2,1)}, u32[]{:S(2)}) copy-start(bf16[1,128,1024]{2,1,0:T(8,128)(2,1)} %param.8) | copy-start | bytes 786436
  39.3 66.7 %all-to-all-start.1 = ((bf16[8,4,2,16,1024]{4,3,2,1,0:T(8,128)(2,1)}), bf16[8,4,2,16,1024]{4,3,2,1,0:T(8,128)(2,1)}, u32[]{:S(2)}, u32[]{:S(2)}) async-start(bf16[8,4,2,16,1024]{4,3,2,1,0:T(8,128)(2,1)} %broadcast_in_dim.15), calls=%async_computation.1 | async-start | bytes 4194304 | tf_op jit(solution)/shard_map/all_to_all | solution.py:41
  45.6 47.4 %collective-permute-start.1 = (bf16[384,1024]{1,0:T(8,128)(2,1)S(1)}, bf16[384,1024]{1,0:T(8,128)(2,1)}, u32[]{:S(2)}, u32[]{:S(2)}) collective-permute-start(bf16[384,1024]{1,0:T(8,128)(2,1)S(1)} %pad_maximum_fusion), channel_id=1, source_target_pairs={{0,1},{1,0},{2,3},{3,2},{4,5},{5,4},{6,7},{7,6},{8,9},{9,8},{10,11... | collective-permute-start | bytes 2359304 | tf_op jit(solution)/shard_map/ppermute | solution.py:31
  47.6 26.3 %collective-permute-start.7 = (bf16[128,1024]{1,0:T(8,128)(2,1)S(1)}, bf16[128,1024]{1,0:T(8,128)(2,1)S(1)}, u32[]{:S(2)}, u32[]{:S(2)}) collective-permute-start(bf16[128,1024]{1,0:T(8,128)(2,1)S(1)} %bitcast.34), channel_id=1, source_target_pairs={{0,2},{1,3},{2,0},{3,1},{4,6},{5,7},{6,4},{7,5},{8,10},{9,11},{10,... | collective-permute-start | bytes 786440 | tf_op jit(solution)/shard_map/ppermute | solution.py:27
  60.8 25.4 %collective-permute-start.5 = (bf16[128,1024]{1,0:T(8,128)(2,1)S(1)}, bf16[128,1024]{1,0:T(8,128)(2,1)S(1)}, u32[]{:S(2)}, u32[]{:S(2)}) collective-permute-start(bf16[128,1024]{1,0:T(8,128)(2,1)S(1)} %bitcast.43), channel_id=1, source_target_pairs={{0,2},{1,3},{2,0},{3,1},{4,6},{5,7},{6,4},{7,5},{8,10},{9,11},{10,... | collective-permute-start | bytes 786440 | tf_op jit(solution)/shard_map/ppermute | solution.py:27
  73.8 14.4 %copy-start.9 = (bf16[128,1024]{1,0:T(8,128)(2,1)}, bf16[128,1024]{1,0:T(8,128)(2,1)S(1)}, u32[]{:S(2)}) copy-start(bf16[128,1024]{1,0:T(8,128)(2,1)S(1)} %collective-permute-done.7.far) | copy-start | bytes 786436
  73.8 14.4 %collective-permute-start.8 = (bf16[128,1024]{1,0:T(8,128)(2,1)S(1)}, bf16[128,1024]{1,0:T(8,128)(2,1)S(1)}, u32[]{:S(2)}, u32[]{:S(2)}) collective-permute-start(bf16[128,1024]{1,0:T(8,128)(2,1)S(1)} %collective-permute-done.7.far), channel_id=1, source_target_pairs={{0,1},{1,0},{2,3},{3,2},{4,5},{5,4},{6,7},{7,6},{8,9},{9,8},{10,11... | collective-permute-start | bytes 786440 | tf_op jit(solution)/shard_map/ppermute | solution.py:31
  86.3 14.8 %copy-start.7 = (bf16[128,1024]{1,0:T(8,128)(2,1)}, bf16[128,1024]{1,0:T(8,128)(2,1)S(1)}, u32[]{:S(2)}) copy-start(bf16[128,1024]{1,0:T(8,128)(2,1)S(1)} %collective-permute-done.5.far) | copy-start | bytes 786436
  86.3 14.8 %collective-permute-start.6 = (bf16[128,1024]{1,0:T(8,128)(2,1)S(1)}, bf16[128,1024]{1,0:T(8,128)(2,1)S(1)}, u32[]{:S(2)}, u32[]{:S(2)}) collective-permute-start(bf16[128,1024]{1,0:T(8,128)(2,1)S(1)} %collective-permute-done.5.far), channel_id=1, source_target_pairs={{0,1},{1,0},{2,3},{3,2},{4,5},{5,4},{6,7},{7,6},{8,9},{9,8},{10,11... | collective-permute-start | bytes 786440 | tf_op jit(solution)/shard_map/ppermute | solution.py:31
  88.2 0.7 copy-start.10
  101.0 0.7 copy-start.8
  106.0 31.9 %all-to-all-start.2 = ((bf16[8,4,32,1024]{3,2,1,0:T(8,128)(2,1)}), bf16[8,4,32,1024]{3,2,1,0:T(8,128)(2,1)S(1)}, u32[]{:S(2)}, u32[]{:S(2)}) async-start(bf16[8,4,32,1024]{3,2,1,0:T(8,128)(2,1)} %shard_map.97), calls=%async_computation.2 | async-start | bytes 4194304 | tf_op jit(solution)/shard_map/all_to_all | solution.py:45
  117.1 30.9 %copy-start.2 = (f32[2,128,1024]{2,1,0:T(8,128)S(1)}, f32[2,128,1024]{2,1,0:T(8,128)}, u32[]{:S(2)}) copy-start(f32[2,128,1024]{2,1,0:T(8,128)} %get-tuple-element.24) | copy-start | bytes 3145732
  117.1 30.9 %collective-permute-start.2 = (bf16[2,128,1024]{2,1,0:T(8,128)(2,1)}, bf16[2,128,1024]{2,1,0:T(8,128)(2,1)}, u32[]{:S(2)}, u32[]{:S(2)}) collective-permute-start(bf16[2,128,1024]{2,1,0:T(8,128)(2,1)} %get-tuple-element.25), channel_id=1, source_target_pairs={{0,1},{1,0},{2,3},{3,2},{4,5},{5,4},{6,7},{7,6},{8,9},{9,8},{10,11... | collective-permute-start | bytes 1572872 | tf_op jit(solution)/shard_map/ppermute | solution.py:31
  138.9 10.4 %copy-start.1 = (bf16[1,128,1024]{2,1,0:T(8,128)(2,1)S(1)}, bf16[1,128,1024]{2,1,0:T(8,128)(2,1)}, u32[]{:S(2)}) copy-start(bf16[1,128,1024]{2,1,0:T(8,128)(2,1)} %param.7) | copy-start | bytes 786436
  138.9 10.4 %copy-start.11 = (f32[1,1024]{1,0:T(1,128)S(1)}, f32[1,1024]{1,0:T(1,128)}, u32[]{:S(2)}) copy-start(f32[1,1024]{1,0:T(1,128)} %gain.3) | copy-start | bytes 12292
  138.9 10.6 %copy-start.4 = (bf16[1,128,1024]{2,1,0:T(8,128)(2,1)S(1)}, bf16[1,128,1024]{2,1,0:T(8,128)(2,1)}, u32[]{:S(2)}) copy-start(bf16[1,128,1024]{2,1,0:T(8,128)(2,1)} %param.6) | copy-start | bytes 786436
  138.9 10.6 %copy-start.6 = (bf16[1,128,1024]{2,1,0:T(8,128)(2,1)S(1)}, bf16[1,128,1024]{2,1,0:T(8,128)(2,1)}, u32[]{:S(2)}) copy-start(bf16[1,128,1024]{2,1,0:T(8,128)(2,1)} %param.8) | copy-start | bytes 786436
  138.9 34.1 %all-to-all-start.3 = ((bf16[4,32,1024]{2,1,0:T(8,128)(2,1)}), bf16[4,32,1024]{2,1,0:T(8,128)(2,1)S(1)}, u32[]{:S(2)}, u32[]{:S(2)}) async-start(bf16[4,32,1024]{2,1,0:T(8,128)(2,1)} %shard_map.98), calls=%async_computation.3 | async-start | bytes 524288 | tf_op jit(solution)/shard_map/all_to_all | solution.py:45
  149.8 28.0 %collective-permute-start.3 = (bf16[128,1024]{1,0:T(8,128)(2,1)S(1)}, bf16[128,1024]{1,0:T(8,128)(2,1)S(1)}, u32[]{:S(2)}, u32[]{:S(2)}) collective-permute-start(bf16[128,1024]{1,0:T(8,128)(2,1)S(1)} %get-tuple-element.37), channel_id=1, source_target_pairs={{0,128},{128,256},{256,384},{384,512},{512,640},{640,768},{768,896... | collective-permute-start | bytes 786440 | tf_op jit(solution)/shard_map/ppermute | solution.py:36
  171.1 10.8 %collective-permute-start.4 = (bf16[128,1024]{1,0:T(8,128)(2,1)S(1)}, bf16[128,1024]{1,0:T(8,128)(2,1)S(1)}, u32[]{:S(2)}, u32[]{:S(2)}) collective-permute-start(bf16[128,1024]{1,0:T(8,128)(2,1)S(1)} %get-tuple-element.36), channel_id=1, source_target_pairs={{0,896},{128,0},{256,128},{384,256},{512,384},{640,512},{768,640},... | collective-permute-start | bytes 786440 | tf_op jit(solution)/shard_map/ppermute | solution.py:36
